TPU v7x, 512 devices: a whole 4x8x8 slice. The times are simulated.
512 devices in a mesh: tm: 16 (over y, x_hi), sx: 8 (over z), sy: 4 (over x_lo, core).
Axes of the slice: x: 4 (x_hi: 2, x_lo: 2; x = x_hi * 2 + x_lo), y: 8, z: 8, core: 2. Of those that a mesh axis runs over, the one named last changes fastest.
Arguments:
- driving_input: float32 [128, 8, 64, 512], P('tm', None, 'sx', 'sy'), may hold values from -4 to 4
- regime: int32 [8, 64, 512], P(None, 'sx', 'sy'), may hold values from 0 to 7
- reaction_rates: float32 [8], replicated, may hold values from 0.005 to 1
Outputs:
- solution: float32 [128, 8, 64, 512], P('tm', None, 'sx', 'sy')
All inputs are finite; a program needn't handle non-finite values.
Results may differ from a plain program's by a relative error of at most 0.00007.
Values sent between devices are 32-bit elements; how exact they have to be, the bound alone decides.
No kernel may reach another device: no remote copies, remote signals or barrier semaphores. Data moves between devices by JAX's collectives and lax.ppermute only.
A program may use at most 64 MiB of HBM per device.

v0:
```python
import jax
import jax.numpy as jnp
from jax import lax
from jax.sharding import PartitionSpec as P

AGGREGATE_XCELLS = 8
AGGREGATE_YCELLS = 32
SWEEPS = 4


TWO_PI = 2.0 * 3.141592653589793


def extended(x, sides, width):
    edges = {}
    for axis, dim in sides:
        devices, length = (lax.axis_size(axis), x.shape[dim])
        up = [(i, (i + 1) % devices) for i in range(devices - 1)]
        last = lax.slice_in_dim(x, length - width, length, axis=dim)
        initial = lax.slice_in_dim(x, 0, width, axis=dim)
        edges[dim] = (
            lax.ppermute(last, axis, up),
            lax.ppermute(initial, axis, [(b, a) for a, b in up]),
        )
    done = []
    for _, dim in sides:
        low, high = edges[dim]
        around = [(width, width) if d in done else (0, 0) for d in range(x.ndim)]
        x = jnp.concatenate([jnp.pad(low, around), x, jnp.pad(high, around)], axis=dim)
        done.append(dim)
    return x


def side_by_side(arrays, axis, split_dim, concat_dim, along):
    widths = [a.shape[along] for a in arrays]
    both = jnp.concatenate(arrays, axis=along)
    filled = lax.all_to_all(both, axis, split_axis=split_dim, concat_axis=concat_dim, tiled=True)
    return tuple(jnp.split(filled, [sum(widths[:k]) for k in range(1, len(widths))], axis=along))


def cut_along(x, dim, devices):
    before, after = (x.shape[:dim], x.shape[dim + 1 :])
    return jnp.moveaxis(x.reshape(*before, devices, -1, *after), dim, 0)


def edges_of(length, count):
    hop = length // count
    if hop >= 8:
        hop -= hop % 8
    return [hop * k for k in range(1, count)]


def laid_out(tiles, dim):
    shape = list(tiles.shape[1:])
    shape[dim] *= tiles.shape[0]
    return jnp.moveaxis(tiles, 0, dim).reshape(shape)


def cut_exchange(x, axis, pieces, split_dim, concat_dim):
    tiles = cut_along(x, split_dim, lax.axis_size(axis))
    split_at = max(range(1, max(2, tiles.ndim - 1)), key=lambda d: tiles.shape[d])
    finished = []
    for piece in jnp.split(tiles, edges_of(tiles.shape[split_at], pieces), axis=split_at):
        if piece.size:
            finished.append(lax.all_to_all(piece, axis, split_axis=0, concat_axis=0, tiled=True))
    return laid_out(jnp.concatenate(finished, axis=split_at), concat_dim)


def angle_table(row_index, col_index, cycle_duration):
    product = row_index[:, None] * col_index[None, :] % cycle_duration
    angles = product.astype(jnp.float32) * (TWO_PI / cycle_duration)
    return (jnp.cos(angles), jnp.sin(angles))


def matmul(left_side, right_side):
    return jnp.dot(
        left_side, right_side, precision=lax.Precision.HIGHEST, preferred_element_type=jnp.float32
    )


def complex_mul(left_real, left_imag, pair):
    return jnp.stack(
        [left_real * pair[0] - left_imag * pair[1], left_real * pair[1] + left_imag * pair[0]]
    )


def neighbors(present_guess):
    padded = extended(present_guess, (("sx", 3), ("sy", 4)), 1)
    running = padded[:, :, :, 2:, 1:-1] + padded[:, :, :, :-2, 1:-1]
    running = running + padded[:, :, :, 1:-1, 2:] + padded[:, :, :, 1:-1, :-2]
    running = running + jnp.roll(present_guess, 1, axis=2) + jnp.roll(present_guess, -1, axis=2)
    return running


def local(driving_input, regime, reaction_rates):
    moment_count, third_axis_count, first_axis_count, second_axis_count = driving_input.shape
    temporal_spacing = lax.axis_size("tm")
    sy_size = lax.axis_size("sy")
    cycle_duration = moment_count * temporal_spacing
    unknowns_in_tile = third_axis_count * first_axis_count * second_axis_count
    processor_lines = driving_input.reshape(moment_count, unknowns_in_tile)
    owned_slice_number = lax.axis_index("tm") * moment_count + jnp.arange(
        moment_count, dtype=jnp.int32
    )
    all_index = jnp.arange(cycle_duration, dtype=jnp.int32)
    pencils = lax.all_to_all(processor_lines, "tm", split_axis=1, concat_axis=0, tiled=True)
    cosine, sine = angle_table(all_index, all_index, cycle_duration)
    eigen_spectra = jnp.stack([matmul(cosine, pencils), -matmul(sine, pencils)])
    eigen_spectra = lax.all_to_all(eigen_spectra, "tm", split_axis=1, concat_axis=2, tiled=True)
    source_term = eigen_spectra.reshape(
        2, moment_count, third_axis_count, first_axis_count, second_axis_count
    )
    phase_angle = owned_slice_number.astype(jnp.float32) * (TWO_PI / cycle_duration)
    shift_real = (1.0 - jnp.cos(phase_angle))[:, None, None, None]
    shift_imag = jnp.sin(phase_angle)[:, None, None, None]
    reaction = jnp.zeros(regime.shape, jnp.float32)
    for regime_no in range(reaction_rates.shape[0]):
        reaction = reaction + jnp.where(
            regime == regime_no, reaction_rates[regime_no], jnp.zeros((), jnp.float32)
        )
    diag_real = reaction[None] + 6.0 + shift_real
    diag_imag = jnp.zeros_like(diag_real) + shift_imag
    modulus = diag_real * diag_real + diag_imag * diag_imag
    inverse_real = diag_real / modulus
    inverse_imag = -diag_imag / modulus
    present_guess = complex_mul(inverse_real, inverse_imag, source_term)
    for sweep_no in range(SWEEPS - 1):
        present_guess = complex_mul(
            inverse_real, inverse_imag, source_term + neighbors(present_guess)
        )
    applied = complex_mul(diag_real, diag_imag, present_guess) - neighbors(present_guess)
    residual = source_term - applied
    first_axis_teams = first_axis_count // AGGREGATE_XCELLS
    second_axis_teams = second_axis_count // AGGREGATE_YCELLS
    per_device = first_axis_teams * second_axis_teams

    def aggregate(values):
        leading = values.shape[:-3]
        blocks = values.reshape(
            leading
            + (
                third_axis_count,
                first_axis_teams,
                AGGREGATE_XCELLS,
                second_axis_teams,
                AGGREGATE_YCELLS,
            )
        )
        return jnp.sum(blocks, axis=(-5, -3, -1)).reshape(leading + (per_device,))

    coarse_right = jnp.transpose(aggregate(residual), (1, 0, 2))
    rate_sums = aggregate(reaction)
    shift_column = 1.0 - jnp.cos(phase_angle)
    face_count = 2 * (AGGREGATE_YCELLS * third_axis_count + AGGREGATE_XCELLS * third_axis_count)
    volume = AGGREGATE_XCELLS * AGGREGATE_YCELLS * third_axis_count
    spatial = lax.axis_size("sx") * sy_size
    slot_count = -(-moment_count // spatial)
    padding_rows = slot_count * spatial - moment_count
    padded_right = jnp.pad(coarse_right, ((0, padding_rows), (0, 0), (0, 0)))
    sum_copies = jnp.broadcast_to(rate_sums[None, None, :], (spatial, 1, per_device))
    shared_right, shared_sums = side_by_side((padded_right, sum_copies), ("sx", "sy"), 0, 2, 1)
    spatial_rank = lax.axis_index("sx") * sy_size + lax.axis_index("sy")
    padded_shift = jnp.pad(shift_column, (0, padding_rows))
    slot_shift = lax.dynamic_slice_in_dim(padded_shift, spatial_rank * slot_count, slot_count, 0)
    sum_values = shared_sums[0, 0]
    coarse_total = sum_values.shape[0]
    position = jnp.arange(coarse_total, dtype=jnp.int32)
    device = position // per_device
    within = position % per_device
    coarse_x = device // sy_size * first_axis_teams + within // second_axis_teams
    coarse_y = device % sy_size * second_axis_teams + within % second_axis_teams
    x_gap = jnp.abs(coarse_x[:, None] - coarse_x[None, :])
    y_gap = jnp.abs(coarse_y[:, None] - coarse_y[None, :])
    coupling = -(AGGREGATE_YCELLS * third_axis_count) * ((x_gap == 1) & (y_gap == 0)).astype(
        jnp.float32
    )
    coupling = coupling - AGGREGATE_XCELLS * third_axis_count * (
        (x_gap == 0) & (y_gap == 1)
    ).astype(jnp.float32)
    identity = (position[:, None] == position[None, :]).astype(jnp.float32)
    diagonal = sum_values + face_count
    system = (
        coupling[None]
        + identity[None] * (diagonal[None, :] + volume * slot_shift[:, None])[:, None, :]
    )
    factor = jnp.linalg.cholesky(system)
    right_side = jnp.transpose(shared_right, (0, 2, 1))
    forward_sub = lax.linalg.triangular_solve(factor, right_side, left_side=True, lower=True)
    coarse = lax.linalg.triangular_solve(
        factor, forward_sub, left_side=True, lower=True, transpose_a=True
    )
    solved = jnp.transpose(coarse, (0, 2, 1))
    returned = lax.all_to_all(solved, ("sx", "sy"), split_axis=2, concat_axis=0, tiled=True)
    own_coarse = returned[:moment_count]
    local_part = jnp.transpose(own_coarse, (1, 0, 2)).reshape(
        2, moment_count, 1, first_axis_teams, 1, second_axis_teams, 1
    )
    spread_values = jnp.broadcast_to(
        local_part,
        (
            2,
            moment_count,
            third_axis_count,
            first_axis_teams,
            AGGREGATE_XCELLS,
            second_axis_teams,
            AGGREGATE_YCELLS,
        ),
    )
    present_guess = present_guess + spread_values.reshape(
        2, moment_count, third_axis_count, first_axis_count, second_axis_count
    )
    unrolled_array = present_guess.reshape(2, moment_count, unknowns_in_tile)
    pencils_back = cut_exchange(unrolled_array, "tm", 2, 2, 1)
    result = (matmul(cosine, pencils_back[0]) - matmul(sine, pencils_back[1])) / cycle_duration
    result = lax.all_to_all(result, "tm", split_axis=0, concat_axis=1, tiled=True)
    return result.reshape(driving_input.shape)


def solution(mesh):
    placed = (P("tm", None, "sx", "sy"), P(None, "sx", "sy"), P())
    return jax.shard_map(
        local, mesh=mesh, in_specs=placed, out_specs=P("tm", None, "sx", "sy"), check_vma=False
    )
```

profile of v0, /device:TPU:1, one launch (start us, length us, event | category | flops | bytes accessed | tf_op | source)
XLA Modules:
  0.0 240.8 jit_solution(3244061131927030479)
XLA Ops:
  0.0 1.0 all_to_all.67
  1.2 22.1 %all_to_all.93 = f32[8,16,512]{2,0,1:T(8,128)S(1)} all-to-all(f32[8,16,512]{2,0,1:T(8,128)S(1)} %copy.53), channel_id=1, replica_groups=mesh['tm'=16,'sx'=8,'sy'=4] {'tm'}, dimensions={1} | all-to-all | bytes 524288 | tf_op jit(solution)/shard_map/all_to_all | solution.py:106
  23.2 0.6 fusion.2
  23.9 0.6 convolution_bitcast_fusion
  24.6 1.2 copy.54
  25.8 3.6 %all-to-all-start.1 = ((f32[2,128,512]{2,0,1:T(2,128)}), f32[2,128,512]{2,0,1:T(2,128)S(1)}, u32[]{:S(2)}, u32[]{:S(2)}) async-start(f32[2,128,512]{2,0,1:T(2,128)} %copy.54), calls=%async_computation.1 | async-start | bytes 1048576 | tf_op jit(solution)/shard_map/all_to_all | solution.py:109
  29.4 0.7 fusion.127
  30.1 5.1 %fusion.124 = (f32[128]{0:T(128)S(1)}, f32[8,8,128]{2,1,0:T(8,128)S(1)}) fusion(f32[]{:T(128)} %bitcast.7, s32[8,8,128]{2,1,0:T(8,128)S(1)} %copy-done, f32[]{:T(128)} %bitcast.6, f32[]{:T(128)} %bitcast.5, f32[]{:T(128)} %bitcast.4, f32[]{:T(128)} %bitcast.3, f32[]{:T(128)} %bitcast.2, f32[]{:T(128)} %bitcast.1, f32[]{:T(128)} %bitcast), kind=kLoop, calls=%fused_computation.288 | loop fusion | flops 204672 | bytes 66080 | tf_op jit(solution)/shard_map/reduce_sum | solution.py:149
  35.6 9.5 %all-to-all-done.1 = f32[2,128,512]{2,0,1:T(2,128)S(1)} async-done(((f32[2,128,512]{2,0,1:T(2,128)}), f32[2,128,512]{2,0,1:T(2,128)S(1)}, u32[]{:S(2)}, u32[]{:S(2)}) %all-to-all-start.1) | async-done | bytes 524320 | tf_op jit(solution)/shard_map/all_to_all | solution.py:109
  45.1 0.3 copy.74
  45.7 1.1 fusion.9
  47.0 6.8 %collective-permute-start.3 = (f32[2,8,8,8,1]{4,3,2,1,0:T(8,128)}, f32[2,8,8,8,1]{4,3,2,1,0:T(8,128)S(1)}, u32[]{:S(2)}, u32[]{:S(2)}) collective-permute-start(f32[2,8,8,8,1]{4,3,2,1,0:T(8,128)} %get-tuple-element.37), channel_id=1, source_target_pairs={{0,1},{1,2},{2,3},{4,5},{5,6},{6,7},{8,9},{9,10},{10,11},{12,13},{... | collective-permute-start | bytes 12296 | tf_op jit(solution)/shard_map/ppermute | solution.py:22
  53.7 1.3 collective-permute-start
  55.0 4.6 %collective-permute-start.1 = (f32[2,8,8,1,128]{4,3,2,1,0:T(1,128)S(1)}, f32[2,8,8,1,128]{4,3,2,1,0:T(1,128)S(1)}, u32[]{:S(2)}, u32[]{:S(2)}) collective-permute-start(f32[2,8,8,1,128]{4,3,2,1,0:T(1,128)S(1)} %get-tuple-element.38), channel_id=1, source_target_pairs={{0,4},{4,8},{8,12},{12,16},{16,20},{20,24},{24,28},{1,5},{5,9},{9,... | collective-permute-start | bytes 196616 | tf_op jit(solution)/shard_map/ppermute | solution.py:22
  59.7 1.9 collective-permute-start.2
  61.7 8.8 %collective-permute-done.2 = f32[2,8,8,8,1]{4,3,2,1,0:T(8,128)} collective-permute-done((f32[2,8,8,8,1]{4,3,2,1,0:T(8,128)}, f32[2,8,8,8,1]{4,3,2,1,0:T(8,128)}, u32[]{:S(2)}, u32[]{:S(2)}) %collective-permute-start.2) | collective-permute-done | bytes 4128 | tf_op jit(solution)/shard_map/ppermute | solution.py:23
  70.5 1.8 fusion.42
  72.3 0.2 multiply_subtract_fusion.2
  72.5 0.2 fusion.7
  72.9 1.9 collective-permute-start.7
  74.8 1.3 collective-permute-start.4
  76.1 4.6 %collective-permute-start.5 = (f32[2,8,8,1,128]{4,3,2,1,0:T(1,128)S(1)}, f32[2,8,8,1,128]{4,3,2,1,0:T(1,128)S(1)}, u32[]{:S(2)}, u32[]{:S(2)}) collective-permute-start(f32[2,8,8,1,128]{4,3,2,1,0:T(1,128)S(1)} %get-tuple-element.32), channel_id=1, source_target_pairs={{0,4},{4,8},{8,12},{12,16},{16,20},{20,24},{24,28},{1,5},{5,9},{9,... | collective-permute-start | bytes 196616 | tf_op jit(solution)/shard_map/ppermute | solution.py:22
  80.7 2.7 %collective-permute-start.6 = (f32[2,8,8,8,1]{4,3,2,1,0:T(8,128)S(1)}, f32[2,8,8,8,1]{4,3,2,1,0:T(8,128)S(1)}, u32[]{:S(2)}, u32[]{:S(2)}) collective-permute-start(f32[2,8,8,8,1]{4,3,2,1,0:T(8,128)S(1)} %get-tuple-element.30), channel_id=1, source_target_pairs={{1,0},{2,1},{3,2},{5,4},{6,5},{7,6},{9,8},{10,9},{11,10},{13,12},{... | collective-permute-start | bytes 12296 | tf_op jit(solution)/shard_map/ppermute | solution.py:23
  83.5 7.7 %collective-permute-done.6 = f32[2,8,8,8,1]{4,3,2,1,0:T(8,128)S(1)} collective-permute-done((f32[2,8,8,8,1]{4,3,2,1,0:T(8,128)S(1)}, f32[2,8,8,8,1]{4,3,2,1,0:T(8,128)S(1)}, u32[]{:S(2)}, u32[]{:S(2)}) %collective-permute-start.6) | collective-permute-done | bytes 4128 | tf_op jit(solution)/shard_map/ppermute | solution.py:23
  91.2 0.8 fusion.33
  92.0 0.2 multiply_subtract_fusion.1
  92.2 0.2 fusion.5
  92.6 1.9 collective-permute-start.11
  94.5 1.3 collective-permute-start.8
  95.8 4.6 %collective-permute-start.9 = (f32[2,8,8,1,128]{4,3,2,1,0:T(1,128)S(1)}, f32[2,8,8,1,128]{4,3,2,1,0:T(1,128)S(1)}, u32[]{:S(2)}, u32[]{:S(2)}) collective-permute-start(f32[2,8,8,1,128]{4,3,2,1,0:T(1,128)S(1)} %get-tuple-element.26), channel_id=1, source_target_pairs={{0,4},{4,8},{8,12},{12,16},{16,20},{20,24},{24,28},{1,5},{5,9},{9,... | collective-permute-start | bytes 196616 | tf_op jit(solution)/shard_map/ppermute | solution.py:22
  100.4 2.7 %collective-permute-start.10 = (f32[2,8,8,8,1]{4,3,2,1,0:T(8,128)S(1)}, f32[2,8,8,8,1]{4,3,2,1,0:T(8,128)S(1)}, u32[]{:S(2)}, u32[]{:S(2)}) collective-permute-start(f32[2,8,8,8,1]{4,3,2,1,0:T(8,128)S(1)} %get-tuple-element.24), channel_id=1, source_target_pairs={{1,0},{2,1},{3,2},{5,4},{6,5},{7,6},{9,8},{10,9},{11,10},{13,12},{... | collective-permute-start | bytes 12296 | tf_op jit(solution)/shard_map/ppermute | solution.py:23
  103.2 7.7 %collective-permute-done.10 = f32[2,8,8,8,1]{4,3,2,1,0:T(8,128)S(1)} collective-permute-done((f32[2,8,8,8,1]{4,3,2,1,0:T(8,128)S(1)}, f32[2,8,8,8,1]{4,3,2,1,0:T(8,128)S(1)}, u32[]{:S(2)}, u32[]{:S(2)}) %collective-permute-start.10) | collective-permute-done | bytes 4128 | tf_op jit(solution)/shard_map/ppermute | solution.py:23
  111.0 0.8 fusion.24
  111.7 0.3 fusion.60
  112.0 0.2 fusion.3
  112.5 1.9 collective-permute-start.15
  114.4 1.3 collective-permute-start.12
  115.7 5.8 %collective-permute-start.13 = (f32[2,8,8,1,128]{4,3,2,1,0:T(1,128)S(1)}, f32[2,8,8,1,128]{4,3,2,1,0:T(1,128)S(1)}, u32[]{:S(2)}, u32[]{:S(2)}) collective-permute-start(f32[2,8,8,1,128]{4,3,2,1,0:T(1,128)S(1)} %get-tuple-element.20), channel_id=1, source_target_pairs={{0,4},{4,8},{8,12},{12,16},{16,20},{20,24},{24,28},{1,5},{5,9},{9,... | collective-permute-start | bytes 196616 | tf_op jit(solution)/shard_map/ppermute | solution.py:22
  121.6 2.7 %collective-permute-start.14 = (f32[2,8,8,8,1]{4,3,2,1,0:T(8,128)S(1)}, f32[2,8,8,8,1]{4,3,2,1,0:T(8,128)S(1)}, u32[]{:S(2)}, u32[]{:S(2)}) collective-permute-start(f32[2,8,8,8,1]{4,3,2,1,0:T(8,128)S(1)} %get-tuple-element.18), channel_id=1, source_target_pairs={{1,0},{2,1},{3,2},{5,4},{6,5},{7,6},{9,8},{10,9},{11,10},{13,12},{... | collective-permute-start | bytes 12296 | tf_op jit(solution)/shard_map/ppermute | solution.py:23
  124.3 7.7 %collective-permute-done.14 = f32[2,8,8,8,1]{4,3,2,1,0:T(8,128)S(1)} collective-permute-done((f32[2,8,8,8,1]{4,3,2,1,0:T(8,128)S(1)}, f32[2,8,8,8,1]{4,3,2,1,0:T(8,128)S(1)}, u32[]{:S(2)}, u32[]{:S(2)}) %collective-permute-start.14) | collective-permute-done | bytes 4128 | tf_op jit(solution)/shard_map/ppermute | solution.py:23
  132.1 0.8 fusion.15
  133.2 0.7 copy.57
  134.0 9.3 %all-to-all-start.2 = ((f32[32,3,4]{2,1,0:T(4,128)}), f32[32,3,4]{2,1,0:T(4,128)S(1)}, u32[]{:S(2)}, u32[]{:S(2)}) async-start(f32[32,3,4]{2,1,0:T(4,128)} %copy.57), calls=%async_computation.2 | async-start | bytes 131072 | tf_op jit(solution)/shard_map/all_to_all | solution.py:37
  143.2 0.6 fusion.128
  143.9 7.6 %all-to-all-done.2 = f32[32,3,4]{2,1,0:T(4,128)S(1)} async-done(((f32[32,3,4]{2,1,0:T(4,128)}), f32[32,3,4]{2,1,0:T(4,128)S(1)}, u32[]{:S(2)}, u32[]{:S(2)}) %all-to-all-start.2) | async-done | bytes 1568 | tf_op jit(solution)/shard_map/all_to_all | solution.py:37
  151.6 0.6 fusion.103
  152.6 11.7 %custom-call.9 = f32[1,128,128]{2,1,0:T(8,128)S(1)} custom-call(f32[1,128,128]{2,1,0:T(8,128)S(1)} %fusion.84), custom_call_target="Cholesky" | custom-call | tf_op jit(solution)/shard_map/jit(cholesky)/cholesky | solution.py:186
  164.3 0.6 compare_reduce_fusion
  165.0 0.7 fusion.65
  165.6 9.8 %custom-call.10 = f32[1,1,128,128]{2,3,1,0:T(8,128)S(1)} custom-call(f32[1,1,128,128]{3,2,1,0:T(8,128)S(1)} %fusion.65), custom_call_target="InvertDiagBlocksLowerTriangular" | custom-call | tf_op jit(solution)/shard_map/triangular_solve | solution.py:189
  175.8 0.8 copy.60
  176.6 3.9 %all-to-all-start.3 = ((f32[1,2,128]{1,0,2:T(1,128)}), f32[1,2,128]{1,0,2:T(1,128)S(1)}, u32[]{:S(2)}, u32[]{:S(2)}) async-start(f32[1,2,128]{1,0,2:T(1,128)} %copy.60), calls=%async_computation.3 | async-start | bytes 131072 | tf_op jit(solution)/shard_map/all_to_all | solution.py:193
  180.6 8.3 %all-to-all-done.3 = f32[1,2,128]{1,0,2:T(1,128)S(1)} async-done(((f32[1,2,128]{1,0,2:T(1,128)}), f32[1,2,128]{1,0,2:T(1,128)S(1)}, u32[]{:S(2)}, u32[]{:S(2)}) %all-to-all-start.3) | async-done | bytes 1056 | tf_op jit(solution)/shard_map/all_to_all | solution.py:193
  188.9 0.3 copy.69
  189.4 0.5 broadcast_in_dim.76
  189.9 1.9 reshape.506
  191.9 0.9 copy.65
  192.8 3.5 %all-to-all-start.5 = ((f32[16,2,4,512]{3,2,1,0:T(4,128)}), f32[16,2,4,512]{3,2,1,0:T(4,128)S(1)}, u32[]{:S(2)}, u32[]{:S(2)}) async-start(f32[16,2,4,512]{3,2,1,0:T(4,128)} %copy.65), calls=%async_computation.5 | async-start | bytes 524288 | tf_op jit(solution)/shard_map/all_to_all | solution.py:65
  196.5 12.6 %all-to-all-done.5 = f32[16,2,4,512]{3,2,1,0:T(4,128)S(1)} async-done(((f32[16,2,4,512]{3,2,1,0:T(4,128)}), f32[16,2,4,512]{3,2,1,0:T(4,128)S(1)}, u32[]{:S(2)}, u32[]{:S(2)}) %all-to-all-start.5) | async-done | bytes 262176 | tf_op jit(solution)/shard_map/all_to_all | solution.py:65
  209.1 14.8 %all_to_all.94 = f32[16,2,4,512]{3,2,1,0:T(4,128)S(1)} all-to-all(f32[16,2,4,512]{3,2,1,0:T(4,128)S(1)} %copy.64), channel_id=1, replica_groups=mesh['tm'=16,'sx'=8,'sy'=4] {'tm'}, dimensions={0} | all-to-all | bytes 524288 | tf_op jit(solution)/shard_map/all_to_all | solution.py:65
  224.0 0.6 fusion.62
  224.7 0.6 fusion.1
  225.3 14.5 %all_to_all.95 = f32[16,8,512]{2,1,0:T(8,128)S(1)} all-to-all(f32[16,8,512]{2,1,0:T(8,128)S(1)} %fusion.1), channel_id=1, replica_groups=mesh['tm'=16,'sx'=8,'sy'=4] {'tm'}, dimensions={0} | all-to-all | bytes 524288 | tf_op jit(solution)/shard_map/all_to_all | solution.py:216
  240.0 0.7 reshape.507
  (66 shorter events, 3.6 us)
Async XLA Ops:
  23.2 6.2 %copy-start.1 = (f32[8]{0:T(128)S(1)}, f32[8]{0:T(128)}, u32[]{:S(2)}) copy-start(f32[8]{0:T(128)} %param.5) | copy-start | bytes 100
  23.2 6.8 %copy-start = (s32[8,8,128]{2,1,0:T(8,128)S(1)}, s32[8,8,128]{2,1,0:T(8,128)}, u32[]{:S(2)}) copy-start(s32[8,8,128]{2,1,0:T(8,128)} %param.4) | copy-start | bytes 98308
  25.8 19.3 %all-to-all-start.1 = ((f32[2,128,512]{2,0,1:T(2,128)}), f32[2,128,512]{2,0,1:T(2,128)S(1)}, u32[]{:S(2)}, u32[]{:S(2)}) async-start(f32[2,128,512]{2,0,1:T(2,128)} %copy.54), calls=%async_computation.1 | async-start | bytes 1048576 | tf_op jit(solution)/shard_map/all_to_all | solution.py:109
  47.0 14.7 %collective-permute-start.3 = (f32[2,8,8,8,1]{4,3,2,1,0:T(8,128)}, f32[2,8,8,8,1]{4,3,2,1,0:T(8,128)S(1)}, u32[]{:S(2)}, u32[]{:S(2)}) collective-permute-start(f32[2,8,8,8,1]{4,3,2,1,0:T(8,128)} %get-tuple-element.37), channel_id=1, source_target_pairs={{0,1},{1,2},{2,3},{4,5},{5,6},{6,7},{8,9},{9,10},{10,11},{12,13},{... | collective-permute-start | bytes 12296 | tf_op jit(solution)/shard_map/ppermute | solution.py:22
  53.7 16.8 %collective-permute-start = (f32[2,8,8,1,128]{4,3,2,1,0:T(1,128)S(1)}, f32[2,8,8,1,128]{4,3,2,1,0:T(1,128)S(1)}, u32[]{:S(2)}, u32[]{:S(2)}) collective-permute-start(f32[2,8,8,1,128]{4,3,2,1,0:T(1,128)S(1)} %get-tuple-element.39), channel_id=1, source_target_pairs={{4,0},{8,4},{12,8},{16,12},{20,16},{24,20},{28,24},{5,1},{9,5},{13... | collective-permute-start | bytes 196616 | tf_op jit(solution)/shard_map/ppermute | solution.py:23
  55.0 15.5 %collective-permute-start.1 = (f32[2,8,8,1,128]{4,3,2,1,0:T(1,128)S(1)}, f32[2,8,8,1,128]{4,3,2,1,0:T(1,128)S(1)}, u32[]{:S(2)}, u32[]{:S(2)}) collective-permute-start(f32[2,8,8,1,128]{4,3,2,1,0:T(1,128)S(1)} %get-tuple-element.38), channel_id=1, source_target_pairs={{0,4},{4,8},{8,12},{12,16},{16,20},{20,24},{24,28},{1,5},{5,9},{9,... | collective-permute-start | bytes 196616 | tf_op jit(solution)/shard_map/ppermute | solution.py:22
  59.7 10.8 %collective-permute-start.2 = (f32[2,8,8,8,1]{4,3,2,1,0:T(8,128)}, f32[2,8,8,8,1]{4,3,2,1,0:T(8,128)}, u32[]{:S(2)}, u32[]{:S(2)}) collective-permute-start(f32[2,8,8,8,1]{4,3,2,1,0:T(8,128)} %get-tuple-element.36), channel_id=1, source_target_pairs={{1,0},{2,1},{3,2},{5,4},{6,5},{7,6},{9,8},{10,9},{11,10},{13,12},{... | collective-permute-start | bytes 12296 | tf_op jit(solution)/shard_map/ppermute | solution.py:23
  72.9 10.6 %collective-permute-start.7 = (f32[2,8,8,8,1]{4,3,2,1,0:T(8,128)S(1)}, f32[2,8,8,8,1]{4,3,2,1,0:T(8,128)S(1)}, u32[]{:S(2)}, u32[]{:S(2)}) collective-permute-start(f32[2,8,8,8,1]{4,3,2,1,0:T(8,128)S(1)} %get-tuple-element.31), channel_id=1, source_target_pairs={{0,1},{1,2},{2,3},{4,5},{5,6},{6,7},{8,9},{9,10},{10,11},{12,13},{... | collective-permute-start | bytes 12296 | tf_op jit(solution)/shard_map/ppermute | solution.py:22
  74.8 16.4 %collective-permute-start.4 = (f32[2,8,8,1,128]{4,3,2,1,0:T(1,128)S(1)}, f32[2,8,8,1,128]{4,3,2,1,0:T(1,128)S(1)}, u32[]{:S(2)}, u32[]{:S(2)}) collective-permute-start(f32[2,8,8,1,128]{4,3,2,1,0:T(1,128)S(1)} %get-tuple-element.33), channel_id=1, source_target_pairs={{4,0},{8,4},{12,8},{16,12},{20,16},{24,20},{28,24},{5,1},{9,5},{13... | collective-permute-start | bytes 196616 | tf_op jit(solution)/shard_map/ppermute | solution.py:23
  76.1 15.1 %collective-permute-start.5 = (f32[2,8,8,1,128]{4,3,2,1,0:T(1,128)S(1)}, f32[2,8,8,1,128]{4,3,2,1,0:T(1,128)S(1)}, u32[]{:S(2)}, u32[]{:S(2)}) collective-permute-start(f32[2,8,8,1,128]{4,3,2,1,0:T(1,128)S(1)} %get-tuple-element.32), channel_id=1, source_target_pairs={{0,4},{4,8},{8,12},{12,16},{16,20},{20,24},{24,28},{1,5},{5,9},{9,... | collective-permute-start | bytes 196616 | tf_op jit(solution)/shard_map/ppermute | solution.py:22
  80.7 10.5 %collective-permute-start.6 = (f32[2,8,8,8,1]{4,3,2,1,0:T(8,128)S(1)}, f32[2,8,8,8,1]{4,3,2,1,0:T(8,128)S(1)}, u32[]{:S(2)}, u32[]{:S(2)}) collective-permute-start(f32[2,8,8,8,1]{4,3,2,1,0:T(8,128)S(1)} %get-tuple-element.30), channel_id=1, source_target_pairs={{1,0},{2,1},{3,2},{5,4},{6,5},{7,6},{9,8},{10,9},{11,10},{13,12},{... | collective-permute-start | bytes 12296 | tf_op jit(solution)/shard_map/ppermute | solution.py:23
  92.6 10.6 %collective-permute-start.11 = (f32[2,8,8,8,1]{4,3,2,1,0:T(8,128)S(1)}, f32[2,8,8,8,1]{4,3,2,1,0:T(8,128)S(1)}, u32[]{:S(2)}, u32[]{:S(2)}) collective-permute-start(f32[2,8,8,8,1]{4,3,2,1,0:T(8,128)S(1)} %get-tuple-element.25), channel_id=1, source_target_pairs={{0,1},{1,2},{2,3},{4,5},{5,6},{6,7},{8,9},{9,10},{10,11},{12,13},{... | collective-permute-start | bytes 12296 | tf_op jit(solution)/shard_map/ppermute | solution.py:22
  94.5 16.4 %collective-permute-start.8 = (f32[2,8,8,1,128]{4,3,2,1,0:T(1,128)S(1)}, f32[2,8,8,1,128]{4,3,2,1,0:T(1,128)S(1)}, u32[]{:S(2)}, u32[]{:S(2)}) collective-permute-start(f32[2,8,8,1,128]{4,3,2,1,0:T(1,128)S(1)} %get-tuple-element.27), channel_id=1, source_target_pairs={{4,0},{8,4},{12,8},{16,12},{20,16},{24,20},{28,24},{5,1},{9,5},{13... | collective-permute-start | bytes 196616 | tf_op jit(solution)/shard_map/ppermute | solution.py:23
  95.8 15.1 %collective-permute-start.9 = (f32[2,8,8,1,128]{4,3,2,1,0:T(1,128)S(1)}, f32[2,8,8,1,128]{4,3,2,1,0:T(1,128)S(1)}, u32[]{:S(2)}, u32[]{:S(2)}) collective-permute-start(f32[2,8,8,1,128]{4,3,2,1,0:T(1,128)S(1)} %get-tuple-element.26), channel_id=1, source_target_pairs={{0,4},{4,8},{8,12},{12,16},{16,20},{20,24},{24,28},{1,5},{5,9},{9,... | collective-permute-start | bytes 196616 | tf_op jit(solution)/shard_map/ppermute | solution.py:22
  100.4 10.5 %collective-permute-start.10 = (f32[2,8,8,8,1]{4,3,2,1,0:T(8,128)S(1)}, f32[2,8,8,8,1]{4,3,2,1,0:T(8,128)S(1)}, u32[]{:S(2)}, u32[]{:S(2)}) collective-permute-start(f32[2,8,8,8,1]{4,3,2,1,0:T(8,128)S(1)} %get-tuple-element.24), channel_id=1, source_target_pairs={{1,0},{2,1},{3,2},{5,4},{6,5},{7,6},{9,8},{10,9},{11,10},{13,12},{... | collective-permute-start | bytes 12296 | tf_op jit(solution)/shard_map/ppermute | solution.py:23
  112.5 11.8 %collective-permute-start.15 = (f32[2,8,8,8,1]{4,3,2,1,0:T(8,128)S(1)}, f32[2,8,8,8,1]{4,3,2,1,0:T(8,128)S(1)}, u32[]{:S(2)}, u32[]{:S(2)}) collective-permute-start(f32[2,8,8,8,1]{4,3,2,1,0:T(8,128)S(1)} %get-tuple-element.19), channel_id=1, source_target_pairs={{0,1},{1,2},{2,3},{4,5},{5,6},{6,7},{8,9},{9,10},{10,11},{12,13},{... | collective-permute-start | bytes 12296 | tf_op jit(solution)/shard_map/ppermute | solution.py:22
  114.4 17.6 %collective-permute-start.12 = (f32[2,8,8,1,128]{4,3,2,1,0:T(1,128)S(1)}, f32[2,8,8,1,128]{4,3,2,1,0:T(1,128)S(1)}, u32[]{:S(2)}, u32[]{:S(2)}) collective-permute-start(f32[2,8,8,1,128]{4,3,2,1,0:T(1,128)S(1)} %get-tuple-element.21), channel_id=1, source_target_pairs={{4,0},{8,4},{12,8},{16,12},{20,16},{24,20},{28,24},{5,1},{9,5},{13... | collective-permute-start | bytes 196616 | tf_op jit(solution)/shard_map/ppermute | solution.py:23
  115.7 16.4 %collective-permute-start.13 = (f32[2,8,8,1,128]{4,3,2,1,0:T(1,128)S(1)}, f32[2,8,8,1,128]{4,3,2,1,0:T(1,128)S(1)}, u32[]{:S(2)}, u32[]{:S(2)}) collective-permute-start(f32[2,8,8,1,128]{4,3,2,1,0:T(1,128)S(1)} %get-tuple-element.20), channel_id=1, source_target_pairs={{0,4},{4,8},{8,12},{12,16},{16,20},{20,24},{24,28},{1,5},{5,9},{9,... | collective-permute-start | bytes 196616 | tf_op jit(solution)/shard_map/ppermute | solution.py:22
  121.6 10.5 %collective-permute-start.14 = (f32[2,8,8,8,1]{4,3,2,1,0:T(8,128)S(1)}, f32[2,8,8,8,1]{4,3,2,1,0:T(8,128)S(1)}, u32[]{:S(2)}, u32[]{:S(2)}) collective-permute-start(f32[2,8,8,8,1]{4,3,2,1,0:T(8,128)S(1)} %get-tuple-element.18), channel_id=1, source_target_pairs={{1,0},{2,1},{3,2},{5,4},{6,5},{7,6},{9,8},{10,9},{11,10},{13,12},{... | collective-permute-start | bytes 12296 | tf_op jit(solution)/shard_map/ppermute | solution.py:23
  134.0 17.5 %all-to-all-start.2 = ((f32[32,3,4]{2,1,0:T(4,128)}), f32[32,3,4]{2,1,0:T(4,128)S(1)}, u32[]{:S(2)}, u32[]{:S(2)}) async-start(f32[32,3,4]{2,1,0:T(4,128)} %copy.57), calls=%async_computation.2 | async-start | bytes 131072 | tf_op jit(solution)/shard_map/all_to_all | solution.py:37
  176.6 12.3 %all-to-all-start.3 = ((f32[1,2,128]{1,0,2:T(1,128)}), f32[1,2,128]{1,0,2:T(1,128)S(1)}, u32[]{:S(2)}, u32[]{:S(2)}) async-start(f32[1,2,128]{1,0,2:T(1,128)} %copy.60), calls=%async_computation.3 | async-start | bytes 131072 | tf_op jit(solution)/shard_map/all_to_all | solution.py:193
  192.8 16.3 %all-to-all-start.5 = ((f32[16,2,4,512]{3,2,1,0:T(4,128)}), f32[16,2,4,512]{3,2,1,0:T(4,128)S(1)}, u32[]{:S(2)}, u32[]{:S(2)}) async-start(f32[16,2,4,512]{3,2,1,0:T(4,128)} %copy.65), calls=%async_computation.5 | async-start | bytes 524288 | tf_op jit(solution)/shard_map/all_to_all | solution.py:65
where the time goes:
time: 243 us; the launch traced here: 241 us
  waiting for transfers between devices  70.1 us (29%)
  starting transfers between devices  67.7 us (28%)
  blocking collectives  51.4 us (21%)
  other arithmetic  37.5 us (15%)
  local copies, waits for them, and re-layouts  10.4 us (4%)
  matrix products  2.91 us (1%)
    ppermute x8, starting transfers between devices, extended(): lax.ppermute(last, axis, up)  32.2 us
    ppermute x8, waiting for transfers between devices, extended(): lax.ppermute(initial, axis, [(b, a) for a, b in up])  32.1 us
    all_to_all x1, blocking collectives, local(): lax.all_to_all(processor_lines, 'tm', split_axis=1, concat_axis=0, tiled=...  22.1 us
    ppermute x8, starting transfers between devices, extended(): lax.ppermute(initial, axis, [(b, a) for a, b in up])  15.2 us
    all_to_all x1, blocking collectives, cut_exchange(): lax.all_to_all(piece, axis, split_axis=0, concat_axis=0, tiled=True)  14.8 us
    all_to_all x1, blocking collectives, local(): lax.all_to_all(result, 'tm', split_axis=0, concat_axis=1, tiled=True)  14.5 us
    all_to_all x1, waiting for transfers between devices, cut_exchange(): lax.all_to_all(piece, axis, split_axis=0, concat_axis=0, tiled=True)  12.6 us
    another operation x3, other arithmetic, local(): factor = jnp.linalg.cholesky(system)  12.4 us
  transfers between devices with their start and end apart: 20, of which 8 were waited for; matrix products, arithmetic and copies ran while one was open for 3% of the time, Pallas kernels for 0%

commit v1 on v0

v1 whole, which is shorter than its diff:
```python
import jax
import jax.numpy as jnp
import numpy as np
from jax import lax
from jax.experimental import pallas as pl
from jax.experimental.pallas import tpu as pltpu
from jax.sharding import PartitionSpec as P

L = 128
NZ = 8
BLOCK = 8
WIDTH = 4
SPAN = BLOCK + 2 * WIDTH
TM, SX, SY = 16, 8, 4
FACES = 2 * (32 * NZ + 8 * NZ)
VOLUME = 8 * 32 * NZ
COUPLE_X = 32.0 * NZ
COUPLE_Y = 8.0 * NZ
INTERPRET = False


def strip_of(d):
    return d // 2 if d % 2 == 0 else TM - 1 - d // 2


MEMBER = {strip_of(d): d for d in range(TM)}


def tables():
    n = np.arange(L)
    k = np.arange(64)
    ang = 2.0 * np.pi * ((n[:, None] * k[None, :]) % L) / L
    half = np.where(n % 2 == 0, 1.0, -1.0)
    forward = np.concatenate([np.cos(ang), -np.sin(ang)], axis=1)
    forward[:, 64] = half
    weight = np.full((1, 64), 2.0)
    weight[0, 0] = 1.0
    inverse = np.concatenate([weight * np.cos(ang), -weight * np.sin(ang)], axis=1) / L
    inverse[:, 64] = half / L
    theta = 2.0 * np.pi * k / L
    shift = np.concatenate([1.0 - np.cos(theta)] * 2)
    shift[64] = 2.0
    sine = np.concatenate([np.sin(theta), -np.sin(theta)])
    sine[0] = sine[64] = 0.0
    order = np.array([8 * d + 2 * tp + t2 for t2 in range(2) for d in range(TM) for tp in range(4)])
    lanes = np.zeros((8, L))
    lanes[0] = shift
    lanes[1] = sine
    as32 = lambda a: np.asarray(a, np.float32)
    return as32(forward[order]), as32(inverse[order]), as32(lanes)


FORWARD, INVERSE, LANES = tables()


def vmem(count):
    return [pl.BlockSpec(memory_space=pltpu.VMEM)] * count


def smem(count):
    return [pl.BlockSpec(memory_space=pltpu.SMEM)] * count


def shape(*dims):
    return jax.ShapeDtypeStruct(dims, jnp.float32)


def dot(a, b, dims):
    return lax.dot_general(
        a, b, (dims, ((), ())), precision=lax.Precision.HIGHEST, preferred_element_type=jnp.float32
    )


def lane_index(rows):
    return lax.broadcasted_iota(jnp.int32, (rows, L), 1)


def halves(low, high):
    first = lane_index(low.shape[0]) < 64
    return (
        jnp.where(first, low, pltpu.roll(high, 64, 1)),
        jnp.where(first, pltpu.roll(low, 64, 1), high),
    )


def pack_kernel(rates, field, regime, out, rate_rows, sums):
    for tp in range(4):
        rows = [
            field[pl.ds((2 * tp + t2) * 64 + x, 8, stride=8), :] for t2 in range(2) for x in range(8)
        ]
        turned = jnp.concatenate(rows, axis=0).T
        for d in range(TM):
            s = strip_of(d)
            out[d, tp] = turned[8 * s : 8 * s + 8]
    columns = []
    for x in range(8):
        kind = regime[pl.ds(x, 8, stride=8), :]
        c = jnp.zeros((8, L), jnp.float32)
        for r in range(8):
            c = c + jnp.where(kind == r, rates[r], 0.0)
        columns.append(c)
    columns.append(jnp.zeros((64, L), jnp.float32))
    c_turned = jnp.concatenate(columns, axis=0).T
    rate_rows[...] = c_turned
    sums[0:4, :] = jnp.zeros((4, L), jnp.float32)
    for g in range(4):
        total = jnp.sum(c_turned[32 * g : 32 * g + 32], axis=0, keepdims=True)
        total = jnp.sum(total, axis=1, keepdims=True)
        sums[4 + g : 5 + g, :] = jnp.broadcast_to(total, (1, L))


def transform_kernel(place, received, rate_rows, table, low, high):
    rows = []
    for pair in range(4):
        both = [received[pl.ds(2 * pair + j, 64, stride=8), :] for j in range(2)]
        turned = jnp.concatenate(both, axis=0).T
        rows += list(halves(turned[:64], turned[64:]))
    spectrum = dot(jnp.concatenate(rows, axis=0), table[...], ((1,), (0,)))
    start = pl.multiple_of(place[0] * 8, 8)
    own = rate_rows[pl.ds(start, 8), :]
    for y in range(8):
        part = low if y < 4 else high
        for x in range(8):
            r = (y * 8 + x) * 8
            part[(y % 4) * 8 + x] = spectrum[r : r + 8]
    low[32] = own
    high[32] = pltpu.roll(own, 4, 0)


def x_range(distance):
    return range(distance, SPAN - distance)


def edge_tiles():
    return [(d, y) for d in range(1, WIDTH + 1) for y in x_range(d)]


EDGE = edge_tiles()


def strip_rows(below, low, high, above):
    parts = (below, low, high, above)
    return lambda y, x: parts[y // 4][(y % 4) * 8 + x]


def edge_kernel(below, low, high, above, to_left, to_right):
    tile = strip_rows(below, low, high, above)
    for i, (d, y) in enumerate(EDGE):
        to_left[i] = tile(y, d - 1)
        to_right[i] = tile(y, 8 - d)
    for j, (first, second) in enumerate(((below, low), (high, above))):
        c = jnp.concatenate([first[32][0:4], second[32][0:4]], axis=0)
        to_left[len(EDGE) + j] = c
        to_right[len(EDGE) + j] = c


def solve_kernel(
    valid, below, low, high, above, left, right, lanes, own, total, source, a, b, x0, x1, rate
):
    tile = strip_rows(below, low, high, above)
    zero = jnp.zeros((8, L), jnp.float32)
    for y in range(SPAN):
        for x in range(WIDTH):
            source[y, x] = zero
            source[y, SPAN - 1 - x] = zero
        for x in range(8):
            source[y, WIDTH + x] = tile(y, x)
    for i, (d, y) in enumerate(EDGE):
        source[y, WIDTH - d] = left[i]
        source[y, WIDTH + 7 + d] = right[i]
    lane = lane_index(8)
    for j, (first, second) in enumerate(((below, low), (high, above))):
        mid = jnp.concatenate([first[32][0:4], second[32][0:4]], axis=0)
        c = jnp.where(
            lane < 32,
            pltpu.roll(left[len(EDGE) + j], 96, 1),
            jnp.where(lane < 96, pltpu.roll(mid, 32, 1), pltpu.roll(right[len(EDGE) + j], 96, 1)),
        )
        rate[8 * j : 8 * j + 8, :] = c
    base = lanes[0:1, :] + 6.0
    sine = lanes[1:2, :]
    sine_square = sine * sine

    def prepare(y, carry):
        row = rate[pl.ds(y, 1), :]
        spread = jnp.broadcast_to(row, (L, L)).T
        row_ok = jnp.where(y < WIDTH, valid[2], jnp.where(y < SPAN - WIDTH, 1.0, valid[3]))
        for x in range(SPAN):
            ok = row_ok
            if x < WIDTH:
                ok = row_ok * valid[0]
            elif x >= SPAN - WIDTH:
                ok = row_ok * valid[1]
            d = spread[8 * x : 8 * x + 8] + base
            inverse = ok / (d * d + sine_square)
            ax = d * inverse
            bx = sine * inverse
            a[y, x] = ax
            b[y, x] = bx
            s = source[y, x]
            x0[y, x] = ax * s + bx * pltpu.roll(s, 64, 1)
        return carry

    lax.fori_loop(0, SPAN, prepare, 0)

    def sweep(old, new, margin):
        def row(y, carry):
            for x in range(margin, SPAN - margin):
                v = old[y, x]
                u = source[y, x] + (old[y, x + 1] + old[y, x - 1])
                u = u + (old[y + 1, x] + old[y - 1, x])
                u = u + (pltpu.roll(v, 1, 0) + pltpu.roll(v, 7, 0))
                new[y, x] = a[y, x] * u + b[y, x] * pltpu.roll(u, 64, 1)
            return carry

        lax.fori_loop(margin, SPAN - margin, row, 0)

    sweep(x0, x1, 1)
    sweep(x1, x0, 2)
    sweep(x0, x1, 3)
    lo, hi = WIDTH, WIDTH + BLOCK

    def change(y, x):
        return x1[y, x] - x0[y, x]

    acc = zero
    for y in range(lo - 1, hi + 1):
        line = zero
        for x in range(lo, hi):
            line = line + change(y, x)
        inner = lo <= y < hi
        times = (4 if inner else 0) + (1 if lo - 1 <= y < hi - 1 else 0) + (1 if lo + 1 <= y <= hi else 0)
        acc = acc + float(times) * line
        if inner:
            acc = acc + (change(y, lo - 1) - change(y, lo)) + (change(y, hi) - change(y, hi - 1))
            for x in range(lo, hi):
                own[y - lo, x - lo] = x1[y, x]
    row = jnp.sum(acc, axis=0, keepdims=True)
    for d in range(TM):
        total[d] = row


def gather_kernel(partial, sums, out):
    rows = []
    for g in range(4):
        row = partial[MEMBER[4 * g]]
        for s in range(4 * g + 1, 4 * g + 4):
            row = row + partial[MEMBER[s]]
        rows.append(row)
    block = jnp.concatenate(rows + [sums[4:8, :]], axis=0)
    for j in range(SX * SY):
        out[j] = block


def inverse_of(rows):
    rows = list(rows)
    index = lax.broadcasted_iota(jnp.int32, (8, L), 0)
    for p in range(8):
        here = index == p
        pivot = jnp.broadcast_to(rows[p][p : p + 1], (8, L))
        scale = 1.0 / pivot
        lead = jnp.where(here, scale, rows[p] * scale)
        for r in range(8):
            if r != p:
                factor = jnp.broadcast_to(rows[r][p : p + 1], (8, L))
                rows[r] = jnp.where(here, 0.0, rows[r]) - factor * lead
        rows[p] = lead
    return rows


def apply(rows, v):
    terms = [rows[c] * jnp.broadcast_to(v[c : c + 1], (8, L)) for c in range(8)]
    while len(terms) > 1:
        terms = [terms[i] + terms[i + 1] for i in range(0, len(terms), 2)]
    return terms[0]


def coarse_kernel(place, gathered, field, lanes, table, out, answer):
    index = lax.broadcasted_iota(jnp.int32, (8, L), 0)
    shift = lanes[0:1, :] * float(VOLUME) + float(FACES)

    def right(m):
        return gathered[pl.ds((m // 4) * 8 + m % 4, 8, stride=32), :]

    def block(m, before):
        diagonal = gathered[pl.ds((m // 4) * 8 + 4 + m % 4, 8, stride=32), :] + shift
        rows = []
        for r in range(8):
            row = jnp.where(index == r, diagonal, 0.0)
            row = jnp.where((index == r - 1) | (index == r + 1), -COUPLE_X, row)
            for other in before:
                row = row - (COUPLE_Y * COUPLE_Y) * other[r]
            rows.append(row)
        return rows

    inv, part = {}, {}

    def eliminate(m, sources):
        matrix = inverse_of(block(m, [inv[q] for q in sources]))
        rhs = right(m)
        for q in sources:
            rhs = rhs + COUPLE_Y * part[q]
        inv[m] = matrix
        part[m] = apply(matrix, rhs)

    for i in range(8):
        if i < 7:
            eliminate(i, [i - 1] if i else [])
        eliminate(15 - i, [16 - i] if i else [])
    eliminate(7, [6, 8])
    solved = {7: part[7]}
    for i in range(1, 9):
        for m, q in ((7 - i, 8 - i), (7 + i, 6 + i)):
            if 0 <= m < 16:
                solved[m] = part[m] + COUPLE_Y * apply(inv[m], solved[q])
    for m in range(16):
        answer[8 * m : 8 * m + 8, :] = solved[m]
    mine = answer[pl.ds(place[1], 1), :]
    corrected = field[...] + mine
    result = dot(table[...], corrected, ((1,), (1,)))
    for pair in range(4):
        cut = result[:, 128 * pair : 128 * pair + 128]
        for j, value in enumerate(halves(cut[:64], cut[64:])):
            out[pl.ds(2 * pair + j, 64, stride=8), :] = value


def unpack_kernel(received, out):
    for tp in range(4):
        rows = [received[MEMBER[s], tp] for s in range(TM)]
        turned = jnp.concatenate(rows, axis=0).T
        for t2 in range(2):
            for x in range(8):
                r = t2 * 64 + x * 8
                out[pl.ds((2 * tp + t2) * 64 + x, 8, stride=8), :] = turned[r : r + 8]


def call(kernel, name, out_shape, scalars, arrays, scratch=()):
    outs = out_shape if isinstance(out_shape, tuple) else (out_shape,)
    return pl.pallas_call(
        kernel,
        name=name,
        out_shape=out_shape,
        in_specs=smem(len(scalars)) + vmem(len(arrays)),
        out_specs=tuple(vmem(len(outs))) if isinstance(out_shape, tuple) else vmem(1)[0],
        scratch_shapes=list(scratch),
        interpret=INTERPRET,
    )(*scalars, *arrays)


def y_steps():
    def rank(g):
        return MEMBER[g % TM] * SY + g // TM

    return [(rank(g), rank(g + 1)) for g in range(SY * TM - 1)]


def local(driving_input, regime, reaction_rates):
    tm, sx, sy = (lax.axis_index(n) for n in ("tm", "sx", "sy"))
    strip = jnp.where(tm % 2 == 0, tm // 2, TM - 1 - tm // 2)
    place = jnp.stack([strip, (sy * 4 + strip // 4) * 8 + sx]).astype(jnp.int32)
    inside = jnp.stack(
        [sx > 0, sx < SX - 1, (sy > 0) | (strip > 0), (sy < SY - 1) | (strip < TM - 1)]
    ).astype(jnp.float32)
    forward, inverse, lanes = jnp.asarray(FORWARD), jnp.asarray(INVERSE), jnp.asarray(LANES)

    packed, rate_rows, sums = call(
        pack_kernel,
        "pack",
        (shape(TM, 4, 8, L), shape(L, L), shape(8, L)),
        [reaction_rates],
        [driving_input.reshape(512, L), regime.reshape(64, L)],
    )
    received = lax.all_to_all(packed, "tm", split_axis=0, concat_axis=0, tiled=True)
    low, high = call(
        transform_kernel,
        "transform",
        (shape(33, 8, L), shape(33, 8, L)),
        [place],
        [received.reshape(512, L), rate_rows, forward],
    )
    up = y_steps()
    below = lax.ppermute(high, ("tm", "sy"), up)
    above = lax.ppermute(low, ("tm", "sy"), [(q, p) for p, q in up])
    tiles = len(EDGE) + 2
    to_left, to_right = call(
        edge_kernel, "edges", (shape(tiles, 8, L),) * 2, [], [below, low, high, above]
    )
    across = [(i, i + 1) for i in range(SX - 1)]
    left = lax.ppermute(to_right, "sx", across)
    right = lax.ppermute(to_left, "sx", [(q, p) for p, q in across])
    big = pltpu.VMEM((SPAN, SPAN, 8, L), jnp.float32)
    own, total = call(
        solve_kernel,
        "sweeps",
        (shape(8, 8, 8, L), shape(TM, 1, L)),
        [inside],
        [below, low, high, above, left, right, lanes],
        [big] * 5 + [pltpu.VMEM((SPAN, L), jnp.float32)],
    )
    partial = lax.all_to_all(total, "tm", split_axis=0, concat_axis=0, tiled=True)
    shared = call(gather_kernel, "gather", shape(SX * SY, 8, L), [], [partial, sums])
    gathered = lax.all_to_all(shared, ("sx", "sy"), split_axis=0, concat_axis=0, tiled=True)
    back = call(
        coarse_kernel,
        "coarse",
        shape(512, L),
        [place],
        [gathered.reshape(256, L), own.reshape(512, L), lanes, inverse],
        [pltpu.VMEM((L, L), jnp.float32)],
    )
    returned = lax.all_to_all(
        back.reshape(TM, 4, 8, L), "tm", split_axis=0, concat_axis=0, tiled=True
    )
    result = call(unpack_kernel, "unpack", shape(512, L), [], [returned])
    return result.reshape(driving_input.shape)


def solution(mesh):
    placed = (P("tm", None, "sx", "sy"), P(None, "sx", "sy"), P())
    return jax.shard_map(
        local, mesh=mesh, in_specs=placed, out_specs=P("tm", None, "sx", "sy"), check_vma=False
    )
```

time: 243 us -> 120 us (0.49)
  waiting for transfers between devices: 70.1 us -> 18.9 us
  starting transfers between devices: 67.7 us -> 22.5 us
  other arithmetic: 37.5 us -> 1.24 us
  Pallas kernels: 0 us -> 19.4 us
  local copies, waits for them, and re-layouts: 10.4 us -> 2.03 us
  blocking collectives: 51.4 us -> 55.5 us
  matrix products: 2.91 us -> 0 us
    ppermute x16 -> x4, starting transfers between devices: 47.5 us -> 12.3 us  [the longest x1 5.15 us: local(): above = lax.ppermute(low, ('tm', 'sy'), [(q, p) for p, q in up])]
    all_to_all x4 -> x1, waiting for transfers between devices: 38.1 us -> 11.4 us  [local(): lax.all_to_all(packed, 'tm', split_axis=0, concat_axis=0, tiled=True)]
    another operation x22 -> x1, other arithmetic: 25.2 us -> 0.66 us  [local(): place = jnp.stack([strip, (sy * 4 + strip // 4) * 8 + sx]).astype(jnp.int32)]
    ppermute x16 -> x4, waiting for transfers between devices: 32.1 us -> 7.54 us  [the longest x1 4.35 us: local(): right = lax.ppermute(to_left, 'sx', [(q, p) for p, q in across])]
    pallas_call x0 -> x7, Pallas kernels: none -> 19.4 us  [call(): pl.pallas_call(kernel, name=name, out_shape=out_shape, in_specs=smem(len(...]
    all_to_all x4 -> x1, starting transfers between devices: 20.3 us -> 10.2 us  [local(): lax.all_to_all(packed, 'tm', split_axis=0, concat_axis=0, tiled=True)]
    reduce_sum x4 -> x0, other arithmetic: 6.14 us -> none  [aggregate(): return jnp.sum(blocks, axis=(-5, -3, -1)).reshape(leading + (per_device,))]
    all_to_all x3, blocking collectives: 51.4 us -> 55.5 us  [the longest x1 21.5 us: local(): lax.all_to_all(shared, ('sx', 'sy'), split_axis=0, concat_axis=0, tiled=T...]
  transfers between devices with their start and end apart: 20 -> 5, of which waited for: 8 -> 5; matrix products, arithmetic and copies ran while one was open for 3% -> 1% of each run, Pallas kernels for 0% -> 0%
where the time goes in v1:
time: 120 us
  blocking collectives  55.5 us (46%)
  starting transfers between devices  22.5 us (19%)
  Pallas kernels  19.4 us (16%)
  waiting for transfers between devices  18.9 us (16%)
  local copies, waits for them, and re-layouts  2.03 us (2%)
  other arithmetic  1.24 us (1%)
    all_to_all x1, blocking collectives, local(): lax.all_to_all(shared, ('sx', 'sy'), split_axis=0, concat_axis=0, tiled=T...  21.5 us
    pallas_call x7, Pallas kernels, call(): pl.pallas_call(kernel, name=name, out_shape=out_shape, in_specs=smem(len(...  19.4 us
    all_to_all x1, blocking collectives, local(): lax.all_to_all(total, 'tm', split_axis=0, concat_axis=0, tiled=True)  17 us
    all_to_all x1, blocking collectives, local(): lax.all_to_all(back.reshape(TM, 4, 8, L), 'tm', split_axis=0, concat_axis...  16.9 us
    all_to_all x1, waiting for transfers between devices, local(): lax.all_to_all(packed, 'tm', split_axis=0, concat_axis=0, tiled=True)  11.4 us
    all_to_all x1, starting transfers between devices, local(): lax.all_to_all(packed, 'tm', split_axis=0, concat_axis=0, tiled=True)  10.2 us
    ppermute x1, starting transfers between devices, local(): above = lax.ppermute(low, ('tm', 'sy'), [(q, p) for p, q in up])  5.15 us
    ppermute x1, waiting for transfers between devices, local(): right = lax.ppermute(to_left, 'sx', [(q, p) for p, q in across])  4.35 us
  transfers between devices with their start and end apart: 5, of which 5 were waited for; matrix products, arithmetic and copies ran while one was open for 1% of the time, Pallas kernels for 0%

profile of v1, /device:TPU:1, one launch (start us, length us, event | category | flops | bytes accessed | tf_op | source)
XLA Modules:
  0.0 119.7 jit_solution(11637025605622064241)
XLA Ops:
  0.0 1.9 %pack.1 = (f32[16,4,8,128]{3,2,1,0:T(8,128)}, f32[128,128]{1,0:T(8,128)}, f32[8,128]{1,0:T(8,128)}) custom-call(f32[8]{0:T(128)} %rates.1, f32[512,128]{1,0:T(8,128)} %bitcast.16, s32[64,128]{1,0:T(8,128)} %bitcast.18), custom_call_target="tpu_custom_call" | custom-call | tf_op jit(solution)/shard_map/pack/pallas_call | solution.py:339
  1.9 10.2 %all-to-all-start = ((f32[16,4,8,128]{3,2,1,0:T(8,128)}), f32[16,4,8,128]{3,2,1,0:T(8,128)S(1)}, u32[]{:S(2)}, u32[]{:S(2)}) async-start(f32[16,4,8,128]{3,2,1,0:T(8,128)} %get-tuple-element.14), calls=%async_computation | async-start | bytes 524288 | tf_op jit(solution)/shard_map/all_to_all | solution.py:373
  12.2 0.7 pad_add_fusion.place
  12.8 11.4 %all-to-all-done = f32[16,4,8,128]{3,2,1,0:T(8,128)S(1)} async-done(((f32[16,4,8,128]{3,2,1,0:T(8,128)}), f32[16,4,8,128]{3,2,1,0:T(8,128)S(1)}, u32[]{:S(2)}, u32[]{:S(2)}) %all-to-all-start) | async-done | bytes 262176 | tf_op jit(solution)/shard_map/all_to_all | solution.py:373
  24.2 0.0 copy-start
  24.2 0.7 copy-done
  24.9 2.3 %transform.1 = (f32[33,8,128]{2,1,0:T(8,128)}, f32[33,8,128]{2,1,0:T(8,128)}) custom-call(s32[2]{0:T(128)} %pad_add_fusion.place, f32[512,128]{1,0:T(8,128)} %bitcast.13, f32[128,128]{1,0:T(8,128)} %get-tuple-element.15.rate_rows, f32[128,128]{1,0:T(8,128)} %constant.66.clone.table), custom_call_target="tpu_custom_call" | custom-call | tf_op jit(solution)/shard_map/transform/pallas_call | solution.py:339
  27.2 1.9 %collective-permute-start = (f32[33,8,128]{2,1,0:T(8,128)}, f32[33,8,128]{2,1,0:T(8,128)S(1)}, u32[]{:S(2)}, u32[]{:S(2)}) collective-permute-start(f32[33,8,128]{2,1,0:T(8,128)} %get-tuple-element.16.high), channel_id=1, source_target_pairs={{0,64},{64,128},{128,192},{192,256},{256,320},{320,384},{384,448},... | collective-permute-start | bytes 405512 | tf_op jit(solution)/shard_map/ppermute | solution.py:382
  29.1 5.1 %collective-permute-start.1 = (f32[33,8,128]{2,1,0:T(8,128)}, f32[33,8,128]{2,1,0:T(8,128)S(1)}, u32[]{:S(2)}, u32[]{:S(2)}) collective-permute-start(f32[33,8,128]{2,1,0:T(8,128)} %get-tuple-element.17.low), channel_id=1, source_target_pairs={{64,0},{128,64},{192,128},{256,192},{320,256},{384,320},{448,384},... | collective-permute-start | bytes 405512 | tf_op jit(solution)/shard_map/ppermute | solution.py:383
  34.2 1.0 collective-permute-done.below
  35.2 0.0 copy-start.1
  35.2 1.3 %collective-permute-done.1.above = f32[33,8,128]{2,1,0:T(8,128)S(1)} collective-permute-done((f32[33,8,128]{2,1,0:T(8,128)}, f32[33,8,128]{2,1,0:T(8,128)S(1)}, u32[]{:S(2)}, u32[]{:S(2)}) %collective-permute-start.1) | collective-permute-done | bytes 135200 | tf_op jit(solution)/shard_map/ppermute | solution.py:383
  36.5 0.0 copy-done.1
  36.5 0.0 copy-start.2
  36.5 0.6 copy-done.2
  37.2 1.9 %edges.1 = (f32[46,8,128]{2,1,0:T(8,128)}, f32[46,8,128]{2,1,0:T(8,128)}) custom-call(f32[33,8,128]{2,1,0:T(8,128)} %copy-done.1, f32[33,8,128]{2,1,0:T(8,128)} %get-tuple-element.17.low, f32[33,8,128]{2,1,0:T(8,128)} %get-tuple-element.16.high, f32[33,8,128]{2,1,0:T(8,128)} %copy-done.2), custom_call_target="tpu_custom_call" | custom-call | tf_op jit(solution)/shard_map/edges/pallas_call | solution.py:339
  39.0 4.0 %collective-permute-start.2 = (f32[46,8,128]{2,1,0:T(8,128)}, f32[46,8,128]{2,1,0:T(8,128)S(1)}, u32[]{:S(2)}, u32[]{:S(2)}) collective-permute-start(f32[46,8,128]{2,1,0:T(8,128)} %get-tuple-element.18), channel_id=1, source_target_pairs={{0,4},{4,8},{8,12},{12,16},{16,20},{20,24},{24,28},{1,5},{5,9},{9,... | collective-permute-start | bytes 565256 | tf_op jit(solution)/shard_map/ppermute | solution.py:389
  43.0 1.3 %collective-permute-start.3 = (f32[46,8,128]{2,1,0:T(8,128)}, f32[46,8,128]{2,1,0:T(8,128)S(1)}, u32[]{:S(2)}, u32[]{:S(2)}) collective-permute-start(f32[46,8,128]{2,1,0:T(8,128)} %get-tuple-element.19), channel_id=1, source_target_pairs={{4,0},{8,4},{12,8},{16,12},{20,16},{24,20},{28,24},{5,1},{9,5},{13... | collective-permute-start | bytes 565256 | tf_op jit(solution)/shard_map/ppermute | solution.py:390
  44.4 0.6 add_convert_fusion.valid
  45.0 0.9 collective-permute-done.2.left
  45.9 0.0 copy-start.3
  45.9 4.4 %collective-permute-done.3.right = f32[46,8,128]{2,1,0:T(8,128)S(1)} collective-permute-done((f32[46,8,128]{2,1,0:T(8,128)}, f32[46,8,128]{2,1,0:T(8,128)S(1)}, u32[]{:S(2)}, u32[]{:S(2)}) %collective-permute-start.3) | collective-permute-done | bytes 188448 | tf_op jit(solution)/shard_map/ppermute | solution.py:390
  50.2 0.0 copy-done.3
  50.2 0.0 copy-start.4
  50.2 0.7 copy-done.4
  50.9 7.1 %sweeps.1 = (f32[8,8,8,128]{3,2,1,0:T(8,128)}, f32[16,1,128]{2,1,0:T(1,128)}) custom-call(f32[4]{0:T(128)} %add_convert_fusion.valid, f32[33,8,128]{2,1,0:T(8,128)} %copy-done.1, f32[33,8,128]{2,1,0:T(8,128)} %get-tuple-element.17.low, f32[33,8,128]{2,1,0:T(8,128)} %get-tuple-element.16.high, f32[33,8,128]{2,1,0:T(8,128)} %copy-done.2, ...), custom_call_target="tpu_custom_call" | custom-call | tf_op jit(solution)/shard_map/sweeps/pallas_call | solution.py:339
  58.0 17.0 %all_to_all.20.partial = f32[16,1,128]{2,1,0:T(1,128)} all-to-all(f32[16,1,128]{2,1,0:T(1,128)} %get-tuple-element.20), channel_id=1, replica_groups=mesh['tm'=16,'sx'=8,'sy'=4] {'tm'}, dimensions={0} | all-to-all | bytes 16384 | tf_op jit(solution)/shard_map/all_to_all | solution.py:400
  75.0 1.4 %gather.1 = f32[32,8,128]{2,1,0:T(8,128)} custom-call(f32[16,1,128]{2,1,0:T(1,128)} %all_to_all.20.partial, f32[8,128]{1,0:T(8,128)} %get-tuple-element.21.sums), custom_call_target="tpu_custom_call" | custom-call | tf_op jit(solution)/shard_map/gather/pallas_call | solution.py:339
  76.4 21.5 %all_to_all.21 = f32[32,8,128]{2,1,0:T(8,128)} all-to-all(f32[32,8,128]{2,1,0:T(8,128)} %gather.1), channel_id=1, replica_groups=mesh['tm'=16,'sx'=8,'sy'=4] {'sx','sy'}, dimensions={0} | all-to-all | bytes 262144 | tf_op jit(solution)/shard_map/all_to_all | solution.py:402
  97.9 3.1 %coarse.1 = f32[512,128]{1,0:T(8,128)} custom-call(s32[2]{0:T(128)} %pad_add_fusion.place, f32[256,128]{1,0:T(8,128)} %bitcast.15, f32[512,128]{1,0:T(8,128)} %bitcast.17, f32[8,128]{1,0:T(8,128)} %constant.68.clone.lanes, f32[128,128]{1,0:T(8,128)} %constant.67.clone.table), custom_call_target="tpu_custom_call" | custom-call | tf_op jit(solution)/shard_map/coarse/pallas_call | solution.py:339
  101.0 16.9 %all_to_all.22.received = f32[16,4,8,128]{3,2,1,0:T(8,128)} all-to-all(f32[16,4,8,128]{3,2,1,0:T(8,128)} %bitcast.14), channel_id=1, replica_groups=mesh['tm'=16,'sx'=8,'sy'=4] {'tm'}, dimensions={0} | all-to-all | bytes 524288 | tf_op jit(solution)/shard_map/all_to_all | solution.py:411
  118.0 1.8 %unpack.1 = f32[512,128]{1,0:T(8,128)} custom-call(f32[16,4,8,128]{3,2,1,0:T(8,128)} %all_to_all.22.received), custom_call_target="tpu_custom_call" | custom-call | tf_op jit(solution)/shard_map/unpack/pallas_call | solution.py:339
Async XLA Ops:
  1.9 22.3 %all-to-all-start = ((f32[16,4,8,128]{3,2,1,0:T(8,128)}), f32[16,4,8,128]{3,2,1,0:T(8,128)S(1)}, u32[]{:S(2)}, u32[]{:S(2)}) async-start(f32[16,4,8,128]{3,2,1,0:T(8,128)} %get-tuple-element.14), calls=%async_computation | async-start | bytes 524288 | tf_op jit(solution)/shard_map/all_to_all | solution.py:373
  24.2 0.7 copy-start
  27.2 8.0 %collective-permute-start = (f32[33,8,128]{2,1,0:T(8,128)}, f32[33,8,128]{2,1,0:T(8,128)S(1)}, u32[]{:S(2)}, u32[]{:S(2)}) collective-permute-start(f32[33,8,128]{2,1,0:T(8,128)} %get-tuple-element.16.high), channel_id=1, source_target_pairs={{0,64},{64,128},{128,192},{192,256},{256,320},{320,384},{384,448},... | collective-permute-start | bytes 405512 | tf_op jit(solution)/shard_map/ppermute | solution.py:382
  29.1 7.4 %collective-permute-start.1 = (f32[33,8,128]{2,1,0:T(8,128)}, f32[33,8,128]{2,1,0:T(8,128)S(1)}, u32[]{:S(2)}, u32[]{:S(2)}) collective-permute-start(f32[33,8,128]{2,1,0:T(8,128)} %get-tuple-element.17.low), channel_id=1, source_target_pairs={{64,0},{128,64},{192,128},{256,192},{320,256},{384,320},{448,384},... | collective-permute-start | bytes 405512 | tf_op jit(solution)/shard_map/ppermute | solution.py:383
  35.2 1.3 %copy-start.1 = (f32[33,8,128]{2,1,0:T(8,128)}, f32[33,8,128]{2,1,0:T(8,128)S(1)}, u32[]{:S(2)}) copy-start(f32[33,8,128]{2,1,0:T(8,128)S(1)} %collective-permute-done.below) | copy-start | bytes 405508
  36.5 0.6 copy-start.2
  39.0 6.8 %collective-permute-start.2 = (f32[46,8,128]{2,1,0:T(8,128)}, f32[46,8,128]{2,1,0:T(8,128)S(1)}, u32[]{:S(2)}, u32[]{:S(2)}) collective-permute-start(f32[46,8,128]{2,1,0:T(8,128)} %get-tuple-element.18), channel_id=1, source_target_pairs={{0,4},{4,8},{8,12},{12,16},{16,20},{20,24},{24,28},{1,5},{5,9},{9,... | collective-permute-start | bytes 565256 | tf_op jit(solution)/shard_map/ppermute | solution.py:389
  43.0 7.2 %collective-permute-start.3 = (f32[46,8,128]{2,1,0:T(8,128)}, f32[46,8,128]{2,1,0:T(8,128)S(1)}, u32[]{:S(2)}, u32[]{:S(2)}) collective-permute-start(f32[46,8,128]{2,1,0:T(8,128)} %get-tuple-element.19), channel_id=1, source_target_pairs={{4,0},{8,4},{12,8},{16,12},{20,16},{24,20},{28,24},{5,1},{9,5},{13... | collective-permute-start | bytes 565256 | tf_op jit(solution)/shard_map/ppermute | solution.py:390
  45.9 4.4 %copy-start.3 = (f32[46,8,128]{2,1,0:T(8,128)}, f32[46,8,128]{2,1,0:T(8,128)S(1)}, u32[]{:S(2)}) copy-start(f32[46,8,128]{2,1,0:T(8,128)S(1)} %collective-permute-done.2.left) | copy-start | bytes 565252
  50.2 0.7 copy-start.4

commit v2 on v1

--- a/solution.py
+++ b/solution.py
@@ -16,7 +16,7 @@
 VOLUME = 8 * 32 * NZ
 COUPLE_X = 32.0 * NZ
 COUPLE_Y = 8.0 * NZ
-INTERPRET = False
+TILES = 5
 
 
 def strip_of(d):
@@ -46,11 +46,13 @@
     lanes = np.zeros((8, L))
     lanes[0] = shift
     lanes[1] = sine
+    padded = np.zeros((2, TM, TILES, L))
+    padded[:, :, :4] = inverse[order].reshape(2, TM, 4, L)
     as32 = lambda a: np.asarray(a, np.float32)
-    return as32(forward[order]), as32(inverse[order]), as32(lanes)
-
-
-FORWARD, INVERSE, LANES = tables()
+    return as32(forward[order]), as32(padded.reshape(-1, L)), as32(inverse), as32(lanes)
+
+
+FORWARD, INVERSE, NATURAL, LANES = tables()
 
 
 def vmem(count):
@@ -109,15 +111,19 @@
         sums[4 + g : 5 + g, :] = jnp.broadcast_to(total, (1, L))
 
 
-def transform_kernel(place, received, rate_rows, table, low, high):
+def own_strip():
+    tm = lax.axis_index("tm")
+    return jnp.where(tm & 1 == 0, tm >> 1, TM - 1 - (tm >> 1))
+
+
+def transform_kernel(received, rate_rows, table, low, high):
     rows = []
     for pair in range(4):
         both = [received[pl.ds(2 * pair + j, 64, stride=8), :] for j in range(2)]
         turned = jnp.concatenate(both, axis=0).T
         rows += list(halves(turned[:64], turned[64:]))
     spectrum = dot(jnp.concatenate(rows, axis=0), table[...], ((1,), (0,)))
-    start = pl.multiple_of(place[0] * 8, 8)
-    own = rate_rows[pl.ds(start, 8), :]
+    own = rate_rows[pl.ds(pl.multiple_of(own_strip() * 8, 8), 8), :]
     for y in range(8):
         part = low if y < 4 else high
         for x in range(8):
@@ -155,8 +161,18 @@
 
 
 def solve_kernel(
-    valid, below, low, high, above, left, right, lanes, own, total, source, a, b, x0, x1, rate
+    below, low, high, above, left, right, lanes, table, out, source, a, b, x0, x1, rate
 ):
+    sx, sy, strip = lax.axis_index("sx"), lax.axis_index("sy"), own_strip()
+    valid = [
+        jnp.where(inside, 1.0, 0.0)
+        for inside in (
+            sx > 0,
+            sx < SX - 1,
+            (sy > 0) | (strip > 0),
+            (sy < SY - 1) | (strip < TM - 1),
+        )
+    ]
     tile = strip_rows(below, low, high, above)
     zero = jnp.zeros((8, L), jnp.float32)
     for y in range(SPAN):
@@ -233,19 +249,23 @@
         acc = acc + float(times) * line
         if inner:
             acc = acc + (change(y, lo - 1) - change(y, lo)) + (change(y, hi) - change(y, hi - 1))
-            for x in range(lo, hi):
-                own[y - lo, x - lo] = x1[y, x]
-    row = jnp.sum(acc, axis=0, keepdims=True)
+    own = x1[lo:hi, lo:hi].reshape(512, L)
+    result = dot(table[...], own, ((1,), (1,)))
+    for pair in range(4):
+        cut = result[:, 128 * pair : 128 * pair + 128]
+        for j, value in enumerate(halves(cut[: TM * TILES], cut[TM * TILES :])):
+            out[pl.ds(2 * pair + j, TM * TILES, stride=8), :] = value
+    row = jnp.broadcast_to(jnp.sum(acc, axis=0, keepdims=True), (8, L))
     for d in range(TM):
-        total[d] = row
-
-
-def gather_kernel(partial, sums, out):
+        out[8 * (TILES * d + 4) : 8 * (TILES * d + 5), :] = row
+
+
+def gather_kernel(received, sums, out):
     rows = []
     for g in range(4):
-        row = partial[MEMBER[4 * g]]
+        row = received[MEMBER[4 * g], 4][0:1]
         for s in range(4 * g + 1, 4 * g + 4):
-            row = row + partial[MEMBER[s]]
+            row = row + received[MEMBER[s], 4][0:1]
         rows.append(row)
     block = jnp.concatenate(rows + [sums[4:8, :]], axis=0)
     for j in range(SX * SY):
@@ -275,7 +295,7 @@
     return terms[0]
 
 
-def coarse_kernel(place, gathered, field, lanes, table, out, answer):
+def coarse_kernel(gathered, field, lanes, table, out, answer):
     index = lax.broadcasted_iota(jnp.int32, (8, L), 0)
     shift = lanes[0:1, :] * float(VOLUME) + float(FACES)
 
@@ -315,13 +335,16 @@
                 solved[m] = part[m] + COUPLE_Y * apply(inv[m], solved[q])
     for m in range(16):
         answer[8 * m : 8 * m + 8, :] = solved[m]
-    mine = answer[pl.ds(place[1], 1), :]
-    corrected = field[...] + mine
-    result = dot(table[...], corrected, ((1,), (1,)))
-    for pair in range(4):
-        cut = result[:, 128 * pair : 128 * pair + 128]
-        for j, value in enumerate(halves(cut[:64], cut[64:])):
-            out[pl.ds(2 * pair + j, 64, stride=8), :] = value
+    sx, sy = lax.axis_index("sx"), lax.axis_index("sy")
+    own = table[pl.ds(pl.multiple_of(lax.axis_index("tm") * 8, 8), 8), :]
+    group = lane_index(8) // 32
+    added = jnp.zeros((8, L), jnp.float32)
+    for g in range(4):
+        y = answer[pl.ds((sy * 4 + g) * 8 + sx, 1), :]
+        value = jnp.sum(own * y, axis=1, keepdims=True)
+        added = jnp.where(group == g, value, added)
+    for t in range(8):
+        out[64 * t : 64 * t + 64, :] = field[64 * t : 64 * t + 64, :] + added[t : t + 1, :]
 
 
 def unpack_kernel(received, out):
@@ -334,16 +357,21 @@
                 out[pl.ds((2 * tp + t2) * 64 + x, 8, stride=8), :] = turned[r : r + 8]
 
 
-def call(kernel, name, out_shape, scalars, arrays, scratch=()):
-    outs = out_shape if isinstance(out_shape, tuple) else (out_shape,)
+def call(kernel, name, out_shape, arrays, scratch=(), rates=None, keep=True, flops=0):
+    if keep:
+        out_shape = jax.tree.map(lambda o: pltpu.VMEM(o.shape, o.dtype), out_shape)
+    if rates is None:
+        arrays = [pltpu.with_memory_space_constraint(x, pltpu.VMEM) for x in arrays]
+    scalars = [] if rates is None else [rates]
+    many = isinstance(out_shape, tuple)
     return pl.pallas_call(
         kernel,
         name=name,
         out_shape=out_shape,
         in_specs=smem(len(scalars)) + vmem(len(arrays)),
-        out_specs=tuple(vmem(len(outs))) if isinstance(out_shape, tuple) else vmem(1)[0],
+        out_specs=tuple(vmem(len(out_shape))) if many else vmem(1)[0],
         scratch_shapes=list(scratch),
-        interpret=INTERPRET,
+        cost_estimate=pl.CostEstimate(flops=flops, transcendentals=0, bytes_accessed=0),
     )(*scalars, *arrays)
 
 
@@ -355,27 +383,19 @@
 
 
 def local(driving_input, regime, reaction_rates):
-    tm, sx, sy = (lax.axis_index(n) for n in ("tm", "sx", "sy"))
-    strip = jnp.where(tm % 2 == 0, tm // 2, TM - 1 - tm // 2)
-    place = jnp.stack([strip, (sy * 4 + strip // 4) * 8 + sx]).astype(jnp.int32)
-    inside = jnp.stack(
-        [sx > 0, sx < SX - 1, (sy > 0) | (strip > 0), (sy < SY - 1) | (strip < TM - 1)]
-    ).astype(jnp.float32)
-    forward, inverse, lanes = jnp.asarray(FORWARD), jnp.asarray(INVERSE), jnp.asarray(LANES)
-
+    forward, inverse, natural, lanes = (jnp.asarray(t) for t in (FORWARD, INVERSE, NATURAL, LANES))
     packed, rate_rows, sums = call(
         pack_kernel,
         "pack",
         (shape(TM, 4, 8, L), shape(L, L), shape(8, L)),
-        [reaction_rates],
         [driving_input.reshape(512, L), regime.reshape(64, L)],
+        rates=reaction_rates,
     )
     received = lax.all_to_all(packed, "tm", split_axis=0, concat_axis=0, tiled=True)
     low, high = call(
         transform_kernel,
         "transform",
         (shape(33, 8, L), shape(33, 8, L)),
-        [place],
         [received.reshape(512, L), rate_rows, forward],
     )
     up = y_steps()
@@ -383,35 +403,33 @@
     above = lax.ppermute(low, ("tm", "sy"), [(q, p) for p, q in up])
     tiles = len(EDGE) + 2
     to_left, to_right = call(
-        edge_kernel, "edges", (shape(tiles, 8, L),) * 2, [], [below, low, high, above]
+        edge_kernel, "edges", (shape(tiles, 8, L),) * 2, [below, low, high, above]
     )
     across = [(i, i + 1) for i in range(SX - 1)]
     left = lax.ppermute(to_right, "sx", across)
     right = lax.ppermute(to_left, "sx", [(q, p) for p, q in across])
     big = pltpu.VMEM((SPAN, SPAN, 8, L), jnp.float32)
-    own, total = call(
+    message = call(
         solve_kernel,
         "sweeps",
-        (shape(8, 8, 8, L), shape(TM, 1, L)),
-        [inside],
-        [below, low, high, above, left, right, lanes],
+        shape(TM * TILES * 8, L),
+        [below, low, high, above, left, right, lanes, inverse],
         [big] * 5 + [pltpu.VMEM((SPAN, L), jnp.float32)],
     )
-    partial = lax.all_to_all(total, "tm", split_axis=0, concat_axis=0, tiled=True)
-    shared = call(gather_kernel, "gather", shape(SX * SY, 8, L), [], [partial, sums])
+    returned = lax.all_to_all(
+        message.reshape(TM, TILES, 8, L), "tm", split_axis=0, concat_axis=0, tiled=True
+    )
+    shared = call(gather_kernel, "gather", shape(SX * SY, 8, L), [returned, sums])
     gathered = lax.all_to_all(shared, ("sx", "sy"), split_axis=0, concat_axis=0, tiled=True)
-    back = call(
+    field = call(unpack_kernel, "unpack", shape(512, L), [returned], flops=10**8)
+    result = call(
         coarse_kernel,
         "coarse",
         shape(512, L),
-        [place],
-        [gathered.reshape(256, L), own.reshape(512, L), lanes, inverse],
+        [gathered.reshape(256, L), field, lanes, natural],
         [pltpu.VMEM((L, L), jnp.float32)],
-    )
-    returned = lax.all_to_all(
-        back.reshape(TM, 4, 8, L), "tm", split_axis=0, concat_axis=0, tiled=True
-    )
-    result = call(unpack_kernel, "unpack", shape(512, L), [], [returned])
+        keep=False,
+    )
     return result.reshape(driving_input.shape)
 
 

time: 120 us -> 95.3 us (0.79)
  blocking collectives: 55.5 us -> 42.7 us
  Pallas kernels: 19.4 us -> 10.1 us
  starting transfers between devices: 22.5 us -> 25.4 us
  waiting for transfers between devices: 18.9 us -> 16.7 us
  local copies, waits for them, and re-layouts: 2.03 us -> 0.02 us
  other arithmetic: 1.24 us -> 0 us
    all_to_all x3 -> x2, blocking collectives: 55.5 us -> 42.7 us  [the longest x1 22.2 us: local(): lax.all_to_all(packed, 'tm', split_axis=0, concat_axis=0, tiled=True)]
    pallas_call x7, Pallas kernels: 19.4 us -> 10.1 us  [call(): pl.pallas_call(kernel, name=name, out_shape=out_shape, in_specs=smem(len(...]
    all_to_all x1, starting transfers between devices: 10.2 us -> 12.9 us  [local(): lax.all_to_all(shared, ('sx', 'sy'), split_axis=0, concat_axis=0, tiled=T...]
    all_to_all x1, waiting for transfers between devices: 11.4 us -> 9.08 us  [local(): lax.all_to_all(shared, ('sx', 'sy'), split_axis=0, concat_axis=0, tiled=T...]
    unnamed x10 -> x8, local copies, waits for them, and re-layouts: 2.03 us -> 0.02 us
  transfers between devices with their start and end apart: 5 -> 5, of which waited for: 5 -> 5; matrix products, arithmetic and copies ran while one was open for 1% -> 0% of each run, Pallas kernels for 0% -> 0%
where the time goes in v2:
time: 95.3 us; the launch traced here: 94.9 us
  blocking collectives  42.7 us (45%)
  starting transfers between devices  25.4 us (27%)
  waiting for transfers between devices  16.7 us (18%)
  Pallas kernels  10.1 us (11%)
    all_to_all x1, blocking collectives, local(): lax.all_to_all(packed, 'tm', split_axis=0, concat_axis=0, tiled=True)  22.2 us
    all_to_all x1, blocking collectives, local(): lax.all_to_all(message.reshape(TM, TILES, 8, L), 'tm', split_axis=0, conc...  20.5 us
    all_to_all x1, starting transfers between devices, local(): lax.all_to_all(shared, ('sx', 'sy'), split_axis=0, concat_axis=0, tiled=T...  12.9 us
    pallas_call x7, Pallas kernels, call(): pl.pallas_call(kernel, name=name, out_shape=out_shape, in_specs=smem(len(...  10.1 us
    all_to_all x1, waiting for transfers between devices, local(): lax.all_to_all(shared, ('sx', 'sy'), split_axis=0, concat_axis=0, tiled=T...  9.08 us
    ppermute x1, starting transfers between devices, local(): above = lax.ppermute(low, ('tm', 'sy'), [(q, p) for p, q in up])  5.28 us
    ppermute x1, waiting for transfers between devices, local(): right = lax.ppermute(to_left, 'sx', [(q, p) for p, q in across])  4.46 us
    ppermute x1, starting transfers between devices, local(): left = lax.ppermute(to_right, 'sx', across)  4.01 us
  transfers between devices with their start and end apart: 5, of which 5 were waited for; matrix products, arithmetic and copies ran while one was open for 0% of the time, Pallas kernels for 0%

profile of v2, /device:TPU:1, one launch (start us, length us, event | category | flops | bytes accessed | tf_op | source)
XLA Modules:
  0.0 94.9 jit_solution(7560600810537297409)
XLA Ops:
  0.0 1.2 %pack.1 = (f32[16,4,8,128]{3,2,1,0:T(8,128)S(1)}, f32[128,128]{1,0:T(8,128)S(1)}, f32[8,128]{1,0:T(8,128)S(1)}) custom-call(f32[8]{0:T(128)} %rates.1, f32[512,128]{1,0:T(8,128)} %bitcast.9, s32[64,128]{1,0:T(8,128)} %bitcast.10), custom_call_target="tpu_custom_call" | custom-call | tf_op jit(solution)/shard_map/pack/pallas_call | solution.py:367
  1.2 0.0 copy-start.1
  1.2 22.2 %all_to_all.15 = f32[16,4,8,128]{3,2,1,0:T(8,128)S(1)} all-to-all(f32[16,4,8,128]{3,2,1,0:T(8,128)S(1)} %get-tuple-element.12), channel_id=1, replica_groups=mesh['tm'=16,'sx'=8,'sy'=4] {'tm'}, dimensions={0} | all-to-all | bytes 524288 | tf_op jit(solution)/shard_map/all_to_all | solution.py:394
  23.4 0.0 copy-done.1
  23.4 0.6 transform.1
  24.0 1.9 %collective-permute-start = (f32[33,8,128]{2,1,0:T(8,128)S(1)}, f32[33,8,128]{2,1,0:T(8,128)S(1)}, u32[]{:S(2)}, u32[]{:S(2)}) collective-permute-start(f32[33,8,128]{2,1,0:T(8,128)S(1)} %get-tuple-element.14.high), channel_id=1, source_target_pairs={{0,64},{64,128},{128,192},{192,256},{256,320},{320,384},{384,448},... | collective-permute-start | bytes 405512 | tf_op jit(solution)/shard_map/ppermute | solution.py:402
  26.0 0.0 copy-start
  26.0 5.3 %collective-permute-start.1 = (f32[33,8,128]{2,1,0:T(8,128)S(1)}, f32[33,8,128]{2,1,0:T(8,128)S(1)}, u32[]{:S(2)}, u32[]{:S(2)}) collective-permute-start(f32[33,8,128]{2,1,0:T(8,128)S(1)} %get-tuple-element.15.low), channel_id=1, source_target_pairs={{64,0},{128,64},{192,128},{256,192},{320,256},{384,320},{448,384},... | collective-permute-start | bytes 405512 | tf_op jit(solution)/shard_map/ppermute | solution.py:403
  31.3 0.6 collective-permute-done.below
  31.9 1.4 %collective-permute-done.1.above = f32[33,8,128]{2,1,0:T(8,128)S(1)} collective-permute-done((f32[33,8,128]{2,1,0:T(8,128)S(1)}, f32[33,8,128]{2,1,0:T(8,128)S(1)}, u32[]{:S(2)}, u32[]{:S(2)}) %collective-permute-start.1) | collective-permute-done | bytes 135200 | tf_op jit(solution)/shard_map/ppermute | solution.py:403
  33.2 0.0 copy-start.3
  33.3 4.0 %collective-permute-start.2 = (f32[46,8,128]{2,1,0:T(8,128)S(1)}, f32[46,8,128]{2,1,0:T(8,128)S(1)}, u32[]{:S(2)}, u32[]{:S(2)}) collective-permute-start(f32[46,8,128]{2,1,0:T(8,128)S(1)} %get-tuple-element.16), channel_id=1, source_target_pairs={{0,4},{4,8},{8,12},{12,16},{16,20},{20,24},{24,28},{1,5},{5,9},{9,... | collective-permute-start | bytes 565256 | tf_op jit(solution)/shard_map/ppermute | solution.py:409
  37.3 1.3 %collective-permute-start.3 = (f32[46,8,128]{2,1,0:T(8,128)S(1)}, f32[46,8,128]{2,1,0:T(8,128)S(1)}, u32[]{:S(2)}, u32[]{:S(2)}) collective-permute-start(f32[46,8,128]{2,1,0:T(8,128)S(1)} %get-tuple-element.17), channel_id=1, source_target_pairs={{4,0},{8,4},{12,8},{16,12},{20,16},{24,20},{28,24},{5,1},{9,5},{13... | collective-permute-start | bytes 565256 | tf_op jit(solution)/shard_map/ppermute | solution.py:410
  38.6 1.2 %collective-permute-done.2.left = f32[46,8,128]{2,1,0:T(8,128)S(1)} collective-permute-done((f32[46,8,128]{2,1,0:T(8,128)S(1)}, f32[46,8,128]{2,1,0:T(8,128)S(1)}, u32[]{:S(2)}, u32[]{:S(2)}) %collective-permute-start.2) | collective-permute-done | bytes 188448 | tf_op jit(solution)/shard_map/ppermute | solution.py:409
  39.8 4.5 %collective-permute-done.3.right = f32[46,8,128]{2,1,0:T(8,128)S(1)} collective-permute-done((f32[46,8,128]{2,1,0:T(8,128)S(1)}, f32[46,8,128]{2,1,0:T(8,128)S(1)}, u32[]{:S(2)}, u32[]{:S(2)}) %collective-permute-start.3) | collective-permute-done | bytes 188448 | tf_op jit(solution)/shard_map/ppermute | solution.py:410
  44.2 0.0 copy-done
  44.2 0.0 copy-done.3
  44.2 5.7 %sweeps.1 = f32[640,128]{1,0:T(8,128)S(1)} custom-call(f32[33,8,128]{2,1,0:T(8,128)S(1)} %collective-permute-done.below, f32[33,8,128]{2,1,0:T(8,128)S(1)} %get-tuple-element.15.low, f32[33,8,128]{2,1,0:T(8,128)S(1)} %get-tuple-element.14.high, f32[33,8,128]{2,1,0:T(8,128)S(1)} %collective-permute-done.1.above, ...), custom_call_target="tpu_custom_call" | custom-call | tf_op jit(solution)/shard_map/sweeps/pallas_call | solution.py:367
  50.0 20.5 %all_to_all.16.received = f32[16,5,8,128]{3,2,1,0:T(8,128)S(1)} all-to-all(f32[16,5,8,128]{3,2,1,0:T(8,128)S(1)} %bitcast.6), channel_id=1, replica_groups=mesh['tm'=16,'sx'=8,'sy'=4] {'tm'}, dimensions={0} | all-to-all | bytes 655360 | tf_op jit(solution)/shard_map/all_to_all | solution.py:419
  70.4 0.7 gather.1
  71.1 12.9 %all-to-all-start.2 = ((f32[32,8,128]{2,1,0:T(8,128)}), f32[32,8,128]{2,1,0:T(8,128)S(1)}, u32[]{:S(2)}, u32[]{:S(2)}) async-start(f32[32,8,128]{2,1,0:T(8,128)} %gather.1), calls=%async_computation.2 | async-start | bytes 262144 | tf_op jit(solution)/shard_map/all_to_all | solution.py:423
  84.0 0.0 copy-start.2
  84.0 0.1 unpack.1.field
  84.1 9.1 %all-to-all-done.2 = f32[32,8,128]{2,1,0:T(8,128)S(1)} async-done(((f32[32,8,128]{2,1,0:T(8,128)}), f32[32,8,128]{2,1,0:T(8,128)S(1)}, u32[]{:S(2)}, u32[]{:S(2)}) %all-to-all-start.2) | async-done | bytes 131104 | tf_op jit(solution)/shard_map/all_to_all | solution.py:423
  93.2 0.0 copy-done.2
  93.2 1.7 %coarse.1 = f32[512,128]{1,0:T(8,128)} custom-call(f32[256,128]{1,0:T(8,128)S(1)} %bitcast.8, f32[512,128]{1,0:T(8,128)S(1)} %unpack.1.field, f32[8,128]{1,0:T(8,128)S(1)} %copy-done.3, f32[128,128]{1,0:T(8,128)S(1)} %copy-done.2), custom_call_target="tpu_custom_call" | custom-call | tf_op jit(solution)/shard_map/coarse/pallas_call | solution.py:367
  (1 shorter events, 0.0 us)
Async XLA Ops:
  1.2 22.2 %copy-start.1 = (f32[128,128]{1,0:T(8,128)S(1)}, f32[128,128]{1,0:T(8,128)}, u32[]{:S(2)}) copy-start(f32[128,128]{1,0:T(8,128)} %constant.8.clone.table) | copy-start | bytes 196612
  24.0 7.8 %collective-permute-start = (f32[33,8,128]{2,1,0:T(8,128)S(1)}, f32[33,8,128]{2,1,0:T(8,128)S(1)}, u32[]{:S(2)}, u32[]{:S(2)}) collective-permute-start(f32[33,8,128]{2,1,0:T(8,128)S(1)} %get-tuple-element.14.high), channel_id=1, source_target_pairs={{0,64},{64,128},{128,192},{192,256},{256,320},{320,384},{384,448},... | collective-permute-start | bytes 405512 | tf_op jit(solution)/shard_map/ppermute | solution.py:402
  26.0 18.3 %copy-start = (f32[160,128]{1,0:T(8,128)S(1)}, f32[160,128]{1,0:T(8,128)}, u32[]{:S(2)}) copy-start(f32[160,128]{1,0:T(8,128)} %constant.9.clone.table) | copy-start | bytes 245764
  26.0 7.2 %collective-permute-start.1 = (f32[33,8,128]{2,1,0:T(8,128)S(1)}, f32[33,8,128]{2,1,0:T(8,128)S(1)}, u32[]{:S(2)}, u32[]{:S(2)}) collective-permute-start(f32[33,8,128]{2,1,0:T(8,128)S(1)} %get-tuple-element.15.low), channel_id=1, source_target_pairs={{64,0},{128,64},{192,128},{256,192},{320,256},{384,320},{448,384},... | collective-permute-start | bytes 405512 | tf_op jit(solution)/shard_map/ppermute | solution.py:403
  33.2 11.0 %copy-start.3 = (f32[8,128]{1,0:T(8,128)S(1)}, f32[8,128]{1,0:T(8,128)}, u32[]{:S(2)}) copy-start(f32[8,128]{1,0:T(8,128)} %constant.11.clone.lanes) | copy-start | bytes 12292
  33.3 6.5 %collective-permute-start.2 = (f32[46,8,128]{2,1,0:T(8,128)S(1)}, f32[46,8,128]{2,1,0:T(8,128)S(1)}, u32[]{:S(2)}, u32[]{:S(2)}) collective-permute-start(f32[46,8,128]{2,1,0:T(8,128)S(1)} %get-tuple-element.16), channel_id=1, source_target_pairs={{0,4},{4,8},{8,12},{12,16},{16,20},{20,24},{24,28},{1,5},{5,9},{9,... | collective-permute-start | bytes 565256 | tf_op jit(solution)/shard_map/ppermute | solution.py:409
  37.3 7.0 %collective-permute-start.3 = (f32[46,8,128]{2,1,0:T(8,128)S(1)}, f32[46,8,128]{2,1,0:T(8,128)S(1)}, u32[]{:S(2)}, u32[]{:S(2)}) collective-permute-start(f32[46,8,128]{2,1,0:T(8,128)S(1)} %get-tuple-element.17), channel_id=1, source_target_pairs={{4,0},{8,4},{12,8},{16,12},{20,16},{24,20},{28,24},{5,1},{9,5},{13... | collective-permute-start | bytes 565256 | tf_op jit(solution)/shard_map/ppermute | solution.py:410
  71.1 22.1 %all-to-all-start.2 = ((f32[32,8,128]{2,1,0:T(8,128)}), f32[32,8,128]{2,1,0:T(8,128)S(1)}, u32[]{:S(2)}, u32[]{:S(2)}) async-start(f32[32,8,128]{2,1,0:T(8,128)} %gather.1), calls=%async_computation.2 | async-start | bytes 262144 | tf_op jit(solution)/shard_map/all_to_all | solution.py:423
  84.0 9.2 %copy-start.2 = (f32[128,128]{1,0:T(8,128)S(1)}, f32[128,128]{1,0:T(8,128)}, u32[]{:S(2)}) copy-start(f32[128,128]{1,0:T(8,128)} %constant.10.clone.table) | copy-start | bytes 196612

commit v3 on v2

--- a/solution.py
+++ b/solution.py
@@ -9,8 +9,11 @@
 L = 128
 NZ = 8
 BLOCK = 8
-WIDTH = 4
-SPAN = BLOCK + 2 * WIDTH
+WY = 3
+WX = 4
+SPAN_Y = BLOCK + 2 * WY
+SPAN_X = BLOCK + 2 * WX
+PART = 8 * WY + 1
 TM, SX, SY = 16, 8, 4
 FACES = 2 * (32 * NZ + 8 * NZ)
 VOLUME = 8 * 32 * NZ
@@ -104,11 +107,12 @@
     columns.append(jnp.zeros((64, L), jnp.float32))
     c_turned = jnp.concatenate(columns, axis=0).T
     rate_rows[...] = c_turned
-    sums[0:4, :] = jnp.zeros((4, L), jnp.float32)
+    group = lane_index(1) // 32
+    row = jnp.zeros((1, L), jnp.float32)
     for g in range(4):
         total = jnp.sum(c_turned[32 * g : 32 * g + 32], axis=0, keepdims=True)
-        total = jnp.sum(total, axis=1, keepdims=True)
-        sums[4 + g : 5 + g, :] = jnp.broadcast_to(total, (1, L))
+        row = jnp.where(group == g, jnp.sum(total, axis=1, keepdims=True), row)
+    sums[...] = jnp.broadcast_to(row, (8, L))
 
 
 def own_strip():
@@ -116,52 +120,63 @@
     return jnp.where(tm & 1 == 0, tm >> 1, TM - 1 - (tm >> 1))
 
 
-def transform_kernel(received, rate_rows, table, low, high):
+def transform_kernel(received, rate_rows, table, own, rate, low, high):
     rows = []
     for pair in range(4):
         both = [received[pl.ds(2 * pair + j, 64, stride=8), :] for j in range(2)]
         turned = jnp.concatenate(both, axis=0).T
         rows += list(halves(turned[:64], turned[64:]))
     spectrum = dot(jnp.concatenate(rows, axis=0), table[...], ((1,), (0,)))
-    own = rate_rows[pl.ds(pl.multiple_of(own_strip() * 8, 8), 8), :]
+    mine = rate_rows[pl.ds(pl.multiple_of(own_strip() * 8, 8), 8), :]
     for y in range(8):
-        part = low if y < 4 else high
         for x in range(8):
             r = (y * 8 + x) * 8
-            part[(y % 4) * 8 + x] = spectrum[r : r + 8]
-    low[32] = own
-    high[32] = pltpu.roll(own, 4, 0)
+            own[8 * y + x] = spectrum[r : r + 8]
+            if y < WY:
+                low[8 * y + x] = spectrum[r : r + 8]
+            if y >= 8 - WY:
+                high[8 * (y - 8 + WY) + x] = spectrum[r : r + 8]
+    rate[...] = mine
+    low[PART - 1] = mine
+    high[PART - 1] = pltpu.roll(mine, WY, 0)
 
 
 def x_range(distance):
-    return range(distance, SPAN - distance)
-
-
-def edge_tiles():
-    return [(d, y) for d in range(1, WIDTH + 1) for y in x_range(d)]
-
-
-EDGE = edge_tiles()
-
-
-def strip_rows(below, low, high, above):
-    parts = (below, low, high, above)
-    return lambda y, x: parts[y // 4][(y % 4) * 8 + x]
-
-
-def edge_kernel(below, low, high, above, to_left, to_right):
-    tile = strip_rows(below, low, high, above)
+    return range(distance - 1, SPAN_Y + 1 - distance)
+
+
+EDGE = [(d, y) for d in range(1, WX + 1) for y in x_range(d)]
+
+
+def strip_rows(below, own, above):
+    def tile(y, x):
+        if y < WY:
+            return below[8 * y + x]
+        if y < WY + 8:
+            return own[8 * (y - WY) + x]
+        return above[8 * (y - WY - 8) + x]
+
+    return tile
+
+
+def strip_rates(below, rate, above):
+    rows = [below[PART - 1][0:WY], rate[...], above[PART - 1][0:WY], jnp.zeros((2, L), jnp.float32)]
+    rows = jnp.concatenate(rows, axis=0)
+    return rows[0:8], rows[8:16]
+
+
+def edge_kernel(below, own, rate, above, to_left, to_right):
+    tile = strip_rows(below, own, above)
     for i, (d, y) in enumerate(EDGE):
         to_left[i] = tile(y, d - 1)
         to_right[i] = tile(y, 8 - d)
-    for j, (first, second) in enumerate(((below, low), (high, above))):
-        c = jnp.concatenate([first[32][0:4], second[32][0:4]], axis=0)
+    for j, c in enumerate(strip_rates(below, rate, above)):
         to_left[len(EDGE) + j] = c
         to_right[len(EDGE) + j] = c
 
 
 def solve_kernel(
-    below, low, high, above, left, right, lanes, table, out, source, a, b, x0, x1, rate
+    below, own, rate, above, left, right, lanes, table, out, source, a, b, x0, x1
 ):
     sx, sy, strip = lax.axis_index("sx"), lax.axis_index("sy"), own_strip()
     valid = [
@@ -173,55 +188,56 @@
             (sy < SY - 1) | (strip < TM - 1),
         )
     ]
-    tile = strip_rows(below, low, high, above)
+    tile = strip_rows(below, own, above)
     zero = jnp.zeros((8, L), jnp.float32)
-    for y in range(SPAN):
-        for x in range(WIDTH):
+    for y in range(SPAN_Y):
+        for x in range(WX):
             source[y, x] = zero
-            source[y, SPAN - 1 - x] = zero
+            source[y, SPAN_X - 1 - x] = zero
         for x in range(8):
-            source[y, WIDTH + x] = tile(y, x)
+            source[y, WX + x] = tile(y, x)
     for i, (d, y) in enumerate(EDGE):
-        source[y, WIDTH - d] = left[i]
-        source[y, WIDTH + 7 + d] = right[i]
+        source[y, WX - d] = left[i]
+        source[y, WX + 7 + d] = right[i]
     lane = lane_index(8)
-    for j, (first, second) in enumerate(((below, low), (high, above))):
-        mid = jnp.concatenate([first[32][0:4], second[32][0:4]], axis=0)
-        c = jnp.where(
-            lane < 32,
-            pltpu.roll(left[len(EDGE) + j], 96, 1),
-            jnp.where(lane < 96, pltpu.roll(mid, 32, 1), pltpu.roll(right[len(EDGE) + j], 96, 1)),
+    rows = []
+    for j, mid in enumerate(strip_rates(below, rate, above)):
+        rows.append(
+            jnp.where(
+                lane < 32,
+                pltpu.roll(left[len(EDGE) + j], 96, 1),
+                jnp.where(
+                    lane < 96, pltpu.roll(mid, 32, 1), pltpu.roll(right[len(EDGE) + j], 96, 1)
+                ),
+            )
         )
-        rate[8 * j : 8 * j + 8, :] = c
-    base = lanes[0:1, :] + 6.0
-    sine = lanes[1:2, :]
+    rows.append(jnp.zeros((112, L), jnp.float32))
+    turned = jnp.concatenate(rows, axis=0).T
+    base = jnp.broadcast_to(lanes[0:1, :] + 6.0, (8, L))
+    sine = jnp.broadcast_to(lanes[1:2, :], (8, L))
     sine_square = sine * sine
-
-    def prepare(y, carry):
-        row = rate[pl.ds(y, 1), :]
-        spread = jnp.broadcast_to(row, (L, L)).T
-        row_ok = jnp.where(y < WIDTH, valid[2], jnp.where(y < SPAN - WIDTH, 1.0, valid[3]))
-        for x in range(SPAN):
-            ok = row_ok
-            if x < WIDTH:
-                ok = row_ok * valid[0]
-            elif x >= SPAN - WIDTH:
-                ok = row_ok * valid[1]
-            d = spread[8 * x : 8 * x + 8] + base
-            inverse = ok / (d * d + sine_square)
+    for y in range(SPAN_Y):
+        for x in range(SPAN_X):
+            d = jnp.broadcast_to(turned[8 * x : 8 * x + 8, y : y + 1], (8, L)) + base
+            inverse = 1.0 / (d * d + sine_square)
+            if x < WX:
+                inverse = inverse * valid[0]
+            elif x >= WX + 8:
+                inverse = inverse * valid[1]
+            if y < WY:
+                inverse = inverse * valid[2]
+            elif y >= WY + 8:
+                inverse = inverse * valid[3]
             ax = d * inverse
             bx = sine * inverse
             a[y, x] = ax
             b[y, x] = bx
             s = source[y, x]
             x0[y, x] = ax * s + bx * pltpu.roll(s, 64, 1)
-        return carry
-
-    lax.fori_loop(0, SPAN, prepare, 0)
 
     def sweep(old, new, margin):
         def row(y, carry):
-            for x in range(margin, SPAN - margin):
+            for x in range(margin, SPAN_X - margin):
                 v = old[y, x]
                 u = source[y, x] + (old[y, x + 1] + old[y, x - 1])
                 u = u + (old[y + 1, x] + old[y - 1, x])
@@ -229,45 +245,54 @@
                 new[y, x] = a[y, x] * u + b[y, x] * pltpu.roll(u, 64, 1)
             return carry
 
-        lax.fori_loop(margin, SPAN - margin, row, 0)
+        lax.fori_loop(margin, SPAN_Y - margin, row, 0)
 
     sweep(x0, x1, 1)
     sweep(x1, x0, 2)
     sweep(x0, x1, 3)
-    lo, hi = WIDTH, WIDTH + BLOCK
+    lo, hi = WX, WX + 8
 
     def change(y, x):
         return x1[y, x] - x0[y, x]
 
     acc = zero
-    for y in range(lo - 1, hi + 1):
+    faces = []
+    for y in range(WY, WY + 8):
         line = zero
         for x in range(lo, hi):
             line = line + change(y, x)
-        inner = lo <= y < hi
-        times = (4 if inner else 0) + (1 if lo - 1 <= y < hi - 1 else 0) + (1 if lo + 1 <= y <= hi else 0)
-        acc = acc + float(times) * line
-        if inner:
-            acc = acc + (change(y, lo - 1) - change(y, lo)) + (change(y, hi) - change(y, hi - 1))
-    own = x1[lo:hi, lo:hi].reshape(512, L)
-    result = dot(table[...], own, ((1,), (1,)))
+        end = y in (WY, WY + 7)
+        acc = acc + (5.0 if end else 6.0) * line
+        acc = acc + (change(y, lo - 1) - change(y, lo)) + (change(y, hi) - change(y, hi - 1))
+        if end:
+            faces.append(line)
+    solved = x1[WY : WY + 8, lo:hi].reshape(512, L)
+    result = dot(table[...], solved, ((1,), (1,)))
     for pair in range(4):
         cut = result[:, 128 * pair : 128 * pair + 128]
         for j, value in enumerate(halves(cut[: TM * TILES], cut[TM * TILES :])):
             out[pl.ds(2 * pair + j, TM * TILES, stride=8), :] = value
-    row = jnp.broadcast_to(jnp.sum(acc, axis=0, keepdims=True), (8, L))
+    rows = [jnp.sum(v, axis=0, keepdims=True) for v in (acc, *faces)]
+    rows = jnp.concatenate(rows + [jnp.zeros((5, L), jnp.float32)], axis=0)
     for d in range(TM):
-        out[8 * (TILES * d + 4) : 8 * (TILES * d + 5), :] = row
+        out[8 * (TILES * d + 4) : 8 * (TILES * d + 5), :] = rows
 
 
 def gather_kernel(received, sums, out):
+    part = [received[MEMBER[s], 4] for s in range(TM)]
     rows = []
     for g in range(4):
-        row = received[MEMBER[4 * g], 4][0:1]
+        row = part[4 * g][0:1]
         for s in range(4 * g + 1, 4 * g + 4):
-            row = row + received[MEMBER[s], 4][0:1]
+            row = row + part[s][0:1]
+        for s in range(4 * g, 4 * g + 4):
+            if s > 0:
+                row = row + part[s - 1][2:3]
+            if s < TM - 1:
+                row = row + part[s + 1][1:2]
         rows.append(row)
-    block = jnp.concatenate(rows + [sums[4:8, :]], axis=0)
+    rows += [part[0][1:2], part[TM - 1][2:3], sums[0:1, :], jnp.zeros((1, L), jnp.float32)]
+    block = jnp.concatenate(rows, axis=0)
     for j in range(SX * SY):
         out[j] = block
 
@@ -295,15 +320,27 @@
     return terms[0]
 
 
-def coarse_kernel(gathered, field, lanes, table, out, answer):
+def coarse_kernel(gathered, received, lanes, table, out, answer):
     index = lax.broadcasted_iota(jnp.int32, (8, L), 0)
-    shift = lanes[0:1, :] * float(VOLUME) + float(FACES)
+    shift = jnp.broadcast_to(lanes[0:1, :] * float(VOLUME) + float(FACES), (8, L))
+
+    def rows_of(sy, row):
+        return gathered[pl.ds(sy * 8 + row, 8, stride=32), :]
 
     def right(m):
-        return gathered[pl.ds((m // 4) * 8 + m % 4, 8, stride=32), :]
+        sy, g = m // 4, m % 4
+        rhs = rows_of(sy, g)
+        if g == 0 and sy > 0:
+            rhs = rhs + rows_of(sy - 1, 5)
+        if g == 3 and sy < SY - 1:
+            rhs = rhs + rows_of(sy + 1, 4)
+        return rhs
+
+    sums = [rows_of(sy, 6) for sy in range(SY)]
 
     def block(m, before):
-        diagonal = gathered[pl.ds((m // 4) * 8 + 4 + m % 4, 8, stride=32), :] + shift
+        g = 32 * (m % 4)
+        diagonal = jnp.broadcast_to(sums[m // 4][:, g : g + 1], (8, L)) + shift
         rows = []
         for r in range(8):
             row = jnp.where(index == r, diagonal, 0.0)
@@ -343,21 +380,18 @@
         y = answer[pl.ds((sy * 4 + g) * 8 + sx, 1), :]
         value = jnp.sum(own * y, axis=1, keepdims=True)
         added = jnp.where(group == g, value, added)
-    for t in range(8):
-        out[64 * t : 64 * t + 64, :] = field[64 * t : 64 * t + 64, :] + added[t : t + 1, :]
-
-
-def unpack_kernel(received, out):
     for tp in range(4):
         rows = [received[MEMBER[s], tp] for s in range(TM)]
         turned = jnp.concatenate(rows, axis=0).T
         for t2 in range(2):
+            t = 2 * tp + t2
+            plus = jnp.broadcast_to(added[t : t + 1, :], (8, L))
             for x in range(8):
                 r = t2 * 64 + x * 8
-                out[pl.ds((2 * tp + t2) * 64 + x, 8, stride=8), :] = turned[r : r + 8]
-
-
-def call(kernel, name, out_shape, arrays, scratch=(), rates=None, keep=True, flops=0):
+                out[pl.ds(t * 64 + x, 8, stride=8), :] = turned[r : r + 8] + plus
+
+
+def call(kernel, name, out_shape, arrays, scratch=(), rates=None, keep=True):
     if keep:
         out_shape = jax.tree.map(lambda o: pltpu.VMEM(o.shape, o.dtype), out_shape)
     if rates is None:
@@ -371,7 +405,6 @@
         in_specs=smem(len(scalars)) + vmem(len(arrays)),
         out_specs=tuple(vmem(len(out_shape))) if many else vmem(1)[0],
         scratch_shapes=list(scratch),
-        cost_estimate=pl.CostEstimate(flops=flops, transcendentals=0, bytes_accessed=0),
     )(*scalars, *arrays)
 
 
@@ -392,10 +425,10 @@
         rates=reaction_rates,
     )
     received = lax.all_to_all(packed, "tm", split_axis=0, concat_axis=0, tiled=True)
-    low, high = call(
+    own, rate, low, high = call(
         transform_kernel,
         "transform",
-        (shape(33, 8, L), shape(33, 8, L)),
+        (shape(64, 8, L), shape(8, L), shape(PART, 8, L), shape(PART, 8, L)),
         [received.reshape(512, L), rate_rows, forward],
     )
     up = y_steps()
@@ -403,30 +436,28 @@
     above = lax.ppermute(low, ("tm", "sy"), [(q, p) for p, q in up])
     tiles = len(EDGE) + 2
     to_left, to_right = call(
-        edge_kernel, "edges", (shape(tiles, 8, L),) * 2, [below, low, high, above]
+        edge_kernel, "edges", (shape(tiles, 8, L),) * 2, [below, own, rate, above]
     )
     across = [(i, i + 1) for i in range(SX - 1)]
     left = lax.ppermute(to_right, "sx", across)
     right = lax.ppermute(to_left, "sx", [(q, p) for p, q in across])
-    big = pltpu.VMEM((SPAN, SPAN, 8, L), jnp.float32)
     message = call(
         solve_kernel,
         "sweeps",
         shape(TM * TILES * 8, L),
-        [below, low, high, above, left, right, lanes, inverse],
-        [big] * 5 + [pltpu.VMEM((SPAN, L), jnp.float32)],
+        [below, own, rate, above, left, right, lanes, inverse],
+        [pltpu.VMEM((SPAN_Y, SPAN_X, 8, L), jnp.float32)] * 5,
     )
     returned = lax.all_to_all(
         message.reshape(TM, TILES, 8, L), "tm", split_axis=0, concat_axis=0, tiled=True
     )
     shared = call(gather_kernel, "gather", shape(SX * SY, 8, L), [returned, sums])
     gathered = lax.all_to_all(shared, ("sx", "sy"), split_axis=0, concat_axis=0, tiled=True)
-    field = call(unpack_kernel, "unpack", shape(512, L), [returned], flops=10**8)
     result = call(
         coarse_kernel,
         "coarse",
         shape(512, L),
-        [gathered.reshape(256, L), field, lanes, natural],
+        [gathered.reshape(256, L), returned, lanes, natural],
         [pltpu.VMEM((L, L), jnp.float32)],
         keep=False,
     )

time: 95.3 us -> 91.8 us (0.963)
  blocking collectives: 42.7 us -> 64 us
  starting transfers between devices: 25.4 us -> 12.5 us
  waiting for transfers between devices: 16.7 us -> 7.31 us
  Pallas kernels: 10.1 us -> 7.55 us
    all_to_all x0 -> x1, blocking collectives: none -> 21.4 us  [local(): lax.all_to_all(shared, ('sx', 'sy'), split_axis=0, concat_axis=0, tiled=T...]
    all_to_all x1 -> x0, starting transfers between devices: 12.9 us -> none  [local(): lax.all_to_all(shared, ('sx', 'sy'), split_axis=0, concat_axis=0, tiled=T...]
    all_to_all x1 -> x0, waiting for transfers between devices: 9.08 us -> none  [local(): lax.all_to_all(shared, ('sx', 'sy'), split_axis=0, concat_axis=0, tiled=T...]
    pallas_call x7 -> x6, Pallas kernels: 10.1 us -> 7.55 us  [call(): pl.pallas_call(kernel, name=name, out_shape=out_shape, in_specs=smem(len(...]
  transfers between devices with their start and end apart: 5 -> 4, of which waited for: 5 -> 4; matrix products, arithmetic and copies ran while one was open for 0% -> 0% of each run, Pallas kernels for 0% -> 0%
where the time goes in v3:
time: 91.8 us; the launch traced here: 91.4 us
  blocking collectives  64 us (70%)
  starting transfers between devices  12.5 us (14%)
  Pallas kernels  7.55 us (8%)
  waiting for transfers between devices  7.31 us (8%)
    all_to_all x1, blocking collectives, local(): lax.all_to_all(packed, 'tm', split_axis=0, concat_axis=0, tiled=True)  22.2 us
    all_to_all x1, blocking collectives, local(): lax.all_to_all(shared, ('sx', 'sy'), split_axis=0, concat_axis=0, tiled=T...  21.4 us
    all_to_all x1, blocking collectives, local(): lax.all_to_all(message.reshape(TM, TILES, 8, L), 'tm', split_axis=0, conc...  20.3 us
    pallas_call x6, Pallas kernels, call(): pl.pallas_call(kernel, name=name, out_shape=out_shape, in_specs=smem(len(...  7.55 us
    ppermute x1, starting transfers between devices, local(): above = lax.ppermute(low, ('tm', 'sy'), [(q, p) for p, q in up])  5.15 us
    ppermute x1, waiting for transfers between devices, local(): right = lax.ppermute(to_left, 'sx', [(q, p) for p, q in across])  4.46 us
    ppermute x1, starting transfers between devices, local(): left = lax.ppermute(to_right, 'sx', across)  4.14 us
    ppermute x1, starting transfers between devices, local(): below = lax.ppermute(high, ('tm', 'sy'), up)  1.92 us
  transfers between devices with their start and end apart: 4, of which 4 were waited for; matrix products, arithmetic and copies ran while one was open for 0% of the time, Pallas kernels for 0%

profile of v3, /device:TPU:1, one launch (start us, length us, event | category | flops | bytes accessed | tf_op | source)
XLA Modules:
  0.0 91.4 jit_solution(17991757621304774149)
XLA Ops:
  0.0 1.2 %pack.1 = (f32[16,4,8,128]{3,2,1,0:T(8,128)S(1)}, f32[128,128]{1,0:T(8,128)S(1)}, f32[8,128]{1,0:T(8,128)S(1)}) custom-call(f32[8]{0:T(128)} %rates.1, f32[512,128]{1,0:T(8,128)} %bitcast.9, s32[64,128]{1,0:T(8,128)} %bitcast.10), custom_call_target="tpu_custom_call" | custom-call | tf_op jit(solution)/shard_map/pack/pallas_call | solution.py:401
  1.2 0.0 copy-start.2
  1.2 22.2 %all_to_all.15 = f32[16,4,8,128]{3,2,1,0:T(8,128)S(1)} all-to-all(f32[16,4,8,128]{3,2,1,0:T(8,128)S(1)} %get-tuple-element.14), channel_id=1, replica_groups=mesh['tm'=16,'sx'=8,'sy'=4] {'tm'}, dimensions={0} | all-to-all | bytes 524288 | tf_op jit(solution)/shard_map/all_to_all | solution.py:427
  23.4 0.0 copy-done.2
  23.4 0.6 transform.1
  24.0 1.9 %collective-permute-start = (f32[25,8,128]{2,1,0:T(8,128)S(1)}, f32[25,8,128]{2,1,0:T(8,128)S(1)}, u32[]{:S(2)}, u32[]{:S(2)}) collective-permute-start(f32[25,8,128]{2,1,0:T(8,128)S(1)} %get-tuple-element.16), channel_id=1, source_target_pairs={{0,64},{64,128},{128,192},{192,256},{256,320},{320,384},{384,448},... | collective-permute-start | bytes 307208 | tf_op jit(solution)/shard_map/ppermute | solution.py:435
  26.0 5.1 %collective-permute-start.1 = (f32[25,8,128]{2,1,0:T(8,128)S(1)}, f32[25,8,128]{2,1,0:T(8,128)S(1)}, u32[]{:S(2)}, u32[]{:S(2)}) collective-permute-start(f32[25,8,128]{2,1,0:T(8,128)S(1)} %get-tuple-element.19), channel_id=1, source_target_pairs={{64,0},{128,64},{192,128},{256,192},{320,256},{384,320},{448,384},... | collective-permute-start | bytes 307208 | tf_op jit(solution)/shard_map/ppermute | solution.py:436
  31.1 0.4 collective-permute-done.below
  31.5 1.3 %collective-permute-done.1.above = f32[25,8,128]{2,1,0:T(8,128)S(1)} collective-permute-done((f32[25,8,128]{2,1,0:T(8,128)S(1)}, f32[25,8,128]{2,1,0:T(8,128)S(1)}, u32[]{:S(2)}, u32[]{:S(2)}) %collective-permute-start.1) | collective-permute-done | bytes 102432 | tf_op jit(solution)/shard_map/ppermute | solution.py:436
  32.8 0.0 copy-start
  32.8 0.0 copy-start.3
  32.8 4.1 %collective-permute-start.2 = (f32[46,8,128]{2,1,0:T(8,128)S(1)}, f32[46,8,128]{2,1,0:T(8,128)S(1)}, u32[]{:S(2)}, u32[]{:S(2)}) collective-permute-start(f32[46,8,128]{2,1,0:T(8,128)S(1)} %get-tuple-element.20), channel_id=1, source_target_pairs={{0,4},{4,8},{8,12},{12,16},{16,20},{20,24},{24,28},{1,5},{5,9},{9,... | collective-permute-start | bytes 565256 | tf_op jit(solution)/shard_map/ppermute | solution.py:442
  37.0 1.3 %collective-permute-start.3 = (f32[46,8,128]{2,1,0:T(8,128)S(1)}, f32[46,8,128]{2,1,0:T(8,128)S(1)}, u32[]{:S(2)}, u32[]{:S(2)}) collective-permute-start(f32[46,8,128]{2,1,0:T(8,128)S(1)} %get-tuple-element.21), channel_id=1, source_target_pairs={{4,0},{8,4},{12,8},{16,12},{20,16},{24,20},{28,24},{5,1},{9,5},{13... | collective-permute-start | bytes 565256 | tf_op jit(solution)/shard_map/ppermute | solution.py:443
  38.3 1.2 %collective-permute-done.2.left = f32[46,8,128]{2,1,0:T(8,128)S(1)} collective-permute-done((f32[46,8,128]{2,1,0:T(8,128)S(1)}, f32[46,8,128]{2,1,0:T(8,128)S(1)}, u32[]{:S(2)}, u32[]{:S(2)}) %collective-permute-start.2) | collective-permute-done | bytes 188448 | tf_op jit(solution)/shard_map/ppermute | solution.py:442
  39.5 4.5 %collective-permute-done.3.right = f32[46,8,128]{2,1,0:T(8,128)S(1)} collective-permute-done((f32[46,8,128]{2,1,0:T(8,128)S(1)}, f32[46,8,128]{2,1,0:T(8,128)S(1)}, u32[]{:S(2)}, u32[]{:S(2)}) %collective-permute-start.3) | collective-permute-done | bytes 188448 | tf_op jit(solution)/shard_map/ppermute | solution.py:443
  43.9 0.0 copy-done
  43.9 0.0 copy-done.3
  43.9 3.9 %sweeps.1 = f32[640,128]{1,0:T(8,128)S(1)} custom-call(f32[25,8,128]{2,1,0:T(8,128)S(1)} %collective-permute-done.below, f32[64,8,128]{2,1,0:T(8,128)S(1)} %get-tuple-element.17.own, f32[8,128]{1,0:T(8,128)S(1)} %get-tuple-element.18.rate, f32[25,8,128]{2,1,0:T(8,128)S(1)} %collective-permute-done.1.above, f32[46,8,128]{2,1,0:T(8,128)S(1)} %collective-permute-done.2.left, ...), custom_call_target="tpu_custom_call" | custom-call | tf_op jit(solution)/shard_map/sweeps/pallas_call | solution.py:401
  47.8 20.3 %all_to_all.16.received = f32[16,5,8,128]{3,2,1,0:T(8,128)S(1)} all-to-all(f32[16,5,8,128]{3,2,1,0:T(8,128)S(1)} %bitcast.6), channel_id=1, replica_groups=mesh['tm'=16,'sx'=8,'sy'=4] {'tm'}, dimensions={0} | all-to-all | bytes 655360 | tf_op jit(solution)/shard_map/all_to_all | solution.py:451
  68.2 0.0 copy-start.1
  68.2 21.4 %all_to_all.17 = f32[32,8,128]{2,1,0:T(8,128)S(1)} all-to-all(f32[32,8,128]{2,1,0:T(8,128)S(1)} %gather.1), channel_id=1, replica_groups=mesh['tm'=16,'sx'=8,'sy'=4] {'sx','sy'}, dimensions={0} | all-to-all | bytes 262144 | tf_op jit(solution)/shard_map/all_to_all | solution.py:455
  89.6 0.0 copy-done.1
  89.6 1.8 %coarse.1 = f32[512,128]{1,0:T(8,128)} custom-call(f32[256,128]{1,0:T(8,128)S(1)} %bitcast.8, f32[16,5,8,128]{3,2,1,0:T(8,128)S(1)} %all_to_all.16.received, f32[8,128]{1,0:T(8,128)S(1)} %copy-done.3, f32[128,128]{1,0:T(8,128)S(1)} %copy-done.1), custom_call_target="tpu_custom_call" | custom-call | tf_op jit(solution)/shard_map/coarse/pallas_call | solution.py:401
  (2 shorter events, 0.1 us)
Async XLA Ops:
  1.2 22.2 %copy-start.2 = (f32[128,128]{1,0:T(8,128)S(1)}, f32[128,128]{1,0:T(8,128)}, u32[]{:S(2)}) copy-start(f32[128,128]{1,0:T(8,128)} %constant.8.clone.table) | copy-start | bytes 196612
  24.0 7.5 %collective-permute-start = (f32[25,8,128]{2,1,0:T(8,128)S(1)}, f32[25,8,128]{2,1,0:T(8,128)S(1)}, u32[]{:S(2)}, u32[]{:S(2)}) collective-permute-start(f32[25,8,128]{2,1,0:T(8,128)S(1)} %get-tuple-element.16), channel_id=1, source_target_pairs={{0,64},{64,128},{128,192},{192,256},{256,320},{320,384},{384,448},... | collective-permute-start | bytes 307208 | tf_op jit(solution)/shard_map/ppermute | solution.py:435
  26.0 6.8 %collective-permute-start.1 = (f32[25,8,128]{2,1,0:T(8,128)S(1)}, f32[25,8,128]{2,1,0:T(8,128)S(1)}, u32[]{:S(2)}, u32[]{:S(2)}) collective-permute-start(f32[25,8,128]{2,1,0:T(8,128)S(1)} %get-tuple-element.19), channel_id=1, source_target_pairs={{64,0},{128,64},{192,128},{256,192},{320,256},{384,320},{448,384},... | collective-permute-start | bytes 307208 | tf_op jit(solution)/shard_map/ppermute | solution.py:436
  32.8 11.1 %copy-start = (f32[160,128]{1,0:T(8,128)S(1)}, f32[160,128]{1,0:T(8,128)}, u32[]{:S(2)}) copy-start(f32[160,128]{1,0:T(8,128)} %constant.9.clone.table) | copy-start | bytes 245764
  32.8 11.1 %copy-start.3 = (f32[8,128]{1,0:T(8,128)S(1)}, f32[8,128]{1,0:T(8,128)}, u32[]{:S(2)}) copy-start(f32[8,128]{1,0:T(8,128)} %constant.11.clone.lanes) | copy-start | bytes 12292
  32.8 6.6 %collective-permute-start.2 = (f32[46,8,128]{2,1,0:T(8,128)S(1)}, f32[46,8,128]{2,1,0:T(8,128)S(1)}, u32[]{:S(2)}, u32[]{:S(2)}) collective-permute-start(f32[46,8,128]{2,1,0:T(8,128)S(1)} %get-tuple-element.20), channel_id=1, source_target_pairs={{0,4},{4,8},{8,12},{12,16},{16,20},{20,24},{24,28},{1,5},{5,9},{9,... | collective-permute-start | bytes 565256 | tf_op jit(solution)/shard_map/ppermute | solution.py:442
  37.0 7.0 %collective-permute-start.3 = (f32[46,8,128]{2,1,0:T(8,128)S(1)}, f32[46,8,128]{2,1,0:T(8,128)S(1)}, u32[]{:S(2)}, u32[]{:S(2)}) collective-permute-start(f32[46,8,128]{2,1,0:T(8,128)S(1)} %get-tuple-element.21), channel_id=1, source_target_pairs={{4,0},{8,4},{12,8},{16,12},{20,16},{24,20},{28,24},{5,1},{9,5},{13... | collective-permute-start | bytes 565256 | tf_op jit(solution)/shard_map/ppermute | solution.py:443
  68.2 21.4 %copy-start.1 = (f32[128,128]{1,0:T(8,128)S(1)}, f32[128,128]{1,0:T(8,128)}, u32[]{:S(2)}) copy-start(f32[128,128]{1,0:T(8,128)} %constant.10.clone.table) | copy-start | bytes 196612

commit v4 on v3

--- a/solution.py
+++ b/solution.py
@@ -89,14 +89,16 @@
 
 
 def pack_kernel(rates, field, regime, out, rate_rows, sums):
+    margin = jnp.zeros((8, L), jnp.float32)
     for tp in range(4):
         rows = [
             field[pl.ds((2 * tp + t2) * 64 + x, 8, stride=8), :] for t2 in range(2) for x in range(8)
         ]
         turned = jnp.concatenate(rows, axis=0).T
+        shifted = jnp.concatenate([margin[:WY], turned, margin], axis=0)
         for d in range(TM):
             s = strip_of(d)
-            out[d, tp] = turned[8 * s : 8 * s + 8]
+            out[d, SPAN_Y * tp : SPAN_Y * (tp + 1)] = shifted[8 * s : 8 * s + SPAN_Y]
     columns = []
     for x in range(8):
         kind = regime[pl.ds(x, 8, stride=8), :]
@@ -106,7 +108,7 @@
         columns.append(c)
     columns.append(jnp.zeros((64, L), jnp.float32))
     c_turned = jnp.concatenate(columns, axis=0).T
-    rate_rows[...] = c_turned
+    rate_rows[...] = jnp.concatenate([margin, c_turned, margin], axis=0)
     group = lane_index(1) // 32
     row = jnp.zeros((1, L), jnp.float32)
     for g in range(4):
@@ -120,25 +122,23 @@
     return jnp.where(tm & 1 == 0, tm >> 1, TM - 1 - (tm >> 1))
 
 
-def transform_kernel(received, rate_rows, table, own, rate, low, high):
+def transform_kernel(received, rate_rows, table, window, rate, swap):
     rows = []
-    for pair in range(4):
-        both = [received[pl.ds(2 * pair + j, 64, stride=8), :] for j in range(2)]
+    for pair in range(SPAN_Y // 2):
+        both = [received[pl.ds(2 * pair + j, 64, stride=SPAN_Y), :] for j in range(2)]
         turned = jnp.concatenate(both, axis=0).T
         rows += list(halves(turned[:64], turned[64:]))
     spectrum = dot(jnp.concatenate(rows, axis=0), table[...], ((1,), (0,)))
-    mine = rate_rows[pl.ds(pl.multiple_of(own_strip() * 8, 8), 8), :]
-    for y in range(8):
-        for x in range(8):
-            r = (y * 8 + x) * 8
-            own[8 * y + x] = spectrum[r : r + 8]
-            if y < WY:
-                low[8 * y + x] = spectrum[r : r + 8]
-            if y >= 8 - WY:
-                high[8 * (y - 8 + WY) + x] = spectrum[r : r + 8]
+    for i in range(8 * SPAN_Y):
+        window[i] = spectrum[8 * i : 8 * i + 8]
+    strip = own_strip()
+    near = rate_rows[pl.ds(pl.multiple_of(strip * 8, 8), 24), :]
+    mine = jnp.concatenate([near[8 - WY : 16 + WY], jnp.zeros((2, L), jnp.float32)], axis=0)
     rate[...] = mine
-    low[PART - 1] = mine
-    high[PART - 1] = pltpu.roll(mine, WY, 0)
+    first = strip == 0
+    for i in range(8 * WY):
+        swap[i] = jnp.where(first, window[8 * WY + i], window[64 + i])
+    swap[PART - 1] = jnp.where(first, pltpu.roll(mine[0:8], 8 - WY, 0), mine[8:16])
 
 
 def x_range(distance):
@@ -148,35 +148,37 @@
 EDGE = [(d, y) for d in range(1, WX + 1) for y in x_range(d)]
 
 
-def strip_rows(below, own, above):
+def completed(window, rate, swapped):
+    strip = own_strip()
+    first = jnp.where(strip == 0, 1.0, 0.0)
+    last = jnp.where(strip == TM - 1, 1.0, 0.0)
+
     def tile(y, x):
         if y < WY:
-            return below[8 * y + x]
+            return window[8 * y + x] + first * swapped[8 * y + x]
         if y < WY + 8:
-            return own[8 * (y - WY) + x]
-        return above[8 * (y - WY - 8) + x]
-
-    return tile
-
-
-def strip_rates(below, rate, above):
-    rows = [below[PART - 1][0:WY], rate[...], above[PART - 1][0:WY], jnp.zeros((2, L), jnp.float32)]
-    rows = jnp.concatenate(rows, axis=0)
-    return rows[0:8], rows[8:16]
-
-
-def edge_kernel(below, own, rate, above, to_left, to_right):
-    tile = strip_rows(below, own, above)
+            return window[8 * y + x]
+        return window[8 * y + x] + last * swapped[8 * (y - WY - 8) + x]
+
+    row = lax.broadcasted_iota(jnp.int32, (8, L), 0)
+    other = jnp.where(row < WY, swapped[PART - 1], 0.0)
+    low = rate[0:8, :] + first * other
+    high = rate[8:16, :] + last * pltpu.roll(other, WY, 0)
+    return tile, (low, high)
+
+
+def edge_kernel(window, rate, swapped, to_left, to_right):
+    tile, rates = completed(window, rate, swapped)
     for i, (d, y) in enumerate(EDGE):
         to_left[i] = tile(y, d - 1)
         to_right[i] = tile(y, 8 - d)
-    for j, c in enumerate(strip_rates(below, rate, above)):
+    for j, c in enumerate(rates):
         to_left[len(EDGE) + j] = c
         to_right[len(EDGE) + j] = c
 
 
 def solve_kernel(
-    below, own, rate, above, left, right, lanes, table, out, source, a, b, x0, x1
+    window, rate, swapped, left, right, sums, lanes, table, out, source, a, b, x0, x1
 ):
     sx, sy, strip = lax.axis_index("sx"), lax.axis_index("sy"), own_strip()
     valid = [
@@ -188,7 +190,7 @@
             (sy < SY - 1) | (strip < TM - 1),
         )
     ]
-    tile = strip_rows(below, own, above)
+    tile, rates = completed(window, rate, swapped)
     zero = jnp.zeros((8, L), jnp.float32)
     for y in range(SPAN_Y):
         for x in range(WX):
@@ -201,7 +203,7 @@
         source[y, WX + 7 + d] = right[i]
     lane = lane_index(8)
     rows = []
-    for j, mid in enumerate(strip_rates(below, rate, above)):
+    for j, mid in enumerate(rates):
         rows.append(
             jnp.where(
                 lane < 32,
@@ -216,24 +218,26 @@
     base = jnp.broadcast_to(lanes[0:1, :] + 6.0, (8, L))
     sine = jnp.broadcast_to(lanes[1:2, :], (8, L))
     sine_square = sine * sine
-    for y in range(SPAN_Y):
+
+    def prepare(y, turned):
+        row_ok = jnp.where(y < WY, valid[2], jnp.where(y < WY + 8, 1.0, valid[3]))
         for x in range(SPAN_X):
-            d = jnp.broadcast_to(turned[8 * x : 8 * x + 8, y : y + 1], (8, L)) + base
-            inverse = 1.0 / (d * d + sine_square)
+            ok = row_ok
             if x < WX:
-                inverse = inverse * valid[0]
+                ok = row_ok * valid[0]
             elif x >= WX + 8:
-                inverse = inverse * valid[1]
-            if y < WY:
-                inverse = inverse * valid[2]
-            elif y >= WY + 8:
-                inverse = inverse * valid[3]
+                ok = row_ok * valid[1]
+            d = jnp.broadcast_to(turned[8 * x : 8 * x + 8, 0:1], (8, L)) + base
+            inverse = ok / (d * d + sine_square)
             ax = d * inverse
             bx = sine * inverse
             a[y, x] = ax
             b[y, x] = bx
             s = source[y, x]
             x0[y, x] = ax * s + bx * pltpu.roll(s, 64, 1)
+        return pltpu.roll(turned, L - 1, 1)
+
+    lax.fori_loop(0, SPAN_Y, prepare, turned)
 
     def sweep(old, new, margin):
         def row(y, carry):
@@ -272,27 +276,24 @@
         cut = result[:, 128 * pair : 128 * pair + 128]
         for j, value in enumerate(halves(cut[: TM * TILES], cut[TM * TILES :])):
             out[pl.ds(2 * pair + j, TM * TILES, stride=8), :] = value
-    rows = [jnp.sum(v, axis=0, keepdims=True) for v in (acc, *faces)]
-    rows = jnp.concatenate(rows + [jnp.zeros((5, L), jnp.float32)], axis=0)
+    homes = (
+        strip >> 2,
+        jnp.where(strip == 0, 4, (strip - 1) >> 2),
+        jnp.where(strip == TM - 1, 5, (strip + 1) >> 2),
+    )
+    index = lax.broadcasted_iota(jnp.int32, (8, L), 0)
+    share = jnp.where((index == 6) & (strip == 0), sums[...], 0.0)
+    for home, v in zip(homes, (acc, *faces)):
+        v = jnp.broadcast_to(jnp.sum(v, axis=0, keepdims=True), (8, L))
+        share = share + jnp.where(index == home, v, 0.0)
     for d in range(TM):
-        out[8 * (TILES * d + 4) : 8 * (TILES * d + 5), :] = rows
-
-
-def gather_kernel(received, sums, out):
-    part = [received[MEMBER[s], 4] for s in range(TM)]
-    rows = []
-    for g in range(4):
-        row = part[4 * g][0:1]
-        for s in range(4 * g + 1, 4 * g + 4):
-            row = row + part[s][0:1]
-        for s in range(4 * g, 4 * g + 4):
-            if s > 0:
-                row = row + part[s - 1][2:3]
-            if s < TM - 1:
-                row = row + part[s + 1][1:2]
-        rows.append(row)
-    rows += [part[0][1:2], part[TM - 1][2:3], sums[0:1, :], jnp.zeros((1, L), jnp.float32)]
-    block = jnp.concatenate(rows, axis=0)
+        out[8 * (TILES * d + 4) : 8 * (TILES * d + 5), :] = share
+
+
+def gather_kernel(received, out):
+    block = received[0, 4]
+    for d in range(1, TM):
+        block = block + received[d, 4]
     for j in range(SX * SY):
         out[j] = block
 
@@ -320,64 +321,68 @@
     return terms[0]
 
 
-def coarse_kernel(gathered, received, lanes, table, out, answer):
+def coarse_kernel(gathered, received, lanes, table, out, answer, diagonal, rhs, inverses):
     index = lax.broadcasted_iota(jnp.int32, (8, L), 0)
     shift = jnp.broadcast_to(lanes[0:1, :] * float(VOLUME) + float(FACES), (8, L))
 
     def rows_of(sy, row):
         return gathered[pl.ds(sy * 8 + row, 8, stride=32), :]
 
-    def right(m):
-        sy, g = m // 4, m % 4
-        rhs = rows_of(sy, g)
-        if g == 0 and sy > 0:
-            rhs = rhs + rows_of(sy - 1, 5)
-        if g == 3 and sy < SY - 1:
-            rhs = rhs + rows_of(sy + 1, 4)
-        return rhs
-
-    sums = [rows_of(sy, 6) for sy in range(SY)]
-
-    def block(m, before):
-        g = 32 * (m % 4)
-        diagonal = jnp.broadcast_to(sums[m // 4][:, g : g + 1], (8, L)) + shift
+    for sy in range(SY):
+        sums = rows_of(sy, 6)
+        for g in range(4):
+            f = rows_of(sy, g)
+            if g == 0 and sy > 0:
+                f = f + rows_of(sy - 1, 5)
+            if g == 3 and sy < SY - 1:
+                f = f + rows_of(sy + 1, 4)
+            rhs[4 * sy + g] = f
+            diagonal[4 * sy + g] = jnp.broadcast_to(sums[:, 32 * g : 32 * g + 1], (8, L)) + shift
+
+    def eliminate(m, before):
+        d = diagonal[m]
+        f = rhs[m]
         rows = []
         for r in range(8):
-            row = jnp.where(index == r, diagonal, 0.0)
+            row = jnp.where(index == r, d, 0.0)
             row = jnp.where((index == r - 1) | (index == r + 1), -COUPLE_X, row)
-            for other in before:
+            for other, _ in before:
                 row = row - (COUPLE_Y * COUPLE_Y) * other[r]
             rows.append(row)
-        return rows
-
-    inv, part = {}, {}
-
-    def eliminate(m, sources):
-        matrix = inverse_of(block(m, [inv[q] for q in sources]))
-        rhs = right(m)
-        for q in sources:
-            rhs = rhs + COUPLE_Y * part[q]
-        inv[m] = matrix
-        part[m] = apply(matrix, rhs)
-
-    for i in range(8):
-        if i < 7:
-            eliminate(i, [i - 1] if i else [])
-        eliminate(15 - i, [16 - i] if i else [])
-    eliminate(7, [6, 8])
-    solved = {7: part[7]}
-    for i in range(1, 9):
-        for m, q in ((7 - i, 8 - i), (7 + i, 6 + i)):
-            if 0 <= m < 16:
-                solved[m] = part[m] + COUPLE_Y * apply(inv[m], solved[q])
-    for m in range(16):
-        answer[8 * m : 8 * m + 8, :] = solved[m]
+        for _, part in before:
+            f = f + COUPLE_Y * part
+        matrix = inverse_of(rows)
+        part = apply(matrix, f)
+        for r in range(8):
+            inverses[m, r] = matrix[r]
+        rhs[m] = part
+        return matrix, part
+
+    def both_ends(i, carry):
+        return eliminate(i, [carry[0]]), eliminate(15 - i, [carry[1]])
+
+    nothing = ([jnp.zeros((8, L), jnp.float32)] * 8, jnp.zeros((8, L), jnp.float32))
+    top, bottom = lax.fori_loop(0, 7, both_ends, (nothing, nothing))
+    bottom = eliminate(8, [bottom])
+    _, middle = eliminate(7, [top, bottom])
+    answer[7] = middle
+
+    def back(m, solved):
+        result = rhs[m] + COUPLE_Y * apply([inverses[m, r] for r in range(8)], solved)
+        answer[m] = result
+        return result
+
+    def outward(i, carry):
+        return back(7 - i, carry[0]), back(8 + i, carry[1])
+
+    below = back(8, middle)
+    lax.fori_loop(1, 8, outward, (middle, below))
     sx, sy = lax.axis_index("sx"), lax.axis_index("sy")
     own = table[pl.ds(pl.multiple_of(lax.axis_index("tm") * 8, 8), 8), :]
     group = lane_index(8) // 32
     added = jnp.zeros((8, L), jnp.float32)
     for g in range(4):
-        y = answer[pl.ds((sy * 4 + g) * 8 + sx, 1), :]
+        y = answer[sy * 4 + g, pl.ds(sx, 1), :]
         value = jnp.sum(own * y, axis=1, keepdims=True)
         added = jnp.where(group == g, value, added)
     for tp in range(4):
@@ -408,11 +413,9 @@
     )(*scalars, *arrays)
 
 
-def y_steps():
-    def rank(g):
-        return MEMBER[g % TM] * SY + g // TM
-
-    return [(rank(g), rank(g + 1)) for g in range(SY * TM - 1)]
+def block_swaps():
+    pairs = [(MEMBER[TM - 1] * SY + sy, MEMBER[0] * SY + sy + 1) for sy in range(SY - 1)]
+    return pairs + [(q, p) for p, q in pairs]
 
 
 def local(driving_input, regime, reaction_rates):
@@ -420,23 +423,21 @@
     packed, rate_rows, sums = call(
         pack_kernel,
         "pack",
-        (shape(TM, 4, 8, L), shape(L, L), shape(8, L)),
+        (shape(TM, 4 * SPAN_Y, L), shape(L + 16, L), shape(8, L)),
         [driving_input.reshape(512, L), regime.reshape(64, L)],
         rates=reaction_rates,
     )
     received = lax.all_to_all(packed, "tm", split_axis=0, concat_axis=0, tiled=True)
-    own, rate, low, high = call(
+    window, rate, swap = call(
         transform_kernel,
         "transform",
-        (shape(64, 8, L), shape(8, L), shape(PART, 8, L), shape(PART, 8, L)),
-        [received.reshape(512, L), rate_rows, forward],
-    )
-    up = y_steps()
-    below = lax.ppermute(high, ("tm", "sy"), up)
-    above = lax.ppermute(low, ("tm", "sy"), [(q, p) for p, q in up])
+        (shape(8 * SPAN_Y, 8, L), shape(16, L), shape(PART, 8, L)),
+        [received.reshape(TM * 4 * SPAN_Y, L), rate_rows, forward],
+    )
+    swapped = lax.ppermute(swap, ("tm", "sy"), block_swaps())
     tiles = len(EDGE) + 2
     to_left, to_right = call(
-        edge_kernel, "edges", (shape(tiles, 8, L),) * 2, [below, own, rate, above]
+        edge_kernel, "edges", (shape(tiles, 8, L),) * 2, [window, rate, swapped]
     )
     across = [(i, i + 1) for i in range(SX - 1)]
     left = lax.ppermute(to_right, "sx", across)
@@ -445,20 +446,20 @@
         solve_kernel,
         "sweeps",
         shape(TM * TILES * 8, L),
-        [below, own, rate, above, left, right, lanes, inverse],
+        [window, rate, swapped, left, right, sums, lanes, inverse],
         [pltpu.VMEM((SPAN_Y, SPAN_X, 8, L), jnp.float32)] * 5,
     )
     returned = lax.all_to_all(
         message.reshape(TM, TILES, 8, L), "tm", split_axis=0, concat_axis=0, tiled=True
     )
-    shared = call(gather_kernel, "gather", shape(SX * SY, 8, L), [returned, sums])
+    shared = call(gather_kernel, "gather", shape(SX * SY, 8, L), [returned])
     gathered = lax.all_to_all(shared, ("sx", "sy"), split_axis=0, concat_axis=0, tiled=True)
     result = call(
         coarse_kernel,
         "coarse",
         shape(512, L),
         [gathered.reshape(256, L), returned, lanes, natural],
-        [pltpu.VMEM((L, L), jnp.float32)],
+        [pltpu.VMEM((16, 8, L), jnp.float32)] * 3 + [pltpu.VMEM((16, 8, 8, L), jnp.float32)],
         keep=False,
     )
     return result.reshape(driving_input.shape)

time: 91.8 us -> 92.9 us (1.012)
  starting transfers between devices: 12.5 us -> 9.29 us
  waiting for transfers between devices: 7.31 us -> 9.14 us
  Pallas kernels: 7.55 us -> 9.06 us
    all_to_all x1, blocking collectives: 22.2 us -> 26.2 us  [local(): lax.all_to_all(packed, 'tm', split_axis=0, concat_axis=0, tiled=True)]
    ppermute x2 -> x1, starting transfers between devices: 7.07 us -> 3.99 us  [local(): swapped = lax.ppermute(swap, ('tm', 'sy'), block_swaps())]
    all_to_all x1, blocking collectives: 20.3 us -> 17.4 us  [local(): lax.all_to_all(message.reshape(TM, TILES, 8, L), 'tm', split_axis=0, conc...]
    ppermute x2 -> x1, waiting for transfers between devices: 1.66 us -> 3.48 us  [local(): swapped = lax.ppermute(swap, ('tm', 'sy'), block_swaps())]
    pallas_call x6, Pallas kernels: 7.55 us -> 9.06 us  [call(): pl.pallas_call(kernel, name=name, out_shape=out_shape, in_specs=smem(len(...]
  transfers between devices with their start and end apart: 4 -> 3, of which waited for: 4 -> 3; matrix products, arithmetic and copies ran while one was open for 0% -> 0% of each run, Pallas kernels for 0% -> 0%
where the time goes in v4:
time: 92.9 us; the launch traced here: 92.5 us
  blocking collectives  64.9 us (70%)
  starting transfers between devices  9.29 us (10%)
  waiting for transfers between devices  9.14 us (10%)
  Pallas kernels  9.06 us (10%)
    all_to_all x1, blocking collectives, local(): lax.all_to_all(packed, 'tm', split_axis=0, concat_axis=0, tiled=True)  26.2 us
    all_to_all x1, blocking collectives, local(): lax.all_to_all(shared, ('sx', 'sy'), split_axis=0, concat_axis=0, tiled=T...  21.2 us
    all_to_all x1, blocking collectives, local(): lax.all_to_all(message.reshape(TM, TILES, 8, L), 'tm', split_axis=0, conc...  17.4 us
    pallas_call x6, Pallas kernels, call(): pl.pallas_call(kernel, name=name, out_shape=out_shape, in_specs=smem(len(...  9.06 us
    ppermute x1, waiting for transfers between devices, local(): right = lax.ppermute(to_left, 'sx', [(q, p) for p, q in across])  4.46 us
    ppermute x1, starting transfers between devices, local(): left = lax.ppermute(to_right, 'sx', across)  4.01 us
    ppermute x1, starting transfers between devices, local(): swapped = lax.ppermute(swap, ('tm', 'sy'), block_swaps())  3.99 us
    ppermute x1, waiting for transfers between devices, local(): swapped = lax.ppermute(swap, ('tm', 'sy'), block_swaps())  3.48 us
  transfers between devices with their start and end apart: 3, of which 3 were waited for; matrix products, arithmetic and copies ran while one was open for 0% of the time, Pallas kernels for 0%

profile of v4, /device:TPU:1, one launch (start us, length us, event | category | flops | bytes accessed | tf_op | source)
XLA Modules:
  0.0 92.5 jit_solution(10775099791851891606)
XLA Ops:
  0.0 1.2 %pack.1 = (f32[16,56,128]{2,1,0:T(8,128)S(1)}, f32[144,128]{1,0:T(8,128)S(1)}, f32[8,128]{1,0:T(8,128)S(1)}) custom-call(f32[8]{0:T(128)} %rates.1, f32[512,128]{1,0:T(8,128)} %bitcast.9, s32[64,128]{1,0:T(8,128)} %bitcast.10), custom_call_target="tpu_custom_call" | custom-call | tf_op jit(solution)/shard_map/pack/pallas_call | solution.py:406
  1.2 0.0 copy-start.2
  1.2 26.2 %all_to_all.15 = f32[16,56,128]{2,1,0:T(8,128)S(1)} all-to-all(f32[16,56,128]{2,1,0:T(8,128)S(1)} %get-tuple-element.13), channel_id=1, replica_groups=mesh['tm'=16,'sx'=8,'sy'=4] {'tm'}, dimensions={0} | all-to-all | bytes 917504 | tf_op jit(solution)/shard_map/all_to_all | solution.py:430
  27.4 0.0 copy-done.2
  27.4 0.8 transform.1
  28.2 4.0 %collective-permute-start = (f32[25,8,128]{2,1,0:T(8,128)S(1)}, f32[25,8,128]{2,1,0:T(8,128)S(1)}, u32[]{:S(2)}, u32[]{:S(2)}) collective-permute-start(f32[25,8,128]{2,1,0:T(8,128)S(1)} %get-tuple-element.17), channel_id=1, source_target_pairs={{32,1},{33,2},{34,3},{1,32},{2,33},{3,34},{36,5},{37,6},{38,7},{5,... | collective-permute-start | bytes 307208 | tf_op jit(solution)/shard_map/ppermute | solution.py:437
  32.2 3.5 %collective-permute-done.swapped = f32[25,8,128]{2,1,0:T(8,128)S(1)} collective-permute-done((f32[25,8,128]{2,1,0:T(8,128)S(1)}, f32[25,8,128]{2,1,0:T(8,128)S(1)}, u32[]{:S(2)}, u32[]{:S(2)}) %collective-permute-start) | collective-permute-done | bytes 102432 | tf_op jit(solution)/shard_map/ppermute | solution.py:437
  35.7 0.0 copy-start
  35.7 0.0 copy-start.3
  35.7 4.0 %collective-permute-start.1 = (f32[46,8,128]{2,1,0:T(8,128)S(1)}, f32[46,8,128]{2,1,0:T(8,128)S(1)}, u32[]{:S(2)}, u32[]{:S(2)}) collective-permute-start(f32[46,8,128]{2,1,0:T(8,128)S(1)} %get-tuple-element.18), channel_id=1, source_target_pairs={{0,4},{4,8},{8,12},{12,16},{16,20},{20,24},{24,28},{1,5},{5,9},{9,... | collective-permute-start | bytes 565256 | tf_op jit(solution)/shard_map/ppermute | solution.py:443
  39.7 1.3 %collective-permute-start.2 = (f32[46,8,128]{2,1,0:T(8,128)S(1)}, f32[46,8,128]{2,1,0:T(8,128)S(1)}, u32[]{:S(2)}, u32[]{:S(2)}) collective-permute-start(f32[46,8,128]{2,1,0:T(8,128)S(1)} %get-tuple-element.19), channel_id=1, source_target_pairs={{4,0},{8,4},{12,8},{16,12},{20,16},{24,20},{28,24},{5,1},{9,5},{13... | collective-permute-start | bytes 565256 | tf_op jit(solution)/shard_map/ppermute | solution.py:444
  41.0 1.2 %collective-permute-done.1.left = f32[46,8,128]{2,1,0:T(8,128)S(1)} collective-permute-done((f32[46,8,128]{2,1,0:T(8,128)S(1)}, f32[46,8,128]{2,1,0:T(8,128)S(1)}, u32[]{:S(2)}, u32[]{:S(2)}) %collective-permute-start.1) | collective-permute-done | bytes 188448 | tf_op jit(solution)/shard_map/ppermute | solution.py:443
  42.2 4.5 %collective-permute-done.2.right = f32[46,8,128]{2,1,0:T(8,128)S(1)} collective-permute-done((f32[46,8,128]{2,1,0:T(8,128)S(1)}, f32[46,8,128]{2,1,0:T(8,128)S(1)}, u32[]{:S(2)}, u32[]{:S(2)}) %collective-permute-start.2) | collective-permute-done | bytes 188448 | tf_op jit(solution)/shard_map/ppermute | solution.py:444
  46.7 0.0 copy-done
  46.7 0.0 copy-done.3
  46.7 5.0 %sweeps.1 = f32[640,128]{1,0:T(8,128)S(1)} custom-call(f32[112,8,128]{2,1,0:T(8,128)S(1)} %get-tuple-element.15.window, f32[16,128]{1,0:T(8,128)S(1)} %get-tuple-element.16.rate, f32[25,8,128]{2,1,0:T(8,128)S(1)} %collective-permute-done.swapped, f32[46,8,128]{2,1,0:T(8,128)S(1)} %collective-permute-done.1.left, ...), custom_call_target="tpu_custom_call" | custom-call | tf_op jit(solution)/shard_map/sweeps/pallas_call | solution.py:406
  51.8 17.4 %all_to_all.16.received = f32[16,5,8,128]{3,2,1,0:T(8,128)S(1)} all-to-all(f32[16,5,8,128]{3,2,1,0:T(8,128)S(1)} %bitcast.7), channel_id=1, replica_groups=mesh['tm'=16,'sx'=8,'sy'=4] {'tm'}, dimensions={0} | all-to-all | bytes 655360 | tf_op jit(solution)/shard_map/all_to_all | solution.py:452
  69.2 0.0 copy-start.1
  69.2 21.2 %all_to_all.17 = f32[32,8,128]{2,1,0:T(8,128)S(1)} all-to-all(f32[32,8,128]{2,1,0:T(8,128)S(1)} %gather.1), channel_id=1, replica_groups=mesh['tm'=16,'sx'=8,'sy'=4] {'sx','sy'}, dimensions={0} | all-to-all | bytes 262144 | tf_op jit(solution)/shard_map/all_to_all | solution.py:456
  90.5 0.0 copy-done.1
  90.5 2.0 %coarse.1 = f32[512,128]{1,0:T(8,128)} custom-call(f32[256,128]{1,0:T(8,128)S(1)} %bitcast.8, f32[16,5,8,128]{3,2,1,0:T(8,128)S(1)} %all_to_all.16.received, f32[8,128]{1,0:T(8,128)S(1)} %copy-done.3, f32[128,128]{1,0:T(8,128)S(1)} %copy-done.1), custom_call_target="tpu_custom_call" | custom-call | tf_op jit(solution)/shard_map/coarse/pallas_call | solution.py:406
  (2 shorter events, 0.1 us)
Async XLA Ops:
  1.2 26.2 %copy-start.2 = (f32[128,128]{1,0:T(8,128)S(1)}, f32[128,128]{1,0:T(8,128)}, u32[]{:S(2)}) copy-start(f32[128,128]{1,0:T(8,128)} %constant.8.clone.table) | copy-start | bytes 196612
  28.2 7.5 %collective-permute-start = (f32[25,8,128]{2,1,0:T(8,128)S(1)}, f32[25,8,128]{2,1,0:T(8,128)S(1)}, u32[]{:S(2)}, u32[]{:S(2)}) collective-permute-start(f32[25,8,128]{2,1,0:T(8,128)S(1)} %get-tuple-element.17), channel_id=1, source_target_pairs={{32,1},{33,2},{34,3},{1,32},{2,33},{3,34},{36,5},{37,6},{38,7},{5,... | collective-permute-start | bytes 307208 | tf_op jit(solution)/shard_map/ppermute | solution.py:437
  35.7 11.0 %copy-start = (f32[160,128]{1,0:T(8,128)S(1)}, f32[160,128]{1,0:T(8,128)}, u32[]{:S(2)}) copy-start(f32[160,128]{1,0:T(8,128)} %constant.9.clone.table) | copy-start | bytes 245764
  35.7 11.0 %copy-start.3 = (f32[8,128]{1,0:T(8,128)S(1)}, f32[8,128]{1,0:T(8,128)}, u32[]{:S(2)}) copy-start(f32[8,128]{1,0:T(8,128)} %constant.11.clone.lanes) | copy-start | bytes 12292
  35.7 6.5 %collective-permute-start.1 = (f32[46,8,128]{2,1,0:T(8,128)S(1)}, f32[46,8,128]{2,1,0:T(8,128)S(1)}, u32[]{:S(2)}, u32[]{:S(2)}) collective-permute-start(f32[46,8,128]{2,1,0:T(8,128)S(1)} %get-tuple-element.18), channel_id=1, source_target_pairs={{0,4},{4,8},{8,12},{12,16},{16,20},{20,24},{24,28},{1,5},{5,9},{9,... | collective-permute-start | bytes 565256 | tf_op jit(solution)/shard_map/ppermute | solution.py:443
  39.7 7.0 %collective-permute-start.2 = (f32[46,8,128]{2,1,0:T(8,128)S(1)}, f32[46,8,128]{2,1,0:T(8,128)S(1)}, u32[]{:S(2)}, u32[]{:S(2)}) collective-permute-start(f32[46,8,128]{2,1,0:T(8,128)S(1)} %get-tuple-element.19), channel_id=1, source_target_pairs={{4,0},{8,4},{12,8},{16,12},{20,16},{24,20},{28,24},{5,1},{9,5},{13... | collective-permute-start | bytes 565256 | tf_op jit(solution)/shard_map/ppermute | solution.py:444
  69.2 21.2 %copy-start.1 = (f32[128,128]{1,0:T(8,128)S(1)}, f32[128,128]{1,0:T(8,128)}, u32[]{:S(2)}) copy-start(f32[128,128]{1,0:T(8,128)} %constant.10.clone.table) | copy-start | bytes 196612

commit v5 on v3

--- a/solution.py
+++ b/solution.py
@@ -13,6 +13,7 @@
 WX = 4
 SPAN_Y = BLOCK + 2 * WY
 SPAN_X = BLOCK + 2 * WX
+ROWS = 12
 PART = 8 * WY + 1
 TM, SX, SY = 16, 8, 4
 FACES = 2 * (32 * NZ + 8 * NZ)
@@ -89,14 +90,19 @@
 
 
 def pack_kernel(rates, field, regime, out, rate_rows, sums):
+    margin = jnp.zeros((8, L), jnp.float32)
     for tp in range(4):
         rows = [
             field[pl.ds((2 * tp + t2) * 64 + x, 8, stride=8), :] for t2 in range(2) for x in range(8)
         ]
         turned = jnp.concatenate(rows, axis=0).T
+        starts = (
+            jnp.concatenate([turned, margin], axis=0),
+            jnp.concatenate([margin[:WY], turned, margin[WY:]], axis=0),
+        )
         for d in range(TM):
             s = strip_of(d)
-            out[d, tp] = turned[8 * s : 8 * s + 8]
+            out[d, ROWS * tp : ROWS * (tp + 1)] = starts[s % 2][8 * s : 8 * s + ROWS]
     columns = []
     for x in range(8):
         kind = regime[pl.ds(x, 8, stride=8), :]
@@ -106,7 +112,7 @@
         columns.append(c)
     columns.append(jnp.zeros((64, L), jnp.float32))
     c_turned = jnp.concatenate(columns, axis=0).T
-    rate_rows[...] = c_turned
+    rate_rows[...] = jnp.concatenate([margin, c_turned, margin], axis=0)
     group = lane_index(1) // 32
     row = jnp.zeros((1, L), jnp.float32)
     for g in range(4):
@@ -120,25 +126,28 @@
     return jnp.where(tm & 1 == 0, tm >> 1, TM - 1 - (tm >> 1))
 
 
-def transform_kernel(received, rate_rows, table, own, rate, low, high):
+def transform_kernel(received, rate_rows, table, window, rate, swap):
     rows = []
-    for pair in range(4):
-        both = [received[pl.ds(2 * pair + j, 64, stride=8), :] for j in range(2)]
+    for pair in range(ROWS // 2):
+        both = [received[pl.ds(2 * pair + j, 64, stride=ROWS), :] for j in range(2)]
         turned = jnp.concatenate(both, axis=0).T
         rows += list(halves(turned[:64], turned[64:]))
-    spectrum = dot(jnp.concatenate(rows, axis=0), table[...], ((1,), (0,)))
-    mine = rate_rows[pl.ds(pl.multiple_of(own_strip() * 8, 8), 8), :]
-    for y in range(8):
-        for x in range(8):
-            r = (y * 8 + x) * 8
-            own[8 * y + x] = spectrum[r : r + 8]
-            if y < WY:
-                low[8 * y + x] = spectrum[r : r + 8]
-            if y >= 8 - WY:
-                high[8 * (y - 8 + WY) + x] = spectrum[r : r + 8]
+    spectrum = dot(jnp.concatenate(rows[: 8 + WY], axis=0), table[...], ((1,), (0,)))
+    strip = own_strip()
+    even = strip & 1 == 0
+    zero = jnp.zeros((8, L), jnp.float32)
+    for i in range(8 * WY):
+        window[i] = zero
+        window[8 * (WY + 8) + i] = zero
+    offset = jnp.where(even, 8 * WY, 0)
+    for i in range(8 * (8 + WY)):
+        window[offset + i] = spectrum[8 * i : 8 * i + 8]
+    near = rate_rows[pl.ds(pl.multiple_of(strip * 8, 8), 24), :]
+    mine = jnp.concatenate([near[8 - WY : 16 + WY], jnp.zeros((2, L), jnp.float32)], axis=0)
     rate[...] = mine
-    low[PART - 1] = mine
-    high[PART - 1] = pltpu.roll(mine, WY, 0)
+    for i in range(8 * WY):
+        swap[i] = jnp.where(even, window[8 * WY + i], window[64 + i])
+    swap[PART - 1] = jnp.where(even, pltpu.roll(mine[0:8], 8 - WY, 0), mine[8:16])
 
 
 def x_range(distance):
@@ -148,35 +157,39 @@
 EDGE = [(d, y) for d in range(1, WX + 1) for y in x_range(d)]
 
 
-def strip_rows(below, own, above):
+def completed(window, rate, swapped):
+    strip = own_strip()
+    even = jnp.where(strip & 1 == 0, 1.0, 0.0)
+    odd = 1.0 - even
+
     def tile(y, x):
         if y < WY:
-            return below[8 * y + x]
+            return window[8 * y + x] + even * swapped[8 * y + x]
         if y < WY + 8:
-            return own[8 * (y - WY) + x]
-        return above[8 * (y - WY - 8) + x]
-
-    return tile
-
-
-def strip_rates(below, rate, above):
-    rows = [below[PART - 1][0:WY], rate[...], above[PART - 1][0:WY], jnp.zeros((2, L), jnp.float32)]
-    rows = jnp.concatenate(rows, axis=0)
-    return rows[0:8], rows[8:16]
-
-
-def edge_kernel(below, own, rate, above, to_left, to_right):
-    tile = strip_rows(below, own, above)
+            return window[8 * y + x]
+        return window[8 * y + x] + odd * swapped[8 * (y - WY - 8) + x]
+
+    first = jnp.where(strip == 0, 1.0, 0.0)
+    last = jnp.where(strip == TM - 1, 1.0, 0.0)
+    row = lax.broadcasted_iota(jnp.int32, (8, L), 0)
+    other = jnp.where(row < WY, swapped[PART - 1], 0.0)
+    low = rate[0:8, :] + first * other
+    high = rate[8:16, :] + last * pltpu.roll(other, WY, 0)
+    return tile, (low, high)
+
+
+def edge_kernel(window, rate, swapped, to_left, to_right):
+    tile, rates = completed(window, rate, swapped)
     for i, (d, y) in enumerate(EDGE):
         to_left[i] = tile(y, d - 1)
         to_right[i] = tile(y, 8 - d)
-    for j, c in enumerate(strip_rates(below, rate, above)):
+    for j, c in enumerate(rates):
         to_left[len(EDGE) + j] = c
         to_right[len(EDGE) + j] = c
 
 
 def solve_kernel(
-    below, own, rate, above, left, right, lanes, table, out, source, a, b, x0, x1
+    window, rate, swapped, left, right, sums, lanes, table, out, source, a, b, x0, x1
 ):
     sx, sy, strip = lax.axis_index("sx"), lax.axis_index("sy"), own_strip()
     valid = [
@@ -188,7 +201,7 @@
             (sy < SY - 1) | (strip < TM - 1),
         )
     ]
-    tile = strip_rows(below, own, above)
+    tile, rates = completed(window, rate, swapped)
     zero = jnp.zeros((8, L), jnp.float32)
     for y in range(SPAN_Y):
         for x in range(WX):
@@ -201,7 +214,7 @@
         source[y, WX + 7 + d] = right[i]
     lane = lane_index(8)
     rows = []
-    for j, mid in enumerate(strip_rates(below, rate, above)):
+    for j, mid in enumerate(rates):
         rows.append(
             jnp.where(
                 lane < 32,
@@ -272,27 +285,24 @@
         cut = result[:, 128 * pair : 128 * pair + 128]
         for j, value in enumerate(halves(cut[: TM * TILES], cut[TM * TILES :])):
             out[pl.ds(2 * pair + j, TM * TILES, stride=8), :] = value
-    rows = [jnp.sum(v, axis=0, keepdims=True) for v in (acc, *faces)]
-    rows = jnp.concatenate(rows + [jnp.zeros((5, L), jnp.float32)], axis=0)
+    homes = (
+        strip >> 2,
+        jnp.where(strip == 0, 4, (strip - 1) >> 2),
+        jnp.where(strip == TM - 1, 5, (strip + 1) >> 2),
+    )
+    index = lax.broadcasted_iota(jnp.int32, (8, L), 0)
+    share = jnp.where((index == 6) & (strip == 0), sums[...], 0.0)
+    for home, v in zip(homes, (acc, *faces)):
+        v = jnp.broadcast_to(jnp.sum(v, axis=0, keepdims=True), (8, L))
+        share = share + jnp.where(index == home, v, 0.0)
     for d in range(TM):
-        out[8 * (TILES * d + 4) : 8 * (TILES * d + 5), :] = rows
-
-
-def gather_kernel(received, sums, out):
-    part = [received[MEMBER[s], 4] for s in range(TM)]
-    rows = []
-    for g in range(4):
-        row = part[4 * g][0:1]
-        for s in range(4 * g + 1, 4 * g + 4):
-            row = row + part[s][0:1]
-        for s in range(4 * g, 4 * g + 4):
-            if s > 0:
-                row = row + part[s - 1][2:3]
-            if s < TM - 1:
-                row = row + part[s + 1][1:2]
-        rows.append(row)
-    rows += [part[0][1:2], part[TM - 1][2:3], sums[0:1, :], jnp.zeros((1, L), jnp.float32)]
-    block = jnp.concatenate(rows, axis=0)
+        out[8 * (TILES * d + 4) : 8 * (TILES * d + 5), :] = share
+
+
+def gather_kernel(received, out):
+    block = received[0, 4]
+    for d in range(1, TM):
+        block = block + received[d, 4]
     for j in range(SX * SY):
         out[j] = block
 
@@ -408,11 +418,12 @@
     )(*scalars, *arrays)
 
 
-def y_steps():
+def swaps():
     def rank(g):
         return MEMBER[g % TM] * SY + g // TM
 
-    return [(rank(g), rank(g + 1)) for g in range(SY * TM - 1)]
+    pairs = [(rank(g), rank(g + 1)) for g in range(1, SY * TM - 1, 2)]
+    return pairs + [(q, p) for p, q in pairs]
 
 
 def local(driving_input, regime, reaction_rates):
@@ -420,23 +431,21 @@
     packed, rate_rows, sums = call(
         pack_kernel,
         "pack",
-        (shape(TM, 4, 8, L), shape(L, L), shape(8, L)),
+        (shape(TM, 4 * ROWS, L), shape(L + 16, L), shape(8, L)),
         [driving_input.reshape(512, L), regime.reshape(64, L)],
         rates=reaction_rates,
     )
     received = lax.all_to_all(packed, "tm", split_axis=0, concat_axis=0, tiled=True)
-    own, rate, low, high = call(
+    window, rate, swap = call(
         transform_kernel,
         "transform",
-        (shape(64, 8, L), shape(8, L), shape(PART, 8, L), shape(PART, 8, L)),
-        [received.reshape(512, L), rate_rows, forward],
-    )
-    up = y_steps()
-    below = lax.ppermute(high, ("tm", "sy"), up)
-    above = lax.ppermute(low, ("tm", "sy"), [(q, p) for p, q in up])
+        (shape(8 * SPAN_Y, 8, L), shape(16, L), shape(PART, 8, L)),
+        [received.reshape(TM * 4 * ROWS, L), rate_rows, forward],
+    )
+    swapped = lax.ppermute(swap, ("tm", "sy"), swaps())
     tiles = len(EDGE) + 2
     to_left, to_right = call(
-        edge_kernel, "edges", (shape(tiles, 8, L),) * 2, [below, own, rate, above]
+        edge_kernel, "edges", (shape(tiles, 8, L),) * 2, [window, rate, swapped]
     )
     across = [(i, i + 1) for i in range(SX - 1)]
     left = lax.ppermute(to_right, "sx", across)
@@ -445,13 +454,13 @@
         solve_kernel,
         "sweeps",
         shape(TM * TILES * 8, L),
-        [below, own, rate, above, left, right, lanes, inverse],
+        [window, rate, swapped, left, right, sums, lanes, inverse],
         [pltpu.VMEM((SPAN_Y, SPAN_X, 8, L), jnp.float32)] * 5,
     )
     returned = lax.all_to_all(
         message.reshape(TM, TILES, 8, L), "tm", split_axis=0, concat_axis=0, tiled=True
     )
-    shared = call(gather_kernel, "gather", shape(SX * SY, 8, L), [returned, sums])
+    shared = call(gather_kernel, "gather", shape(SX * SY, 8, L), [returned])
     gathered = lax.all_to_all(shared, ("sx", "sy"), split_axis=0, concat_axis=0, tiled=True)
     result = call(
         coarse_kernel,

time: 91.8 us -> 90.2 us (0.983)
  starting transfers between devices: 12.5 us -> 9.35 us
  waiting for transfers between devices: 7.31 us -> 9.08 us
    all_to_all x1, blocking collectives: 20.3 us -> 16.8 us  [local(): lax.all_to_all(message.reshape(TM, TILES, 8, L), 'tm', split_axis=0, conc...]
    ppermute x2 -> x1, starting transfers between devices: 7.07 us -> 4.05 us  [local(): swapped = lax.ppermute(swap, ('tm', 'sy'), swaps())]
    all_to_all x1, blocking collectives: 22.2 us -> 25 us  [local(): lax.all_to_all(packed, 'tm', split_axis=0, concat_axis=0, tiled=True)]
    ppermute x2 -> x1, waiting for transfers between devices: 1.66 us -> 3.42 us  [local(): swapped = lax.ppermute(swap, ('tm', 'sy'), swaps())]
  transfers between devices with their start and end apart: 4 -> 3, of which waited for: 4 -> 3; matrix products, arithmetic and copies ran while one was open for 0% -> 0% of each run, Pallas kernels for 0% -> 0%
where the time goes in v5:
time: 90.2 us; the launch traced here: 89.8 us
  blocking collectives  63.5 us (70%)
  starting transfers between devices  9.35 us (10%)
  waiting for transfers between devices  9.08 us (10%)
  Pallas kernels  7.77 us (9%)
    all_to_all x1, blocking collectives, local(): lax.all_to_all(packed, 'tm', split_axis=0, concat_axis=0, tiled=True)  25 us
    all_to_all x1, blocking collectives, local(): lax.all_to_all(shared, ('sx', 'sy'), split_axis=0, concat_axis=0, tiled=T...  21.7 us
    all_to_all x1, blocking collectives, local(): lax.all_to_all(message.reshape(TM, TILES, 8, L), 'tm', split_axis=0, conc...  16.8 us
    pallas_call x6, Pallas kernels, call(): pl.pallas_call(kernel, name=name, out_shape=out_shape, in_specs=smem(len(...  7.77 us
    ppermute x1, waiting for transfers between devices, local(): right = lax.ppermute(to_left, 'sx', [(q, p) for p, q in across])  4.46 us
    ppermute x1, starting transfers between devices, local(): swapped = lax.ppermute(swap, ('tm', 'sy'), swaps())  4.05 us
    ppermute x1, starting transfers between devices, local(): left = lax.ppermute(to_right, 'sx', across)  4.01 us
    ppermute x1, waiting for transfers between devices, local(): swapped = lax.ppermute(swap, ('tm', 'sy'), swaps())  3.42 us
  transfers between devices with their start and end apart: 3, of which 3 were waited for; matrix products, arithmetic and copies ran while one was open for 0% of the time, Pallas kernels for 0%

profile of v5, /device:TPU:1, one launch (start us, length us, event | category | flops | bytes accessed | tf_op | source)
XLA Modules:
  0.0 89.8 jit_solution(14391601076482022086)
XLA Ops:
  0.0 1.2 %pack.1 = (f32[16,48,128]{2,1,0:T(8,128)S(1)}, f32[144,128]{1,0:T(8,128)S(1)}, f32[8,128]{1,0:T(8,128)S(1)}) custom-call(f32[8]{0:T(128)} %rates.1, f32[512,128]{1,0:T(8,128)} %bitcast.9, s32[64,128]{1,0:T(8,128)} %bitcast.10), custom_call_target="tpu_custom_call" | custom-call | tf_op jit(solution)/shard_map/pack/pallas_call | solution.py:411
  1.2 0.0 copy-start.2
  1.2 25.0 %all_to_all.15 = f32[16,48,128]{2,1,0:T(8,128)S(1)} all-to-all(f32[16,48,128]{2,1,0:T(8,128)S(1)} %get-tuple-element.13), channel_id=1, replica_groups=mesh['tm'=16,'sx'=8,'sy'=4] {'tm'}, dimensions={0} | all-to-all | bytes 786432 | tf_op jit(solution)/shard_map/all_to_all | solution.py:438
  26.3 0.0 copy-done.2
  26.3 0.8 transform.1
  27.0 4.1 %collective-permute-start = (f32[25,8,128]{2,1,0:T(8,128)S(1)}, f32[25,8,128]{2,1,0:T(8,128)S(1)}, u32[]{:S(2)}, u32[]{:S(2)}) collective-permute-start(f32[25,8,128]{2,1,0:T(8,128)S(1)} %get-tuple-element.17), channel_id=1, source_target_pairs={{64,128},{192,256},{320,384},{448,480},{416,352},{288,224},{160,96... | collective-permute-start | bytes 307208 | tf_op jit(solution)/shard_map/ppermute | solution.py:445
  31.1 3.4 %collective-permute-done.swapped = f32[25,8,128]{2,1,0:T(8,128)S(1)} collective-permute-done((f32[25,8,128]{2,1,0:T(8,128)S(1)}, f32[25,8,128]{2,1,0:T(8,128)S(1)}, u32[]{:S(2)}, u32[]{:S(2)}) %collective-permute-start) | collective-permute-done | bytes 102432 | tf_op jit(solution)/shard_map/ppermute | solution.py:445
  34.5 0.0 copy-start
  34.6 0.0 copy-start.3
  34.6 4.0 %collective-permute-start.1 = (f32[46,8,128]{2,1,0:T(8,128)S(1)}, f32[46,8,128]{2,1,0:T(8,128)S(1)}, u32[]{:S(2)}, u32[]{:S(2)}) collective-permute-start(f32[46,8,128]{2,1,0:T(8,128)S(1)} %get-tuple-element.18), channel_id=1, source_target_pairs={{0,4},{4,8},{8,12},{12,16},{16,20},{20,24},{24,28},{1,5},{5,9},{9,... | collective-permute-start | bytes 565256 | tf_op jit(solution)/shard_map/ppermute | solution.py:451
  38.6 1.3 %collective-permute-start.2 = (f32[46,8,128]{2,1,0:T(8,128)S(1)}, f32[46,8,128]{2,1,0:T(8,128)S(1)}, u32[]{:S(2)}, u32[]{:S(2)}) collective-permute-start(f32[46,8,128]{2,1,0:T(8,128)S(1)} %get-tuple-element.19), channel_id=1, source_target_pairs={{4,0},{8,4},{12,8},{16,12},{20,16},{24,20},{28,24},{5,1},{9,5},{13... | collective-permute-start | bytes 565256 | tf_op jit(solution)/shard_map/ppermute | solution.py:452
  39.9 1.2 %collective-permute-done.1.left = f32[46,8,128]{2,1,0:T(8,128)S(1)} collective-permute-done((f32[46,8,128]{2,1,0:T(8,128)S(1)}, f32[46,8,128]{2,1,0:T(8,128)S(1)}, u32[]{:S(2)}, u32[]{:S(2)}) %collective-permute-start.1) | collective-permute-done | bytes 188448 | tf_op jit(solution)/shard_map/ppermute | solution.py:451
  41.1 4.5 %collective-permute-done.2.right = f32[46,8,128]{2,1,0:T(8,128)S(1)} collective-permute-done((f32[46,8,128]{2,1,0:T(8,128)S(1)}, f32[46,8,128]{2,1,0:T(8,128)S(1)}, u32[]{:S(2)}, u32[]{:S(2)}) %collective-permute-start.2) | collective-permute-done | bytes 188448 | tf_op jit(solution)/shard_map/ppermute | solution.py:452
  45.5 0.0 copy-done
  45.6 0.0 copy-done.3
  45.6 4.0 %sweeps.1 = f32[640,128]{1,0:T(8,128)S(1)} custom-call(f32[112,8,128]{2,1,0:T(8,128)S(1)} %get-tuple-element.15.window, f32[16,128]{1,0:T(8,128)S(1)} %get-tuple-element.16.rate, f32[25,8,128]{2,1,0:T(8,128)S(1)} %collective-permute-done.swapped, f32[46,8,128]{2,1,0:T(8,128)S(1)} %collective-permute-done.1.left, ...), custom_call_target="tpu_custom_call" | custom-call | tf_op jit(solution)/shard_map/sweeps/pallas_call | solution.py:411
  49.5 16.8 %all_to_all.16.received = f32[16,5,8,128]{3,2,1,0:T(8,128)S(1)} all-to-all(f32[16,5,8,128]{3,2,1,0:T(8,128)S(1)} %bitcast.7), channel_id=1, replica_groups=mesh['tm'=16,'sx'=8,'sy'=4] {'tm'}, dimensions={0} | all-to-all | bytes 655360 | tf_op jit(solution)/shard_map/all_to_all | solution.py:460
  66.3 0.0 copy-start.1
  66.3 21.7 %all_to_all.17 = f32[32,8,128]{2,1,0:T(8,128)S(1)} all-to-all(f32[32,8,128]{2,1,0:T(8,128)S(1)} %gather.1), channel_id=1, replica_groups=mesh['tm'=16,'sx'=8,'sy'=4] {'sx','sy'}, dimensions={0} | all-to-all | bytes 262144 | tf_op jit(solution)/shard_map/all_to_all | solution.py:464
  88.0 0.0 copy-done.1
  88.0 1.8 %coarse.1 = f32[512,128]{1,0:T(8,128)} custom-call(f32[256,128]{1,0:T(8,128)S(1)} %bitcast.8, f32[16,5,8,128]{3,2,1,0:T(8,128)S(1)} %all_to_all.16.received, f32[8,128]{1,0:T(8,128)S(1)} %copy-done.3, f32[128,128]{1,0:T(8,128)S(1)} %copy-done.1), custom_call_target="tpu_custom_call" | custom-call | tf_op jit(solution)/shard_map/coarse/pallas_call | solution.py:411
  (2 shorter events, 0.1 us)
Async XLA Ops:
  1.2 25.1 %copy-start.2 = (f32[128,128]{1,0:T(8,128)S(1)}, f32[128,128]{1,0:T(8,128)}, u32[]{:S(2)}) copy-start(f32[128,128]{1,0:T(8,128)} %constant.8.clone.table) | copy-start | bytes 196612
  27.0 7.5 %collective-permute-start = (f32[25,8,128]{2,1,0:T(8,128)S(1)}, f32[25,8,128]{2,1,0:T(8,128)S(1)}, u32[]{:S(2)}, u32[]{:S(2)}) collective-permute-start(f32[25,8,128]{2,1,0:T(8,128)S(1)} %get-tuple-element.17), channel_id=1, source_target_pairs={{64,128},{192,256},{320,384},{448,480},{416,352},{288,224},{160,96... | collective-permute-start | bytes 307208 | tf_op jit(solution)/shard_map/ppermute | solution.py:445
  34.5 11.0 %copy-start = (f32[160,128]{1,0:T(8,128)S(1)}, f32[160,128]{1,0:T(8,128)}, u32[]{:S(2)}) copy-start(f32[160,128]{1,0:T(8,128)} %constant.9.clone.table) | copy-start | bytes 245764
  34.6 11.0 %copy-start.3 = (f32[8,128]{1,0:T(8,128)S(1)}, f32[8,128]{1,0:T(8,128)}, u32[]{:S(2)}) copy-start(f32[8,128]{1,0:T(8,128)} %constant.11.clone.lanes) | copy-start | bytes 12292
  34.6 6.5 %collective-permute-start.1 = (f32[46,8,128]{2,1,0:T(8,128)S(1)}, f32[46,8,128]{2,1,0:T(8,128)S(1)}, u32[]{:S(2)}, u32[]{:S(2)}) collective-permute-start(f32[46,8,128]{2,1,0:T(8,128)S(1)} %get-tuple-element.18), channel_id=1, source_target_pairs={{0,4},{4,8},{8,12},{12,16},{16,20},{20,24},{24,28},{1,5},{5,9},{9,... | collective-permute-start | bytes 565256 | tf_op jit(solution)/shard_map/ppermute | solution.py:451
  38.6 7.0 %collective-permute-start.2 = (f32[46,8,128]{2,1,0:T(8,128)S(1)}, f32[46,8,128]{2,1,0:T(8,128)S(1)}, u32[]{:S(2)}, u32[]{:S(2)}) collective-permute-start(f32[46,8,128]{2,1,0:T(8,128)S(1)} %get-tuple-element.19), channel_id=1, source_target_pairs={{4,0},{8,4},{12,8},{16,12},{20,16},{24,20},{28,24},{5,1},{9,5},{13... | collective-permute-start | bytes 565256 | tf_op jit(solution)/shard_map/ppermute | solution.py:452
  66.3 21.7 %copy-start.1 = (f32[128,128]{1,0:T(8,128)S(1)}, f32[128,128]{1,0:T(8,128)}, u32[]{:S(2)}) copy-start(f32[128,128]{1,0:T(8,128)} %constant.10.clone.table) | copy-start | bytes 196612

commit v6 on v5

--- a/solution.py
+++ b/solution.py
@@ -28,6 +28,12 @@
 
 
 MEMBER = {strip_of(d): d for d in range(TM)}
+
+
+def two_parts(table):
+    value = np.asarray(table, jnp.bfloat16)
+    rest = np.asarray(table - np.asarray(value, np.float64), jnp.bfloat16)
+    return np.stack([value, rest])
 
 
 def tables():
@@ -53,7 +59,7 @@
     padded = np.zeros((2, TM, TILES, L))
     padded[:, :, :4] = inverse[order].reshape(2, TM, 4, L)
     as32 = lambda a: np.asarray(a, np.float32)
-    return as32(forward[order]), as32(padded.reshape(-1, L)), as32(inverse), as32(lanes)
+    return two_parts(forward[order]), two_parts(padded.reshape(-1, L)), as32(inverse), as32(lanes)
 
 
 FORWARD, INVERSE, NATURAL, LANES = tables()
@@ -71,10 +77,15 @@
     return jax.ShapeDtypeStruct(dims, jnp.float32)
 
 
-def dot(a, b, dims):
-    return lax.dot_general(
-        a, b, (dims, ((), ())), precision=lax.Precision.HIGHEST, preferred_element_type=jnp.float32
-    )
+def dot(a, table, dims, table_first=False):
+    value = a.astype(jnp.bfloat16)
+    rest = (a - value.astype(jnp.float32)).astype(jnp.bfloat16)
+    total = None
+    for x, t in ((rest, table[0]), (value, table[1]), (value, table[0])):
+        pair = (t, x) if table_first else (x, t)
+        term = lax.dot_general(*pair, (dims, ((), ())), preferred_element_type=jnp.float32)
+        total = term if total is None else total + term
+    return total
 
 
 def lane_index(rows):
@@ -132,7 +143,7 @@
         both = [received[pl.ds(2 * pair + j, 64, stride=ROWS), :] for j in range(2)]
         turned = jnp.concatenate(both, axis=0).T
         rows += list(halves(turned[:64], turned[64:]))
-    spectrum = dot(jnp.concatenate(rows[: 8 + WY], axis=0), table[...], ((1,), (0,)))
+    spectrum = dot(jnp.concatenate(rows[: 8 + WY], axis=0), table, ((1,), (0,)))
     strip = own_strip()
     even = strip & 1 == 0
     zero = jnp.zeros((8, L), jnp.float32)
@@ -178,91 +189,135 @@
     return tile, (low, high)
 
 
-def edge_kernel(window, rate, swapped, to_left, to_right):
+def edge_kernel(window, rate, swapped, to_odd, to_even):
     tile, rates = completed(window, rate, swapped)
+    even = lax.axis_index("sx") & 1 == 0
     for i, (d, y) in enumerate(EDGE):
-        to_left[i] = tile(y, d - 1)
-        to_right[i] = tile(y, 8 - d)
+        left, right = tile(y, d - 1), tile(y, 8 - d)
+        to_odd[i] = jnp.where(even, right, left)
+        to_even[i] = jnp.where(even, left, right)
     for j, c in enumerate(rates):
-        to_left[len(EDGE) + j] = c
-        to_right[len(EDGE) + j] = c
-
-
-def solve_kernel(
-    window, rate, swapped, left, right, sums, lanes, table, out, source, a, b, x0, x1
-):
+        to_odd[len(EDGE) + j] = c
+        to_even[len(EDGE) + j] = c
+
+
+def inside():
     sx, sy, strip = lax.axis_index("sx"), lax.axis_index("sy"), own_strip()
-    valid = [
-        jnp.where(inside, 1.0, 0.0)
-        for inside in (
+    return [
+        jnp.where(ok, 1.0, 0.0)
+        for ok in (
             sx > 0,
             sx < SX - 1,
             (sy > 0) | (strip > 0),
             (sy < SY - 1) | (strip < TM - 1),
         )
     ]
+
+
+def cell_terms(c, lanes):
+    d = c + lanes[0:1, :] + 6.0
+    sine = lanes[1:2, :]
+    inverse = 1.0 / (d * d + sine * sine)
+    return d * inverse, sine * inverse
+
+
+def prepare_kernel(window, rate, swapped, lanes, source, a, b, first):
     tile, rates = completed(window, rate, swapped)
+    valid = inside()
+    rows = jnp.concatenate([*rates, jnp.zeros((112, L), jnp.float32)], axis=0)
+    turned = rows.T
+    for y in range(SPAN_Y):
+        for x in range(8):
+            c = jnp.broadcast_to(turned[8 * x : 8 * x + 8, y : y + 1], (8, L))
+            ax, bx = cell_terms(c, lanes)
+            if not WY <= y < WY + 8:
+                ok = valid[2] if y < WY else valid[3]
+                ax, bx = ax * ok, bx * ok
+            s = tile(y, x)
+            source[y, x] = s
+            a[y, x] = ax
+            b[y, x] = bx
+            first[y, x] = ax * s + bx * pltpu.roll(s, 64, 1)
+
+
+def solve_kernel(
+    own_s, own_a, own_b, own_x, from_odd, from_even, sums, lanes, table, out, hs, ha, hb, hx, x0, x1
+):
+    strip = own_strip()
+    valid = inside()
+    even = lax.axis_index("sx") & 1 == 0
     zero = jnp.zeros((8, L), jnp.float32)
+
+    def left(i):
+        return jnp.where(even, from_even[i], from_odd[i])
+
+    def right(i):
+        return jnp.where(even, from_odd[i], from_even[i])
+
     for y in range(SPAN_Y):
-        for x in range(WX):
-            source[y, x] = zero
-            source[y, SPAN_X - 1 - x] = zero
-        for x in range(8):
-            source[y, WX + x] = tile(y, x)
+        for h in range(8):
+            hs[y, h] = zero
     for i, (d, y) in enumerate(EDGE):
-        source[y, WX - d] = left[i]
-        source[y, WX + 7 + d] = right[i]
+        hs[y, WX - d] = left(i)
+        hs[y, WX - 1 + d] = right(i)
     lane = lane_index(8)
     rows = []
-    for j, mid in enumerate(rates):
-        rows.append(
-            jnp.where(
-                lane < 32,
-                pltpu.roll(left[len(EDGE) + j], 96, 1),
-                jnp.where(
-                    lane < 96, pltpu.roll(mid, 32, 1), pltpu.roll(right[len(EDGE) + j], 96, 1)
-                ),
-            )
-        )
+    for j in range(2):
+        n = len(EDGE) + j
+        rows.append(jnp.where(lane < 32, pltpu.roll(left(n), 96, 1), pltpu.roll(right(n), 32, 1)))
     rows.append(jnp.zeros((112, L), jnp.float32))
     turned = jnp.concatenate(rows, axis=0).T
-    base = jnp.broadcast_to(lanes[0:1, :] + 6.0, (8, L))
-    sine = jnp.broadcast_to(lanes[1:2, :], (8, L))
-    sine_square = sine * sine
     for y in range(SPAN_Y):
-        for x in range(SPAN_X):
-            d = jnp.broadcast_to(turned[8 * x : 8 * x + 8, y : y + 1], (8, L)) + base
-            inverse = 1.0 / (d * d + sine_square)
+        for h in range(8):
+            distance = WX - h if h < WX else h - WX + 1
+            if y not in x_range(distance):
+                ha[y, h] = zero
+                hb[y, h] = zero
+                hx[y, h] = zero
+                continue
+            c = jnp.broadcast_to(turned[8 * h : 8 * h + 8, y : y + 1], (8, L))
+            ax, bx = cell_terms(c, lanes)
+            ok = valid[0] if h < WX else valid[1]
+            if y < WY:
+                ok = ok * valid[2]
+            elif y >= WY + 8:
+                ok = ok * valid[3]
+            ax, bx = ax * ok, bx * ok
+            s = hs[y, h]
+            ha[y, h] = ax
+            hb[y, h] = bx
+            hx[y, h] = ax * s + bx * pltpu.roll(s, 64, 1)
+
+    def split(own, halo):
+        def get(y, x):
             if x < WX:
-                inverse = inverse * valid[0]
-            elif x >= WX + 8:
-                inverse = inverse * valid[1]
-            if y < WY:
-                inverse = inverse * valid[2]
-            elif y >= WY + 8:
-                inverse = inverse * valid[3]
-            ax = d * inverse
-            bx = sine * inverse
-            a[y, x] = ax
-            b[y, x] = bx
-            s = source[y, x]
-            x0[y, x] = ax * s + bx * pltpu.roll(s, 64, 1)
+                return halo[y, x]
+            if x < WX + 8:
+                return own[y, x - WX]
+            return halo[y, x - 8]
+
+        return get
+
+    source, a, b = split(own_s, hs), split(own_a, ha), split(own_b, hb)
+
+    def whole(ref):
+        return lambda y, x: ref[y, x]
 
     def sweep(old, new, margin):
         def row(y, carry):
             for x in range(margin, SPAN_X - margin):
-                v = old[y, x]
-                u = source[y, x] + (old[y, x + 1] + old[y, x - 1])
-                u = u + (old[y + 1, x] + old[y - 1, x])
+                v = old(y, x)
+                u = source(y, x) + (old(y, x + 1) + old(y, x - 1))
+                u = u + (old(y + 1, x) + old(y - 1, x))
                 u = u + (pltpu.roll(v, 1, 0) + pltpu.roll(v, 7, 0))
-                new[y, x] = a[y, x] * u + b[y, x] * pltpu.roll(u, 64, 1)
+                new[y, x] = a(y, x) * u + b(y, x) * pltpu.roll(u, 64, 1)
             return carry
 
         lax.fori_loop(margin, SPAN_Y - margin, row, 0)
 
-    sweep(x0, x1, 1)
-    sweep(x1, x0, 2)
-    sweep(x0, x1, 3)
+    sweep(split(own_x, hx), x1, 1)
+    sweep(whole(x1), x0, 2)
+    sweep(whole(x0), x1, 3)
     lo, hi = WX, WX + 8
 
     def change(y, x):
@@ -280,7 +335,7 @@
         if end:
             faces.append(line)
     solved = x1[WY : WY + 8, lo:hi].reshape(512, L)
-    result = dot(table[...], solved, ((1,), (1,)))
+    result = dot(solved, table, ((1,), (1,)), table_first=True)
     for pair in range(4):
         cut = result[:, 128 * pair : 128 * pair + 128]
         for j, value in enumerate(halves(cut[: TM * TILES], cut[TM * TILES :])):
@@ -401,7 +456,7 @@
                 out[pl.ds(t * 64 + x, 8, stride=8), :] = turned[r : r + 8] + plus
 
 
-def call(kernel, name, out_shape, arrays, scratch=(), rates=None, keep=True):
+def call(kernel, name, out_shape, arrays, scratch=(), rates=None, keep=True, flops=0):
     if keep:
         out_shape = jax.tree.map(lambda o: pltpu.VMEM(o.shape, o.dtype), out_shape)
     if rates is None:
@@ -415,6 +470,8 @@
         in_specs=smem(len(scalars)) + vmem(len(arrays)),
         out_specs=tuple(vmem(len(out_shape))) if many else vmem(1)[0],
         scratch_shapes=list(scratch),
+        compiler_params=pltpu.CompilerParams(vmem_limit_bytes=24 * 2**20),
+        cost_estimate=pl.CostEstimate(flops=flops, transcendentals=0, bytes_accessed=0),
     )(*scalars, *arrays)
 
 
@@ -444,18 +501,30 @@
     )
     swapped = lax.ppermute(swap, ("tm", "sy"), swaps())
     tiles = len(EDGE) + 2
-    to_left, to_right = call(
+    to_odd, to_even = call(
         edge_kernel, "edges", (shape(tiles, 8, L),) * 2, [window, rate, swapped]
     )
-    across = [(i, i + 1) for i in range(SX - 1)]
-    left = lax.ppermute(to_right, "sx", across)
-    right = lax.ppermute(to_left, "sx", [(q, p) for p, q in across])
+
+    def x_swaps(first):
+        pairs = [(i, i + 1) for i in range(first, SX - 1, 2)]
+        return pairs + [(q, p) for p, q in pairs]
+
+    from_odd = lax.ppermute(to_odd, "sx", x_swaps(0))
+    from_even = lax.ppermute(to_even, "sx", x_swaps(1))
+    prepared = call(
+        prepare_kernel,
+        "prepare",
+        (shape(SPAN_Y, 8, 8, L),) * 4,
+        [window, rate, swapped, lanes],
+        flops=10**7,
+    )
+    half = pltpu.VMEM((SPAN_Y, 8, 8, L), jnp.float32)
     message = call(
         solve_kernel,
         "sweeps",
         shape(TM * TILES * 8, L),
-        [window, rate, swapped, left, right, sums, lanes, inverse],
-        [pltpu.VMEM((SPAN_Y, SPAN_X, 8, L), jnp.float32)] * 5,
+        [*prepared, from_odd, from_even, sums, lanes, inverse],
+        [half] * 4 + [pltpu.VMEM((SPAN_Y, SPAN_X, 8, L), jnp.float32)] * 2,
     )
     returned = lax.all_to_all(
         message.reshape(TM, TILES, 8, L), "tm", split_axis=0, concat_axis=0, tiled=True

time: 90.2 us -> 92.7 us (1.028)
  blocking collectives: 63.5 us -> 68.6 us
  waiting for transfers between devices: 9.08 us -> 5.1 us
  local copies, waits for them, and re-layouts: 0.02 us -> 2.39 us
    all_to_all x1, blocking collectives: 21.7 us -> 26.2 us  [local(): lax.all_to_all(shared, ('sx', 'sy'), split_axis=0, concat_axis=0, tiled=T...]
    ppermute x2, waiting for transfers between devices: 5.66 us -> 1.68 us  [the longest x1 1.68 us: local(): from_odd = lax.ppermute(to_odd, 'sx', x_swaps(0))]
    unnamed x8 -> x14, local copies, waits for them, and re-layouts: 0.02 us -> 2.39 us
    pallas_call x6 -> x7, Pallas kernels: 7.77 us -> 7.17 us  [call(): pl.pallas_call(kernel, name=name, out_shape=out_shape, in_specs=smem(len(...]
  transfers between devices with their start and end apart: 3 -> 3, of which waited for: 3 -> 2; matrix products, arithmetic and copies ran while one was open for 0% -> 0% of each run, Pallas kernels for 0% -> 0%
where the time goes in v6:
time: 92.7 us; the launch traced here: 92.2 us
  blocking collectives  68.6 us (74%)
  starting transfers between devices  8.86 us (10%)
  Pallas kernels  7.17 us (8%)
  waiting for transfers between devices  5.1 us (6%)
  local copies, waits for them, and re-layouts  2.39 us (3%)
    all_to_all x1, blocking collectives, local(): lax.all_to_all(shared, ('sx', 'sy'), split_axis=0, concat_axis=0, tiled=T...  26.2 us
    all_to_all x1, blocking collectives, local(): lax.all_to_all(packed, 'tm', split_axis=0, concat_axis=0, tiled=True)  25 us
    all_to_all x1, blocking collectives, local(): lax.all_to_all(message.reshape(TM, TILES, 8, L), 'tm', split_axis=0, conc...  17.3 us
    pallas_call x7, Pallas kernels, call(): pl.pallas_call(kernel, name=name, out_shape=out_shape, in_specs=smem(len(...  7.17 us
    ppermute x1, starting transfers between devices, local(): swapped = lax.ppermute(swap, ('tm', 'sy'), swaps())  4.06 us
    ppermute x1, starting transfers between devices, local(): from_odd = lax.ppermute(to_odd, 'sx', x_swaps(0))  4 us
    ppermute x1, waiting for transfers between devices, local(): swapped = lax.ppermute(swap, ('tm', 'sy'), swaps())  3.42 us
    unnamed x14, local copies, waits for them, and re-layouts  2.39 us
  transfers between devices with their start and end apart: 3, of which 2 were waited for; matrix products, arithmetic and copies ran while one was open for 0% of the time, Pallas kernels for 0%

profile of v6, /device:TPU:1, one launch (start us, length us, event | category | flops | bytes accessed | tf_op | source)
XLA Modules:
  0.0 92.2 jit_solution(4639457907619967428)
XLA Ops:
  0.0 0.0 copy-start.6
  0.0 0.7 copy-done.6
  0.7 0.0 copy-start
  0.7 0.9 %copy-done = f32[8,8,8,128]{3,2,1,0:T(8,128)S(1)} copy-done((f32[8,8,8,128]{3,2,1,0:T(8,128)S(1)}, f32[8,8,8,128]{3,2,1,0:T(8,128)}, u32[]{:S(2)}) %copy-start) | copy-done | bytes 262168
  1.6 0.0 copy-start.5
  1.6 0.8 copy-done.5
  2.4 0.8 pack.1
  3.1 0.0 copy-start.3
  3.2 25.0 %all_to_all.15 = f32[16,48,128]{2,1,0:T(8,128)S(1)} all-to-all(f32[16,48,128]{2,1,0:T(8,128)S(1)} %get-tuple-element.17), channel_id=1, replica_groups=mesh['tm'=16,'sx'=8,'sy'=4] {'tm'}, dimensions={0} | all-to-all | bytes 786432 | tf_op jit(solution)/shard_map/all_to_all | solution.py:495
  28.2 0.0 copy-done.3
  28.2 0.6 transform.1
  28.8 4.1 %collective-permute-start = (f32[25,8,128]{2,1,0:T(8,128)S(1)}, f32[25,8,128]{2,1,0:T(8,128)S(1)}, u32[]{:S(2)}, u32[]{:S(2)}) collective-permute-start(f32[25,8,128]{2,1,0:T(8,128)S(1)} %get-tuple-element.21), channel_id=1, source_target_pairs={{64,128},{192,256},{320,384},{448,480},{416,352},{288,224},{160,96... | collective-permute-start | bytes 307208 | tf_op jit(solution)/shard_map/ppermute | solution.py:502
  32.9 3.4 %collective-permute-done.swapped = f32[25,8,128]{2,1,0:T(8,128)S(1)} collective-permute-done((f32[25,8,128]{2,1,0:T(8,128)S(1)}, f32[25,8,128]{2,1,0:T(8,128)S(1)}, u32[]{:S(2)}, u32[]{:S(2)}) %collective-permute-start) | collective-permute-done | bytes 102432 | tf_op jit(solution)/shard_map/ppermute | solution.py:502
  36.3 0.0 copy-start.4
  36.4 4.0 %collective-permute-start.1 = (f32[46,8,128]{2,1,0:T(8,128)S(1)}, f32[46,8,128]{2,1,0:T(8,128)S(1)}, u32[]{:S(2)}, u32[]{:S(2)}) collective-permute-start(f32[46,8,128]{2,1,0:T(8,128)S(1)} %get-tuple-element.26), channel_id=1, source_target_pairs={{0,4},{8,12},{16,20},{24,28},{4,0},{12,8},{20,16},{28,24},{1,5},{9... | collective-permute-start | bytes 565256 | tf_op jit(solution)/shard_map/ppermute | solution.py:512
  40.4 0.0 copy-start.1
  40.4 0.8 collective-permute-start.2
  41.2 0.0 copy-done.4
  41.2 0.4 prepare.1
  41.7 1.7 %collective-permute-done.1.from_odd = f32[46,8,128]{2,1,0:T(8,128)S(1)} collective-permute-done((f32[46,8,128]{2,1,0:T(8,128)S(1)}, f32[46,8,128]{2,1,0:T(8,128)S(1)}, u32[]{:S(2)}, u32[]{:S(2)}) %collective-permute-start.1) | collective-permute-done | bytes 188448 | tf_op jit(solution)/shard_map/ppermute | solution.py:512
  43.3 0.0 collective-permute-done.2.from_even
  43.3 0.0 copy-done.1
  43.3 3.5 %sweeps.1 = f32[640,128]{1,0:T(8,128)S(1)} custom-call(f32[14,8,8,128]{3,2,1,0:T(8,128)S(1)} %get-tuple-element.22.own_s, f32[14,8,8,128]{3,2,1,0:T(8,128)S(1)} %get-tuple-element.23.own_a, f32[14,8,8,128]{3,2,1,0:T(8,128)S(1)} %get-tuple-element.24.own_b, f32[14,8,8,128]{3,2,1,0:T(8,128)S(1)} %get-tuple-element.25.own_x, ...), custom_call_target="tpu_custom_call" | custom-call | tf_op jit(solution)/shard_map/sweeps/pallas_call | solution.py:466
  46.8 17.3 %all_to_all.16.received = f32[16,5,8,128]{3,2,1,0:T(8,128)S(1)} all-to-all(f32[16,5,8,128]{3,2,1,0:T(8,128)S(1)} %bitcast.7), channel_id=1, replica_groups=mesh['tm'=16,'sx'=8,'sy'=4] {'tm'}, dimensions={0} | all-to-all | bytes 655360 | tf_op jit(solution)/shard_map/all_to_all | solution.py:529
  64.2 0.0 copy-start.2
  64.2 26.2 %all_to_all.17 = f32[32,8,128]{2,1,0:T(8,128)S(1)} all-to-all(f32[32,8,128]{2,1,0:T(8,128)S(1)} %gather.1), channel_id=1, replica_groups=mesh['tm'=16,'sx'=8,'sy'=4] {'sx','sy'}, dimensions={0} | all-to-all | bytes 262144 | tf_op jit(solution)/shard_map/all_to_all | solution.py:533
  90.4 0.0 copy-done.2
  90.4 1.8 %coarse.1 = f32[512,128]{1,0:T(8,128)} custom-call(f32[256,128]{1,0:T(8,128)S(1)} %bitcast.8, f32[16,5,8,128]{3,2,1,0:T(8,128)S(1)} %all_to_all.16.received, f32[8,128]{1,0:T(8,128)S(1)} %copy-done.4, f32[128,128]{1,0:T(8,128)S(1)} %copy-done.2), custom_call_target="tpu_custom_call" | custom-call | tf_op jit(solution)/shard_map/coarse/pallas_call | solution.py:466
  (2 shorter events, 0.1 us)
Async XLA Ops:
  0.0 0.7 copy-start.6
  0.7 0.9 %copy-start = (f32[8,8,8,128]{3,2,1,0:T(8,128)S(1)}, f32[8,8,8,128]{3,2,1,0:T(8,128)}, u32[]{:S(2)}) copy-start(f32[8,8,8,128]{3,2,1,0:T(8,128)} %param.7) | copy-start | bytes 786436
  1.6 0.8 copy-start.5
  3.1 25.1 %copy-start.3 = (bf16[2,128,128]{2,1,0:T(8,128)(2,1)S(1)}, bf16[2,128,128]{2,1,0:T(8,128)(2,1)}, u32[]{:S(2)}) copy-start(bf16[2,128,128]{2,1,0:T(8,128)(2,1)} %constant.8.clone.table) | copy-start | bytes 196612
  28.8 7.5 %collective-permute-start = (f32[25,8,128]{2,1,0:T(8,128)S(1)}, f32[25,8,128]{2,1,0:T(8,128)S(1)}, u32[]{:S(2)}, u32[]{:S(2)}) collective-permute-start(f32[25,8,128]{2,1,0:T(8,128)S(1)} %get-tuple-element.21), channel_id=1, source_target_pairs={{64,128},{192,256},{320,384},{448,480},{416,352},{288,224},{160,96... | collective-permute-start | bytes 307208 | tf_op jit(solution)/shard_map/ppermute | solution.py:502
  36.3 4.9 %copy-start.4 = (f32[8,128]{1,0:T(8,128)S(1)}, f32[8,128]{1,0:T(8,128)}, u32[]{:S(2)}) copy-start(f32[8,128]{1,0:T(8,128)} %constant.11.clone.lanes) | copy-start | bytes 12292
  36.4 7.0 %collective-permute-start.1 = (f32[46,8,128]{2,1,0:T(8,128)S(1)}, f32[46,8,128]{2,1,0:T(8,128)S(1)}, u32[]{:S(2)}, u32[]{:S(2)}) collective-permute-start(f32[46,8,128]{2,1,0:T(8,128)S(1)} %get-tuple-element.26), channel_id=1, source_target_pairs={{0,4},{8,12},{16,20},{24,28},{4,0},{12,8},{20,16},{28,24},{1,5},{9... | collective-permute-start | bytes 565256 | tf_op jit(solution)/shard_map/ppermute | solution.py:512
  40.4 3.0 %copy-start.1 = (bf16[2,160,128]{2,1,0:T(8,128)(2,1)S(1)}, bf16[2,160,128]{2,1,0:T(8,128)(2,1)}, u32[]{:S(2)}) copy-start(bf16[2,160,128]{2,1,0:T(8,128)(2,1)} %constant.9.clone.table) | copy-start | bytes 245764
  40.4 2.9 %collective-permute-start.2 = (f32[46,8,128]{2,1,0:T(8,128)S(1)}, f32[46,8,128]{2,1,0:T(8,128)S(1)}, u32[]{:S(2)}, u32[]{:S(2)}) collective-permute-start(f32[46,8,128]{2,1,0:T(8,128)S(1)} %get-tuple-element.27), channel_id=1, source_target_pairs={{4,8},{12,16},{20,24},{8,4},{16,12},{24,20},{5,9},{13,17},{21,25},... | collective-permute-start | bytes 565256 | tf_op jit(solution)/shard_map/ppermute | solution.py:513
  64.2 26.2 %copy-start.2 = (f32[128,128]{1,0:T(8,128)S(1)}, f32[128,128]{1,0:T(8,128)}, u32[]{:S(2)}) copy-start(f32[128,128]{1,0:T(8,128)} %constant.10.clone.table) | copy-start | bytes 196612

commit v7 on v6

--- a/solution.py
+++ b/solution.py
@@ -189,16 +189,14 @@
     return tile, (low, high)
 
 
-def edge_kernel(window, rate, swapped, to_odd, to_even):
+def edge_kernel(window, rate, swapped, to_left, to_right):
     tile, rates = completed(window, rate, swapped)
-    even = lax.axis_index("sx") & 1 == 0
     for i, (d, y) in enumerate(EDGE):
-        left, right = tile(y, d - 1), tile(y, 8 - d)
-        to_odd[i] = jnp.where(even, right, left)
-        to_even[i] = jnp.where(even, left, right)
+        to_left[i] = tile(y, d - 1)
+        to_right[i] = tile(y, 8 - d)
     for j, c in enumerate(rates):
-        to_odd[len(EDGE) + j] = c
-        to_even[len(EDGE) + j] = c
+        to_left[len(EDGE) + j] = c
+        to_right[len(EDGE) + j] = c
 
 
 def inside():
@@ -241,30 +239,23 @@
 
 
 def solve_kernel(
-    own_s, own_a, own_b, own_x, from_odd, from_even, sums, lanes, table, out, hs, ha, hb, hx, x0, x1
+    own_s, own_a, own_b, own_x, left, right, sums, lanes, table, out, hs, ha, hb, hx, x0, x1
 ):
     strip = own_strip()
     valid = inside()
-    even = lax.axis_index("sx") & 1 == 0
     zero = jnp.zeros((8, L), jnp.float32)
-
-    def left(i):
-        return jnp.where(even, from_even[i], from_odd[i])
-
-    def right(i):
-        return jnp.where(even, from_odd[i], from_even[i])
 
     for y in range(SPAN_Y):
         for h in range(8):
             hs[y, h] = zero
     for i, (d, y) in enumerate(EDGE):
-        hs[y, WX - d] = left(i)
-        hs[y, WX - 1 + d] = right(i)
+        hs[y, WX - d] = left[i]
+        hs[y, WX - 1 + d] = right[i]
     lane = lane_index(8)
     rows = []
     for j in range(2):
         n = len(EDGE) + j
-        rows.append(jnp.where(lane < 32, pltpu.roll(left(n), 96, 1), pltpu.roll(right(n), 32, 1)))
+        rows.append(jnp.where(lane < 32, pltpu.roll(left[n], 96, 1), pltpu.roll(right[n], 32, 1)))
     rows.append(jnp.zeros((112, L), jnp.float32))
     turned = jnp.concatenate(rows, axis=0).T
     for y in range(SPAN_Y):
@@ -462,6 +453,7 @@
     if rates is None:
         arrays = [pltpu.with_memory_space_constraint(x, pltpu.VMEM) for x in arrays]
     scalars = [] if rates is None else [rates]
+    limit = 24 * 2**20 if rates is None else None
     many = isinstance(out_shape, tuple)
     return pl.pallas_call(
         kernel,
@@ -470,7 +462,7 @@
         in_specs=smem(len(scalars)) + vmem(len(arrays)),
         out_specs=tuple(vmem(len(out_shape))) if many else vmem(1)[0],
         scratch_shapes=list(scratch),
-        compiler_params=pltpu.CompilerParams(vmem_limit_bytes=24 * 2**20),
+        compiler_params=pltpu.CompilerParams(vmem_limit_bytes=limit),
         cost_estimate=pl.CostEstimate(flops=flops, transcendentals=0, bytes_accessed=0),
     )(*scalars, *arrays)
 
@@ -501,16 +493,12 @@
     )
     swapped = lax.ppermute(swap, ("tm", "sy"), swaps())
     tiles = len(EDGE) + 2
-    to_odd, to_even = call(
+    to_left, to_right = call(
         edge_kernel, "edges", (shape(tiles, 8, L),) * 2, [window, rate, swapped]
     )
-
-    def x_swaps(first):
-        pairs = [(i, i + 1) for i in range(first, SX - 1, 2)]
-        return pairs + [(q, p) for p, q in pairs]
-
-    from_odd = lax.ppermute(to_odd, "sx", x_swaps(0))
-    from_even = lax.ppermute(to_even, "sx", x_swaps(1))
+    across = [(i, i + 1) for i in range(SX - 1)]
+    left = lax.ppermute(to_right, "sx", across)
+    right = lax.ppermute(to_left, "sx", [(q, p) for p, q in across])
     prepared = call(
         prepare_kernel,
         "prepare",
@@ -523,7 +511,7 @@
         solve_kernel,
         "sweeps",
         shape(TM * TILES * 8, L),
-        [*prepared, from_odd, from_even, sums, lanes, inverse],
+        [*prepared, left, right, sums, lanes, inverse],
         [half] * 4 + [pltpu.VMEM((SPAN_Y, SPAN_X, 8, L), jnp.float32)] * 2,
     )
     returned = lax.all_to_all(

time: 92.7 us -> 89.7 us (0.968)
  blocking collectives: 68.6 us -> 63.5 us
  waiting for transfers between devices: 5.1 us -> 8.63 us
  local copies, waits for them, and re-layouts: 2.39 us -> 0.02 us
    all_to_all x1, blocking collectives: 26.2 us -> 21.7 us  [local(): lax.all_to_all(shared, ('sx', 'sy'), split_axis=0, concat_axis=0, tiled=T...]
    ppermute x2, waiting for transfers between devices: 1.68 us -> 5.2 us  [the longest x1 4.6 us: local(): right = lax.ppermute(to_left, 'sx', [(q, p) for p, q in across])]
    unnamed x14 -> x8, local copies, waits for them, and re-layouts: 2.39 us -> 0.02 us
  transfers between devices with their start and end apart: 3 -> 3, of which waited for: 2 -> 3; matrix products, arithmetic and copies ran while one was open for 0% -> 0% of each run, Pallas kernels for 0% -> 0%
where the time goes in v7:
time: 89.7 us; the launch traced here: 89.3 us
  blocking collectives  63.5 us (71%)
  starting transfers between devices  9.48 us (11%)
  waiting for transfers between devices  8.63 us (10%)
  Pallas kernels  7.56 us (8%)
    all_to_all x1, blocking collectives, local(): lax.all_to_all(packed, 'tm', split_axis=0, concat_axis=0, tiled=True)  25 us
    all_to_all x1, blocking collectives, local(): lax.all_to_all(shared, ('sx', 'sy'), split_axis=0, concat_axis=0, tiled=T...  21.7 us
    all_to_all x1, blocking collectives, local(): lax.all_to_all(message.reshape(TM, TILES, 8, L), 'tm', split_axis=0, conc...  16.7 us
    pallas_call x7, Pallas kernels, call(): pl.pallas_call(kernel, name=name, out_shape=out_shape, in_specs=smem(len(...  7.56 us
    ppermute x1, waiting for transfers between devices, local(): right = lax.ppermute(to_left, 'sx', [(q, p) for p, q in across])  4.6 us
    ppermute x1, starting transfers between devices, local(): swapped = lax.ppermute(swap, ('tm', 'sy'), swaps())  4.05 us
    ppermute x1, starting transfers between devices, local(): left = lax.ppermute(to_right, 'sx', across)  4.01 us
    ppermute x1, waiting for transfers between devices, local(): swapped = lax.ppermute(swap, ('tm', 'sy'), swaps())  3.42 us
  transfers between devices with their start and end apart: 3, of which 3 were waited for; matrix products, arithmetic and copies ran while one was open for 0% of the time, Pallas kernels for 0%

profile of v7, /device:TPU:1, one launch (start us, length us, event | category | flops | bytes accessed | tf_op | source)
XLA Modules:
  0.0 89.3 jit_solution(13197988505618218303)
XLA Ops:
  0.0 1.2 %pack.1 = (f32[16,48,128]{2,1,0:T(8,128)S(1)}, f32[144,128]{1,0:T(8,128)S(1)}, f32[8,128]{1,0:T(8,128)S(1)}) custom-call(f32[8]{0:T(128)} %rates.1, f32[512,128]{1,0:T(8,128)} %bitcast.9, s32[64,128]{1,0:T(8,128)} %bitcast.10), custom_call_target="tpu_custom_call" | custom-call | tf_op jit(solution)/shard_map/pack/pallas_call | solution.py:458
  1.2 0.0 copy-start.2
  1.2 25.0 %all_to_all.15 = f32[16,48,128]{2,1,0:T(8,128)S(1)} all-to-all(f32[16,48,128]{2,1,0:T(8,128)S(1)} %get-tuple-element.17), channel_id=1, replica_groups=mesh['tm'=16,'sx'=8,'sy'=4] {'tm'}, dimensions={0} | all-to-all | bytes 786432 | tf_op jit(solution)/shard_map/all_to_all | solution.py:487
  26.3 0.0 copy-done.2
  26.3 0.6 transform.1
  26.9 4.1 %collective-permute-start = (f32[25,8,128]{2,1,0:T(8,128)S(1)}, f32[25,8,128]{2,1,0:T(8,128)S(1)}, u32[]{:S(2)}, u32[]{:S(2)}) collective-permute-start(f32[25,8,128]{2,1,0:T(8,128)S(1)} %get-tuple-element.21), channel_id=1, source_target_pairs={{64,128},{192,256},{320,384},{448,480},{416,352},{288,224},{160,96... | collective-permute-start | bytes 307208 | tf_op jit(solution)/shard_map/ppermute | solution.py:494
  31.0 3.4 %collective-permute-done.swapped = f32[25,8,128]{2,1,0:T(8,128)S(1)} collective-permute-done((f32[25,8,128]{2,1,0:T(8,128)S(1)}, f32[25,8,128]{2,1,0:T(8,128)S(1)}, u32[]{:S(2)}, u32[]{:S(2)}) %collective-permute-start) | collective-permute-done | bytes 102432 | tf_op jit(solution)/shard_map/ppermute | solution.py:494
  34.4 0.0 copy-start.3
  34.4 4.0 %collective-permute-start.1 = (f32[46,8,128]{2,1,0:T(8,128)S(1)}, f32[46,8,128]{2,1,0:T(8,128)S(1)}, u32[]{:S(2)}, u32[]{:S(2)}) collective-permute-start(f32[46,8,128]{2,1,0:T(8,128)S(1)} %get-tuple-element.26), channel_id=1, source_target_pairs={{0,4},{4,8},{8,12},{12,16},{16,20},{20,24},{24,28},{1,5},{5,9},{9,... | collective-permute-start | bytes 565256 | tf_op jit(solution)/shard_map/ppermute | solution.py:500
  38.4 0.0 copy-start
  38.4 1.4 %collective-permute-start.2 = (f32[46,8,128]{2,1,0:T(8,128)S(1)}, f32[46,8,128]{2,1,0:T(8,128)S(1)}, u32[]{:S(2)}, u32[]{:S(2)}) collective-permute-start(f32[46,8,128]{2,1,0:T(8,128)S(1)} %get-tuple-element.27), channel_id=1, source_target_pairs={{4,0},{8,4},{12,8},{16,12},{20,16},{24,20},{28,24},{5,1},{9,5},{13... | collective-permute-start | bytes 565256 | tf_op jit(solution)/shard_map/ppermute | solution.py:501
  39.9 0.0 copy-done.3
  39.9 0.4 prepare.1
  40.3 0.6 collective-permute-done.1.left
  40.9 4.6 %collective-permute-done.2.right = f32[46,8,128]{2,1,0:T(8,128)S(1)} collective-permute-done((f32[46,8,128]{2,1,0:T(8,128)S(1)}, f32[46,8,128]{2,1,0:T(8,128)S(1)}, u32[]{:S(2)}, u32[]{:S(2)}) %collective-permute-start.2) | collective-permute-done | bytes 188448 | tf_op jit(solution)/shard_map/ppermute | solution.py:501
  45.5 0.0 copy-done
  45.5 3.5 %sweeps.1 = f32[640,128]{1,0:T(8,128)S(1)} custom-call(f32[14,8,8,128]{3,2,1,0:T(8,128)S(1)} %get-tuple-element.22.own_s, f32[14,8,8,128]{3,2,1,0:T(8,128)S(1)} %get-tuple-element.23.own_a, f32[14,8,8,128]{3,2,1,0:T(8,128)S(1)} %get-tuple-element.24.own_b, f32[14,8,8,128]{3,2,1,0:T(8,128)S(1)} %get-tuple-element.25.own_x, ...), custom_call_target="tpu_custom_call" | custom-call | tf_op jit(solution)/shard_map/sweeps/pallas_call | solution.py:458
  49.0 16.7 %all_to_all.16.received = f32[16,5,8,128]{3,2,1,0:T(8,128)S(1)} all-to-all(f32[16,5,8,128]{3,2,1,0:T(8,128)S(1)} %bitcast.7), channel_id=1, replica_groups=mesh['tm'=16,'sx'=8,'sy'=4] {'tm'}, dimensions={0} | all-to-all | bytes 655360 | tf_op jit(solution)/shard_map/all_to_all | solution.py:517
  65.8 0.0 copy-start.1
  65.8 21.7 %all_to_all.17 = f32[32,8,128]{2,1,0:T(8,128)S(1)} all-to-all(f32[32,8,128]{2,1,0:T(8,128)S(1)} %gather.1), channel_id=1, replica_groups=mesh['tm'=16,'sx'=8,'sy'=4] {'sx','sy'}, dimensions={0} | all-to-all | bytes 262144 | tf_op jit(solution)/shard_map/all_to_all | solution.py:521
  87.5 0.0 copy-done.1
  87.5 1.8 %coarse.1 = f32[512,128]{1,0:T(8,128)} custom-call(f32[256,128]{1,0:T(8,128)S(1)} %bitcast.8, f32[16,5,8,128]{3,2,1,0:T(8,128)S(1)} %all_to_all.16.received, f32[8,128]{1,0:T(8,128)S(1)} %copy-done.3, f32[128,128]{1,0:T(8,128)S(1)} %copy-done.1), custom_call_target="tpu_custom_call" | custom-call | tf_op jit(solution)/shard_map/coarse/pallas_call | solution.py:458
  (2 shorter events, 0.1 us)
Async XLA Ops:
  1.2 25.1 %copy-start.2 = (bf16[2,128,128]{2,1,0:T(8,128)(2,1)S(1)}, bf16[2,128,128]{2,1,0:T(8,128)(2,1)}, u32[]{:S(2)}) copy-start(bf16[2,128,128]{2,1,0:T(8,128)(2,1)} %constant.8.clone.table) | copy-start | bytes 196612
  26.9 7.5 %collective-permute-start = (f32[25,8,128]{2,1,0:T(8,128)S(1)}, f32[25,8,128]{2,1,0:T(8,128)S(1)}, u32[]{:S(2)}, u32[]{:S(2)}) collective-permute-start(f32[25,8,128]{2,1,0:T(8,128)S(1)} %get-tuple-element.21), channel_id=1, source_target_pairs={{64,128},{192,256},{320,384},{448,480},{416,352},{288,224},{160,96... | collective-permute-start | bytes 307208 | tf_op jit(solution)/shard_map/ppermute | solution.py:494
  34.4 5.5 %copy-start.3 = (f32[8,128]{1,0:T(8,128)S(1)}, f32[8,128]{1,0:T(8,128)}, u32[]{:S(2)}) copy-start(f32[8,128]{1,0:T(8,128)} %constant.11.clone.lanes) | copy-start | bytes 12292
  34.4 6.5 %collective-permute-start.1 = (f32[46,8,128]{2,1,0:T(8,128)S(1)}, f32[46,8,128]{2,1,0:T(8,128)S(1)}, u32[]{:S(2)}, u32[]{:S(2)}) collective-permute-start(f32[46,8,128]{2,1,0:T(8,128)S(1)} %get-tuple-element.26), channel_id=1, source_target_pairs={{0,4},{4,8},{8,12},{12,16},{16,20},{20,24},{24,28},{1,5},{5,9},{9,... | collective-permute-start | bytes 565256 | tf_op jit(solution)/shard_map/ppermute | solution.py:500
  38.4 7.1 %copy-start = (bf16[2,160,128]{2,1,0:T(8,128)(2,1)S(1)}, bf16[2,160,128]{2,1,0:T(8,128)(2,1)}, u32[]{:S(2)}) copy-start(bf16[2,160,128]{2,1,0:T(8,128)(2,1)} %constant.9.clone.table) | copy-start | bytes 245764
  38.4 7.1 %collective-permute-start.2 = (f32[46,8,128]{2,1,0:T(8,128)S(1)}, f32[46,8,128]{2,1,0:T(8,128)S(1)}, u32[]{:S(2)}, u32[]{:S(2)}) collective-permute-start(f32[46,8,128]{2,1,0:T(8,128)S(1)} %get-tuple-element.27), channel_id=1, source_target_pairs={{4,0},{8,4},{12,8},{16,12},{20,16},{24,20},{28,24},{5,1},{9,5},{13... | collective-permute-start | bytes 565256 | tf_op jit(solution)/shard_map/ppermute | solution.py:501
  65.8 21.7 %copy-start.1 = (f32[128,128]{1,0:T(8,128)S(1)}, f32[128,128]{1,0:T(8,128)}, u32[]{:S(2)}) copy-start(f32[128,128]{1,0:T(8,128)} %constant.10.clone.table) | copy-start | bytes 196612

commit v8 on v7

--- a/solution.py
+++ b/solution.py
@@ -100,12 +100,14 @@
     )
 
 
+def x_major(rows):
+    return jnp.swapaxes(rows.reshape(8, 8, L), 0, 1).reshape(64, L)
+
+
 def pack_kernel(rates, field, regime, out, rate_rows, sums):
     margin = jnp.zeros((8, L), jnp.float32)
     for tp in range(4):
-        rows = [
-            field[pl.ds((2 * tp + t2) * 64 + x, 8, stride=8), :] for t2 in range(2) for x in range(8)
-        ]
+        rows = [x_major(field[64 * t : 64 * t + 64, :]) for t in (2 * tp, 2 * tp + 1)]
         turned = jnp.concatenate(rows, axis=0).T
         starts = (
             jnp.concatenate([turned, margin], axis=0),
@@ -114,15 +116,11 @@
         for d in range(TM):
             s = strip_of(d)
             out[d, ROWS * tp : ROWS * (tp + 1)] = starts[s % 2][8 * s : 8 * s + ROWS]
-    columns = []
-    for x in range(8):
-        kind = regime[pl.ds(x, 8, stride=8), :]
-        c = jnp.zeros((8, L), jnp.float32)
-        for r in range(8):
-            c = c + jnp.where(kind == r, rates[r], 0.0)
-        columns.append(c)
-    columns.append(jnp.zeros((64, L), jnp.float32))
-    c_turned = jnp.concatenate(columns, axis=0).T
+    kind = regime[...]
+    c = jnp.zeros((64, L), jnp.float32)
+    for r in range(8):
+        c = c + jnp.where(kind == r, rates[r], 0.0)
+    c_turned = jnp.concatenate([x_major(c), jnp.zeros((64, L), jnp.float32)], axis=0).T
     rate_rows[...] = jnp.concatenate([margin, c_turned, margin], axis=0)
     group = lane_index(1) // 32
     row = jnp.zeros((1, L), jnp.float32)
@@ -327,10 +325,11 @@
             faces.append(line)
     solved = x1[WY : WY + 8, lo:hi].reshape(512, L)
     result = dot(solved, table, ((1,), (1,)), table_first=True)
+    by_y = []
     for pair in range(4):
         cut = result[:, 128 * pair : 128 * pair + 128]
-        for j, value in enumerate(halves(cut[: TM * TILES], cut[TM * TILES :])):
-            out[pl.ds(2 * pair + j, TM * TILES, stride=8), :] = value
+        by_y += list(halves(cut[: TM * TILES], cut[TM * TILES :]))
+    out[...] = jnp.swapaxes(jnp.stack(by_y), 0, 1).reshape(TM * TILES * 8, L)
     homes = (
         strip >> 2,
         jnp.where(strip == 0, 4, (strip - 1) >> 2),
@@ -380,8 +379,10 @@
     index = lax.broadcasted_iota(jnp.int32, (8, L), 0)
     shift = jnp.broadcast_to(lanes[0:1, :] * float(VOLUME) + float(FACES), (8, L))
 
+    by_row = [jnp.swapaxes(gathered[:, sy], 0, 1) for sy in range(SY)]
+
     def rows_of(sy, row):
-        return gathered[pl.ds(sy * 8 + row, 8, stride=32), :]
+        return by_row[sy][row]
 
     def right(m):
         sy, g = m // 4, m % 4
@@ -441,10 +442,7 @@
         turned = jnp.concatenate(rows, axis=0).T
         for t2 in range(2):
             t = 2 * tp + t2
-            plus = jnp.broadcast_to(added[t : t + 1, :], (8, L))
-            for x in range(8):
-                r = t2 * 64 + x * 8
-                out[pl.ds(t * 64 + x, 8, stride=8), :] = turned[r : r + 8] + plus
+            out[64 * t : 64 * t + 64, :] = x_major(turned[64 * t2 : 64 * t2 + 64]) + added[t : t + 1, :]
 
 
 def call(kernel, name, out_shape, arrays, scratch=(), rates=None, keep=True, flops=0):
@@ -523,7 +521,7 @@
         coarse_kernel,
         "coarse",
         shape(512, L),
-        [gathered.reshape(256, L), returned, lanes, natural],
+        [gathered.reshape(SX, SY, 8, L), returned, lanes, natural],
         [pltpu.VMEM((L, L), jnp.float32)],
         keep=False,
     )

time: 89.7 us -> 89.7 us (level)
  no operation moved by 1% of the time
where the time goes in v8:
time: 89.7 us; the launch traced here: 89.3 us
  blocking collectives  63.5 us (71%)
  starting transfers between devices  9.49 us (11%)
  waiting for transfers between devices  8.63 us (10%)
  Pallas kernels  7.6 us (8%)
    all_to_all x1, blocking collectives, local(): lax.all_to_all(packed, 'tm', split_axis=0, concat_axis=0, tiled=True)  25 us
    all_to_all x1, blocking collectives, local(): lax.all_to_all(shared, ('sx', 'sy'), split_axis=0, concat_axis=0, tiled=T...  21.7 us
    all_to_all x1, blocking collectives, local(): lax.all_to_all(message.reshape(TM, TILES, 8, L), 'tm', split_axis=0, conc...  16.8 us
    pallas_call x7, Pallas kernels, call(): pl.pallas_call(kernel, name=name, out_shape=out_shape, in_specs=smem(len(...  7.6 us
    ppermute x1, waiting for transfers between devices, local(): right = lax.ppermute(to_left, 'sx', [(q, p) for p, q in across])  4.6 us
    ppermute x1, starting transfers between devices, local(): swapped = lax.ppermute(swap, ('tm', 'sy'), swaps())  4.05 us
    ppermute x1, starting transfers between devices, local(): left = lax.ppermute(to_right, 'sx', across)  4.01 us
    ppermute x1, waiting for transfers between devices, local(): swapped = lax.ppermute(swap, ('tm', 'sy'), swaps())  3.42 us
  transfers between devices with their start and end apart: 3, of which 3 were waited for; matrix products, arithmetic and copies ran while one was open for 0% of the time, Pallas kernels for 0%

profile of v8, /device:TPU:1, one launch (start us, length us, event | category | flops | bytes accessed | tf_op | source)
XLA Modules:
  0.0 89.3 jit_solution(16697247144931521584)
XLA Ops:
  0.0 1.2 %pack.1 = (f32[16,48,128]{2,1,0:T(8,128)S(1)}, f32[144,128]{1,0:T(8,128)S(1)}, f32[8,128]{1,0:T(8,128)S(1)}) custom-call(f32[8]{0:T(128)} %rates.1, f32[512,128]{1,0:T(8,128)} %bitcast.9, s32[64,128]{1,0:T(8,128)} %bitcast.10), custom_call_target="tpu_custom_call" | custom-call | tf_op jit(solution)/shard_map/pack/pallas_call | solution.py:456
  1.2 0.0 copy-start.2
  1.2 25.0 %all_to_all.15 = f32[16,48,128]{2,1,0:T(8,128)S(1)} all-to-all(f32[16,48,128]{2,1,0:T(8,128)S(1)} %get-tuple-element.17), channel_id=1, replica_groups=mesh['tm'=16,'sx'=8,'sy'=4] {'tm'}, dimensions={0} | all-to-all | bytes 786432 | tf_op jit(solution)/shard_map/all_to_all | solution.py:485
  26.3 0.0 copy-done.2
  26.3 0.6 transform.1
  26.9 4.1 %collective-permute-start = (f32[25,8,128]{2,1,0:T(8,128)S(1)}, f32[25,8,128]{2,1,0:T(8,128)S(1)}, u32[]{:S(2)}, u32[]{:S(2)}) collective-permute-start(f32[25,8,128]{2,1,0:T(8,128)S(1)} %get-tuple-element.21), channel_id=1, source_target_pairs={{64,128},{192,256},{320,384},{448,480},{416,352},{288,224},{160,96... | collective-permute-start | bytes 307208 | tf_op jit(solution)/shard_map/ppermute | solution.py:492
  31.0 3.4 %collective-permute-done.swapped = f32[25,8,128]{2,1,0:T(8,128)S(1)} collective-permute-done((f32[25,8,128]{2,1,0:T(8,128)S(1)}, f32[25,8,128]{2,1,0:T(8,128)S(1)}, u32[]{:S(2)}, u32[]{:S(2)}) %collective-permute-start) | collective-permute-done | bytes 102432 | tf_op jit(solution)/shard_map/ppermute | solution.py:492
  34.4 0.0 copy-start.3
  34.4 4.0 %collective-permute-start.1 = (f32[46,8,128]{2,1,0:T(8,128)S(1)}, f32[46,8,128]{2,1,0:T(8,128)S(1)}, u32[]{:S(2)}, u32[]{:S(2)}) collective-permute-start(f32[46,8,128]{2,1,0:T(8,128)S(1)} %get-tuple-element.26), channel_id=1, source_target_pairs={{0,4},{4,8},{8,12},{12,16},{16,20},{20,24},{24,28},{1,5},{5,9},{9,... | collective-permute-start | bytes 565256 | tf_op jit(solution)/shard_map/ppermute | solution.py:498
  38.4 0.0 copy-start
  38.4 1.4 %collective-permute-start.2 = (f32[46,8,128]{2,1,0:T(8,128)S(1)}, f32[46,8,128]{2,1,0:T(8,128)S(1)}, u32[]{:S(2)}, u32[]{:S(2)}) collective-permute-start(f32[46,8,128]{2,1,0:T(8,128)S(1)} %get-tuple-element.27), channel_id=1, source_target_pairs={{4,0},{8,4},{12,8},{16,12},{20,16},{24,20},{28,24},{5,1},{9,5},{13... | collective-permute-start | bytes 565256 | tf_op jit(solution)/shard_map/ppermute | solution.py:499
  39.9 0.0 copy-done.3
  39.9 0.4 prepare.1
  40.3 0.6 collective-permute-done.1.left
  40.9 4.6 %collective-permute-done.2.right = f32[46,8,128]{2,1,0:T(8,128)S(1)} collective-permute-done((f32[46,8,128]{2,1,0:T(8,128)S(1)}, f32[46,8,128]{2,1,0:T(8,128)S(1)}, u32[]{:S(2)}, u32[]{:S(2)}) %collective-permute-start.2) | collective-permute-done | bytes 188448 | tf_op jit(solution)/shard_map/ppermute | solution.py:499
  45.5 0.0 copy-done
  45.5 3.5 %sweeps.1 = f32[640,128]{1,0:T(8,128)S(1)} custom-call(f32[14,8,8,128]{3,2,1,0:T(8,128)S(1)} %get-tuple-element.22.own_s, f32[14,8,8,128]{3,2,1,0:T(8,128)S(1)} %get-tuple-element.23.own_a, f32[14,8,8,128]{3,2,1,0:T(8,128)S(1)} %get-tuple-element.24.own_b, f32[14,8,8,128]{3,2,1,0:T(8,128)S(1)} %get-tuple-element.25.own_x, ...), custom_call_target="tpu_custom_call" | custom-call | tf_op jit(solution)/shard_map/sweeps/pallas_call | solution.py:456
  49.0 16.8 %all_to_all.16.received = f32[16,5,8,128]{3,2,1,0:T(8,128)S(1)} all-to-all(f32[16,5,8,128]{3,2,1,0:T(8,128)S(1)} %bitcast.7), channel_id=1, replica_groups=mesh['tm'=16,'sx'=8,'sy'=4] {'tm'}, dimensions={0} | all-to-all | bytes 655360 | tf_op jit(solution)/shard_map/all_to_all | solution.py:515
  65.8 0.0 copy-start.1
  65.8 21.7 %all_to_all.17 = f32[32,8,128]{2,1,0:T(8,128)S(1)} all-to-all(f32[32,8,128]{2,1,0:T(8,128)S(1)} %gather.1), channel_id=1, replica_groups=mesh['tm'=16,'sx'=8,'sy'=4] {'sx','sy'}, dimensions={0} | all-to-all | bytes 262144 | tf_op jit(solution)/shard_map/all_to_all | solution.py:519
  87.5 0.0 copy-done.1
  87.5 1.8 %coarse.1 = f32[512,128]{1,0:T(8,128)} custom-call(f32[8,4,8,128]{3,2,1,0:T(8,128)S(1)} %bitcast.8, f32[16,5,8,128]{3,2,1,0:T(8,128)S(1)} %all_to_all.16.received, f32[8,128]{1,0:T(8,128)S(1)} %copy-done.3, f32[128,128]{1,0:T(8,128)S(1)} %copy-done.1), custom_call_target="tpu_custom_call" | custom-call | tf_op jit(solution)/shard_map/coarse/pallas_call | solution.py:456
  (2 shorter events, 0.1 us)
Async XLA Ops:
  1.2 25.1 %copy-start.2 = (bf16[2,128,128]{2,1,0:T(8,128)(2,1)S(1)}, bf16[2,128,128]{2,1,0:T(8,128)(2,1)}, u32[]{:S(2)}) copy-start(bf16[2,128,128]{2,1,0:T(8,128)(2,1)} %constant.8.clone.table) | copy-start | bytes 196612
  26.9 7.5 %collective-permute-start = (f32[25,8,128]{2,1,0:T(8,128)S(1)}, f32[25,8,128]{2,1,0:T(8,128)S(1)}, u32[]{:S(2)}, u32[]{:S(2)}) collective-permute-start(f32[25,8,128]{2,1,0:T(8,128)S(1)} %get-tuple-element.21), channel_id=1, source_target_pairs={{64,128},{192,256},{320,384},{448,480},{416,352},{288,224},{160,96... | collective-permute-start | bytes 307208 | tf_op jit(solution)/shard_map/ppermute | solution.py:492
  34.4 5.5 %copy-start.3 = (f32[8,128]{1,0:T(8,128)S(1)}, f32[8,128]{1,0:T(8,128)}, u32[]{:S(2)}) copy-start(f32[8,128]{1,0:T(8,128)} %constant.11.clone.lanes) | copy-start | bytes 12292
  34.4 6.5 %collective-permute-start.1 = (f32[46,8,128]{2,1,0:T(8,128)S(1)}, f32[46,8,128]{2,1,0:T(8,128)S(1)}, u32[]{:S(2)}, u32[]{:S(2)}) collective-permute-start(f32[46,8,128]{2,1,0:T(8,128)S(1)} %get-tuple-element.26), channel_id=1, source_target_pairs={{0,4},{4,8},{8,12},{12,16},{16,20},{20,24},{24,28},{1,5},{5,9},{9,... | collective-permute-start | bytes 565256 | tf_op jit(solution)/shard_map/ppermute | solution.py:498
  38.4 7.1 %copy-start = (bf16[2,160,128]{2,1,0:T(8,128)(2,1)S(1)}, bf16[2,160,128]{2,1,0:T(8,128)(2,1)}, u32[]{:S(2)}) copy-start(bf16[2,160,128]{2,1,0:T(8,128)(2,1)} %constant.9.clone.table) | copy-start | bytes 245764
  38.4 7.1 %collective-permute-start.2 = (f32[46,8,128]{2,1,0:T(8,128)S(1)}, f32[46,8,128]{2,1,0:T(8,128)S(1)}, u32[]{:S(2)}, u32[]{:S(2)}) collective-permute-start(f32[46,8,128]{2,1,0:T(8,128)S(1)} %get-tuple-element.27), channel_id=1, source_target_pairs={{4,0},{8,4},{12,8},{16,12},{20,16},{24,20},{28,24},{5,1},{9,5},{13... | collective-permute-start | bytes 565256 | tf_op jit(solution)/shard_map/ppermute | solution.py:499
  65.8 21.7 %copy-start.1 = (f32[128,128]{1,0:T(8,128)S(1)}, f32[128,128]{1,0:T(8,128)}, u32[]{:S(2)}) copy-start(f32[128,128]{1,0:T(8,128)} %constant.10.clone.table) | copy-start | bytes 196612

commit v9 on v8

--- a/solution.py
+++ b/solution.py
@@ -293,16 +293,16 @@
         return lambda y, x: ref[y, x]
 
     def sweep(old, new, margin):
-        def row(y, carry):
+        for y in range(margin, SPAN_Y - margin):
             for x in range(margin, SPAN_X - margin):
+                distance = max(WX - x, x - WX - 7, 1)
+                if not distance - 1 + margin <= y < SPAN_Y + 1 - margin - distance:
+                    continue
                 v = old(y, x)
                 u = source(y, x) + (old(y, x + 1) + old(y, x - 1))
                 u = u + (old(y + 1, x) + old(y - 1, x))
                 u = u + (pltpu.roll(v, 1, 0) + pltpu.roll(v, 7, 0))
                 new[y, x] = a(y, x) * u + b(y, x) * pltpu.roll(u, 64, 1)
-            return carry
-
-        lax.fori_loop(margin, SPAN_Y - margin, row, 0)
 
     sweep(split(own_x, hx), x1, 1)
     sweep(whole(x1), x0, 2)

time: 89.7 us -> 87.5 us (0.975)
  Pallas kernels: 7.6 us -> 5.4 us
    pallas_call x7, Pallas kernels: 7.6 us -> 5.4 us  [call(): pl.pallas_call(kernel, name=name, out_shape=out_shape, in_specs=smem(len(...]
where the time goes in v9:
time: 87.5 us; the launch traced here: 87.1 us
  blocking collectives  63.5 us (73%)
  starting transfers between devices  9.49 us (11%)
  waiting for transfers between devices  8.63 us (10%)
  Pallas kernels  5.4 us (6%)
    all_to_all x1, blocking collectives, local(): lax.all_to_all(packed, 'tm', split_axis=0, concat_axis=0, tiled=True)  25 us
    all_to_all x1, blocking collectives, local(): lax.all_to_all(shared, ('sx', 'sy'), split_axis=0, concat_axis=0, tiled=T...  21.7 us
    all_to_all x1, blocking collectives, local(): lax.all_to_all(message.reshape(TM, TILES, 8, L), 'tm', split_axis=0, conc...  16.7 us
    pallas_call x7, Pallas kernels, call(): pl.pallas_call(kernel, name=name, out_shape=out_shape, in_specs=smem(len(...  5.4 us
    ppermute x1, waiting for transfers between devices, local(): right = lax.ppermute(to_left, 'sx', [(q, p) for p, q in across])  4.6 us
    ppermute x1, starting transfers between devices, local(): swapped = lax.ppermute(swap, ('tm', 'sy'), swaps())  4.05 us
    ppermute x1, starting transfers between devices, local(): left = lax.ppermute(to_right, 'sx', across)  4.01 us
    ppermute x1, waiting for transfers between devices, local(): swapped = lax.ppermute(swap, ('tm', 'sy'), swaps())  3.42 us
  transfers between devices with their start and end apart: 3, of which 3 were waited for; matrix products, arithmetic and copies ran while one was open for 0% of the time, Pallas kernels for 0%

profile of v9, /device:TPU:1, one launch (start us, length us, event | category | flops | bytes accessed | tf_op | source)
XLA Modules:
  0.0 87.1 jit_solution(7466951221154381942)
XLA Ops:
  0.0 1.2 %pack.1 = (f32[16,48,128]{2,1,0:T(8,128)S(1)}, f32[144,128]{1,0:T(8,128)S(1)}, f32[8,128]{1,0:T(8,128)S(1)}) custom-call(f32[8]{0:T(128)} %rates.1, f32[512,128]{1,0:T(8,128)} %bitcast.9, s32[64,128]{1,0:T(8,128)} %bitcast.10), custom_call_target="tpu_custom_call" | custom-call | tf_op jit(solution)/shard_map/pack/pallas_call | solution.py:456
  1.2 0.0 copy-start.2
  1.2 25.0 %all_to_all.15 = f32[16,48,128]{2,1,0:T(8,128)S(1)} all-to-all(f32[16,48,128]{2,1,0:T(8,128)S(1)} %get-tuple-element.17), channel_id=1, replica_groups=mesh['tm'=16,'sx'=8,'sy'=4] {'tm'}, dimensions={0} | all-to-all | bytes 786432 | tf_op jit(solution)/shard_map/all_to_all | solution.py:485
  26.3 0.0 copy-done.2
  26.3 0.6 transform.1
  26.9 4.1 %collective-permute-start = (f32[25,8,128]{2,1,0:T(8,128)S(1)}, f32[25,8,128]{2,1,0:T(8,128)S(1)}, u32[]{:S(2)}, u32[]{:S(2)}) collective-permute-start(f32[25,8,128]{2,1,0:T(8,128)S(1)} %get-tuple-element.21), channel_id=1, source_target_pairs={{64,128},{192,256},{320,384},{448,480},{416,352},{288,224},{160,96... | collective-permute-start | bytes 307208 | tf_op jit(solution)/shard_map/ppermute | solution.py:492
  31.0 3.4 %collective-permute-done.swapped = f32[25,8,128]{2,1,0:T(8,128)S(1)} collective-permute-done((f32[25,8,128]{2,1,0:T(8,128)S(1)}, f32[25,8,128]{2,1,0:T(8,128)S(1)}, u32[]{:S(2)}, u32[]{:S(2)}) %collective-permute-start) | collective-permute-done | bytes 102432 | tf_op jit(solution)/shard_map/ppermute | solution.py:492
  34.4 0.0 copy-start.3
  34.4 4.0 %collective-permute-start.1 = (f32[46,8,128]{2,1,0:T(8,128)S(1)}, f32[46,8,128]{2,1,0:T(8,128)S(1)}, u32[]{:S(2)}, u32[]{:S(2)}) collective-permute-start(f32[46,8,128]{2,1,0:T(8,128)S(1)} %get-tuple-element.26), channel_id=1, source_target_pairs={{0,4},{4,8},{8,12},{12,16},{16,20},{20,24},{24,28},{1,5},{5,9},{9,... | collective-permute-start | bytes 565256 | tf_op jit(solution)/shard_map/ppermute | solution.py:498
  38.4 0.0 copy-start
  38.4 1.4 %collective-permute-start.2 = (f32[46,8,128]{2,1,0:T(8,128)S(1)}, f32[46,8,128]{2,1,0:T(8,128)S(1)}, u32[]{:S(2)}, u32[]{:S(2)}) collective-permute-start(f32[46,8,128]{2,1,0:T(8,128)S(1)} %get-tuple-element.27), channel_id=1, source_target_pairs={{4,0},{8,4},{12,8},{16,12},{20,16},{24,20},{28,24},{5,1},{9,5},{13... | collective-permute-start | bytes 565256 | tf_op jit(solution)/shard_map/ppermute | solution.py:499
  39.9 0.0 copy-done.3
  39.9 0.4 prepare.1
  40.3 0.6 collective-permute-done.1.left
  40.9 4.6 %collective-permute-done.2.right = f32[46,8,128]{2,1,0:T(8,128)S(1)} collective-permute-done((f32[46,8,128]{2,1,0:T(8,128)S(1)}, f32[46,8,128]{2,1,0:T(8,128)S(1)}, u32[]{:S(2)}, u32[]{:S(2)}) %collective-permute-start.2) | collective-permute-done | bytes 188448 | tf_op jit(solution)/shard_map/ppermute | solution.py:499
  45.5 0.0 copy-done
  45.5 1.3 %sweeps.1 = f32[640,128]{1,0:T(8,128)S(1)} custom-call(f32[14,8,8,128]{3,2,1,0:T(8,128)S(1)} %get-tuple-element.22.own_s, f32[14,8,8,128]{3,2,1,0:T(8,128)S(1)} %get-tuple-element.23.own_a, f32[14,8,8,128]{3,2,1,0:T(8,128)S(1)} %get-tuple-element.24.own_b, f32[14,8,8,128]{3,2,1,0:T(8,128)S(1)} %get-tuple-element.25.own_x, ...), custom_call_target="tpu_custom_call" | custom-call | tf_op jit(solution)/shard_map/sweeps/pallas_call | solution.py:456
  46.8 16.7 %all_to_all.16.received = f32[16,5,8,128]{3,2,1,0:T(8,128)S(1)} all-to-all(f32[16,5,8,128]{3,2,1,0:T(8,128)S(1)} %bitcast.7), channel_id=1, replica_groups=mesh['tm'=16,'sx'=8,'sy'=4] {'tm'}, dimensions={0} | all-to-all | bytes 655360 | tf_op jit(solution)/shard_map/all_to_all | solution.py:515
  63.6 0.0 copy-start.1
  63.6 21.7 %all_to_all.17 = f32[32,8,128]{2,1,0:T(8,128)S(1)} all-to-all(f32[32,8,128]{2,1,0:T(8,128)S(1)} %gather.1), channel_id=1, replica_groups=mesh['tm'=16,'sx'=8,'sy'=4] {'sx','sy'}, dimensions={0} | all-to-all | bytes 262144 | tf_op jit(solution)/shard_map/all_to_all | solution.py:519
  85.3 0.0 copy-done.1
  85.3 1.8 %coarse.1 = f32[512,128]{1,0:T(8,128)} custom-call(f32[8,4,8,128]{3,2,1,0:T(8,128)S(1)} %bitcast.8, f32[16,5,8,128]{3,2,1,0:T(8,128)S(1)} %all_to_all.16.received, f32[8,128]{1,0:T(8,128)S(1)} %copy-done.3, f32[128,128]{1,0:T(8,128)S(1)} %copy-done.1), custom_call_target="tpu_custom_call" | custom-call | tf_op jit(solution)/shard_map/coarse/pallas_call | solution.py:456
  (2 shorter events, 0.1 us)
Async XLA Ops:
  1.2 25.1 %copy-start.2 = (bf16[2,128,128]{2,1,0:T(8,128)(2,1)S(1)}, bf16[2,128,128]{2,1,0:T(8,128)(2,1)}, u32[]{:S(2)}) copy-start(bf16[2,128,128]{2,1,0:T(8,128)(2,1)} %constant.8.clone.table) | copy-start | bytes 196612
  26.9 7.5 %collective-permute-start = (f32[25,8,128]{2,1,0:T(8,128)S(1)}, f32[25,8,128]{2,1,0:T(8,128)S(1)}, u32[]{:S(2)}, u32[]{:S(2)}) collective-permute-start(f32[25,8,128]{2,1,0:T(8,128)S(1)} %get-tuple-element.21), channel_id=1, source_target_pairs={{64,128},{192,256},{320,384},{448,480},{416,352},{288,224},{160,96... | collective-permute-start | bytes 307208 | tf_op jit(solution)/shard_map/ppermute | solution.py:492
  34.4 5.5 %copy-start.3 = (f32[8,128]{1,0:T(8,128)S(1)}, f32[8,128]{1,0:T(8,128)}, u32[]{:S(2)}) copy-start(f32[8,128]{1,0:T(8,128)} %constant.11.clone.lanes) | copy-start | bytes 12292
  34.4 6.5 %collective-permute-start.1 = (f32[46,8,128]{2,1,0:T(8,128)S(1)}, f32[46,8,128]{2,1,0:T(8,128)S(1)}, u32[]{:S(2)}, u32[]{:S(2)}) collective-permute-start(f32[46,8,128]{2,1,0:T(8,128)S(1)} %get-tuple-element.26), channel_id=1, source_target_pairs={{0,4},{4,8},{8,12},{12,16},{16,20},{20,24},{24,28},{1,5},{5,9},{9,... | collective-permute-start | bytes 565256 | tf_op jit(solution)/shard_map/ppermute | solution.py:498
  38.4 7.1 %copy-start = (bf16[2,160,128]{2,1,0:T(8,128)(2,1)S(1)}, bf16[2,160,128]{2,1,0:T(8,128)(2,1)}, u32[]{:S(2)}) copy-start(bf16[2,160,128]{2,1,0:T(8,128)(2,1)} %constant.9.clone.table) | copy-start | bytes 245764
  38.4 7.1 %collective-permute-start.2 = (f32[46,8,128]{2,1,0:T(8,128)S(1)}, f32[46,8,128]{2,1,0:T(8,128)S(1)}, u32[]{:S(2)}, u32[]{:S(2)}) collective-permute-start(f32[46,8,128]{2,1,0:T(8,128)S(1)} %get-tuple-element.27), channel_id=1, source_target_pairs={{4,0},{8,4},{12,8},{16,12},{20,16},{24,20},{28,24},{5,1},{9,5},{13... | collective-permute-start | bytes 565256 | tf_op jit(solution)/shard_map/ppermute | solution.py:499
  63.6 21.7 %copy-start.1 = (f32[128,128]{1,0:T(8,128)S(1)}, f32[128,128]{1,0:T(8,128)}, u32[]{:S(2)}) copy-start(f32[128,128]{1,0:T(8,128)} %constant.10.clone.table) | copy-start | bytes 196612

commit v10 on v9

--- a/solution.py
+++ b/solution.py
@@ -24,7 +24,9 @@
 
 
 def strip_of(d):
-    return d // 2 if d % 2 == 0 else TM - 1 - d // 2
+    if d % 2 == 1:
+        return 7 + d // 2
+    return {0: 0, 2: TM - 1}.get(d, d // 2 - 1)
 
 
 MEMBER = {strip_of(d): d for d in range(TM)}
@@ -132,7 +134,9 @@
 
 def own_strip():
     tm = lax.axis_index("tm")
-    return jnp.where(tm & 1 == 0, tm >> 1, TM - 1 - (tm >> 1))
+    ends = jnp.where(tm == 0, 0, TM - 1)
+    even = jnp.where(tm <= 2, ends, (tm >> 1) - 1)
+    return jnp.where(tm & 1 == 1, 7 + (tm >> 1), even)
 
 
 def transform_kernel(received, rate_rows, table, window, rate, swap):

time: 87.5 us -> 87.5 us (level)
  waiting for transfers between devices: 8.63 us -> 7.7 us
  blocking collectives: 63.5 us -> 64.4 us
    all_to_all x1, blocking collectives: 16.7 us -> 19.4 us  [local(): lax.all_to_all(message.reshape(TM, TILES, 8, L), 'tm', split_axis=0, conc...]
    all_to_all x1, blocking collectives: 21.7 us -> 20 us  [local(): lax.all_to_all(shared, ('sx', 'sy'), split_axis=0, concat_axis=0, tiled=T...]
    ppermute x1, waiting for transfers between devices: 3.42 us -> 2.51 us  [local(): swapped = lax.ppermute(swap, ('tm', 'sy'), swaps())]
  transfers between devices with their start and end apart: 3 -> 3, of which waited for: 3 -> 3; matrix products, arithmetic and copies ran while one was open for 0% -> 0% of each run, Pallas kernels for 0% -> 1%
where the time goes in v10:
time: 87.5 us; the launch traced here: 87.1 us
  blocking collectives  64.4 us (74%)
  starting transfers between devices  9.49 us (11%)
  waiting for transfers between devices  7.7 us (9%)
  Pallas kernels  5.4 us (6%)
    all_to_all x1, blocking collectives, local(): lax.all_to_all(packed, 'tm', split_axis=0, concat_axis=0, tiled=True)  25 us
    all_to_all x1, blocking collectives, local(): lax.all_to_all(shared, ('sx', 'sy'), split_axis=0, concat_axis=0, tiled=T...  20 us
    all_to_all x1, blocking collectives, local(): lax.all_to_all(message.reshape(TM, TILES, 8, L), 'tm', split_axis=0, conc...  19.4 us
    pallas_call x7, Pallas kernels, call(): pl.pallas_call(kernel, name=name, out_shape=out_shape, in_specs=smem(len(...  5.4 us
    ppermute x1, waiting for transfers between devices, local(): right = lax.ppermute(to_left, 'sx', [(q, p) for p, q in across])  4.6 us
    ppermute x1, starting transfers between devices, local(): swapped = lax.ppermute(swap, ('tm', 'sy'), swaps())  4.05 us
    ppermute x1, starting transfers between devices, local(): left = lax.ppermute(to_right, 'sx', across)  4.01 us
    ppermute x1, waiting for transfers between devices, local(): swapped = lax.ppermute(swap, ('tm', 'sy'), swaps())  2.51 us
  transfers between devices with their start and end apart: 3, of which 3 were waited for; matrix products, arithmetic and copies ran while one was open for 0% of the time, Pallas kernels for 1%

profile of v10, /device:TPU:1, one launch (start us, length us, event | category | flops | bytes accessed | tf_op | source)
XLA Modules:
  0.0 87.1 jit_solution(17584909183122477587)
XLA Ops:
  0.0 1.2 %pack.1 = (f32[16,48,128]{2,1,0:T(8,128)S(1)}, f32[144,128]{1,0:T(8,128)S(1)}, f32[8,128]{1,0:T(8,128)S(1)}) custom-call(f32[8]{0:T(128)} %rates.1, f32[512,128]{1,0:T(8,128)} %bitcast.9, s32[64,128]{1,0:T(8,128)} %bitcast.10), custom_call_target="tpu_custom_call" | custom-call | tf_op jit(solution)/shard_map/pack/pallas_call | solution.py:460
  1.2 0.0 copy-start.2
  1.2 25.0 %all_to_all.15 = f32[16,48,128]{2,1,0:T(8,128)S(1)} all-to-all(f32[16,48,128]{2,1,0:T(8,128)S(1)} %get-tuple-element.17), channel_id=1, replica_groups=mesh['tm'=16,'sx'=8,'sy'=4] {'tm'}, dimensions={0} | all-to-all | bytes 786432 | tf_op jit(solution)/shard_map/all_to_all | solution.py:489
  26.3 0.0 copy-done.2
  26.3 0.6 transform.1
  26.9 4.1 %collective-permute-start = (f32[25,8,128]{2,1,0:T(8,128)S(1)}, f32[25,8,128]{2,1,0:T(8,128)S(1)}, u32[]{:S(2)}, u32[]{:S(2)}) collective-permute-start(f32[25,8,128]{2,1,0:T(8,128)S(1)} %get-tuple-element.21), channel_id=1, source_target_pairs={{128,192},{256,320},{384,448},{32,96},{160,224},{288,352},{416,480... | collective-permute-start | bytes 307208 | tf_op jit(solution)/shard_map/ppermute | solution.py:496
  31.0 2.5 %collective-permute-done.swapped = f32[25,8,128]{2,1,0:T(8,128)S(1)} collective-permute-done((f32[25,8,128]{2,1,0:T(8,128)S(1)}, f32[25,8,128]{2,1,0:T(8,128)S(1)}, u32[]{:S(2)}, u32[]{:S(2)}) %collective-permute-start) | collective-permute-done | bytes 102432 | tf_op jit(solution)/shard_map/ppermute | solution.py:496
  33.5 0.0 copy-start.3
  33.5 4.0 %collective-permute-start.1 = (f32[46,8,128]{2,1,0:T(8,128)S(1)}, f32[46,8,128]{2,1,0:T(8,128)S(1)}, u32[]{:S(2)}, u32[]{:S(2)}) collective-permute-start(f32[46,8,128]{2,1,0:T(8,128)S(1)} %get-tuple-element.26), channel_id=1, source_target_pairs={{0,4},{4,8},{8,12},{12,16},{16,20},{20,24},{24,28},{1,5},{5,9},{9,... | collective-permute-start | bytes 565256 | tf_op jit(solution)/shard_map/ppermute | solution.py:502
  37.5 0.0 copy-start
  37.5 1.4 %collective-permute-start.2 = (f32[46,8,128]{2,1,0:T(8,128)S(1)}, f32[46,8,128]{2,1,0:T(8,128)S(1)}, u32[]{:S(2)}, u32[]{:S(2)}) collective-permute-start(f32[46,8,128]{2,1,0:T(8,128)S(1)} %get-tuple-element.27), channel_id=1, source_target_pairs={{4,0},{8,4},{12,8},{16,12},{20,16},{24,20},{28,24},{5,1},{9,5},{13... | collective-permute-start | bytes 565256 | tf_op jit(solution)/shard_map/ppermute | solution.py:503
  39.0 0.0 copy-done.3
  39.0 0.4 prepare.1
  39.4 0.6 collective-permute-done.1.left
  40.0 4.6 %collective-permute-done.2.right = f32[46,8,128]{2,1,0:T(8,128)S(1)} collective-permute-done((f32[46,8,128]{2,1,0:T(8,128)S(1)}, f32[46,8,128]{2,1,0:T(8,128)S(1)}, u32[]{:S(2)}, u32[]{:S(2)}) %collective-permute-start.2) | collective-permute-done | bytes 188448 | tf_op jit(solution)/shard_map/ppermute | solution.py:503
  44.6 0.0 copy-done
  44.6 1.3 %sweeps.1 = f32[640,128]{1,0:T(8,128)S(1)} custom-call(f32[14,8,8,128]{3,2,1,0:T(8,128)S(1)} %get-tuple-element.22.own_s, f32[14,8,8,128]{3,2,1,0:T(8,128)S(1)} %get-tuple-element.23.own_a, f32[14,8,8,128]{3,2,1,0:T(8,128)S(1)} %get-tuple-element.24.own_b, f32[14,8,8,128]{3,2,1,0:T(8,128)S(1)} %get-tuple-element.25.own_x, ...), custom_call_target="tpu_custom_call" | custom-call | tf_op jit(solution)/shard_map/sweeps/pallas_call | solution.py:460
  45.9 19.4 %all_to_all.16.received = f32[16,5,8,128]{3,2,1,0:T(8,128)S(1)} all-to-all(f32[16,5,8,128]{3,2,1,0:T(8,128)S(1)} %bitcast.7), channel_id=1, replica_groups=mesh['tm'=16,'sx'=8,'sy'=4] {'tm'}, dimensions={0} | all-to-all | bytes 655360 | tf_op jit(solution)/shard_map/all_to_all | solution.py:519
  65.3 0.0 copy-start.1
  65.3 20.0 %all_to_all.17 = f32[32,8,128]{2,1,0:T(8,128)S(1)} all-to-all(f32[32,8,128]{2,1,0:T(8,128)S(1)} %gather.1), channel_id=1, replica_groups=mesh['tm'=16,'sx'=8,'sy'=4] {'sx','sy'}, dimensions={0} | all-to-all | bytes 262144 | tf_op jit(solution)/shard_map/all_to_all | solution.py:523
  85.3 0.0 copy-done.1
  85.3 1.8 %coarse.1 = f32[512,128]{1,0:T(8,128)} custom-call(f32[8,4,8,128]{3,2,1,0:T(8,128)S(1)} %bitcast.8, f32[16,5,8,128]{3,2,1,0:T(8,128)S(1)} %all_to_all.16.received, f32[8,128]{1,0:T(8,128)S(1)} %copy-done.3, f32[128,128]{1,0:T(8,128)S(1)} %copy-done.1), custom_call_target="tpu_custom_call" | custom-call | tf_op jit(solution)/shard_map/coarse/pallas_call | solution.py:460
  (2 shorter events, 0.1 us)
Async XLA Ops:
  1.2 25.1 %copy-start.2 = (bf16[2,128,128]{2,1,0:T(8,128)(2,1)S(1)}, bf16[2,128,128]{2,1,0:T(8,128)(2,1)}, u32[]{:S(2)}) copy-start(bf16[2,128,128]{2,1,0:T(8,128)(2,1)} %constant.8.clone.table) | copy-start | bytes 196612
  26.9 6.6 %collective-permute-start = (f32[25,8,128]{2,1,0:T(8,128)S(1)}, f32[25,8,128]{2,1,0:T(8,128)S(1)}, u32[]{:S(2)}, u32[]{:S(2)}) collective-permute-start(f32[25,8,128]{2,1,0:T(8,128)S(1)} %get-tuple-element.21), channel_id=1, source_target_pairs={{128,192},{256,320},{384,448},{32,96},{160,224},{288,352},{416,480... | collective-permute-start | bytes 307208 | tf_op jit(solution)/shard_map/ppermute | solution.py:496
  33.5 5.5 %copy-start.3 = (f32[8,128]{1,0:T(8,128)S(1)}, f32[8,128]{1,0:T(8,128)}, u32[]{:S(2)}) copy-start(f32[8,128]{1,0:T(8,128)} %constant.11.clone.lanes) | copy-start | bytes 12292
  33.5 6.5 %collective-permute-start.1 = (f32[46,8,128]{2,1,0:T(8,128)S(1)}, f32[46,8,128]{2,1,0:T(8,128)S(1)}, u32[]{:S(2)}, u32[]{:S(2)}) collective-permute-start(f32[46,8,128]{2,1,0:T(8,128)S(1)} %get-tuple-element.26), channel_id=1, source_target_pairs={{0,4},{4,8},{8,12},{12,16},{16,20},{20,24},{24,28},{1,5},{5,9},{9,... | collective-permute-start | bytes 565256 | tf_op jit(solution)/shard_map/ppermute | solution.py:502
  37.5 7.1 %copy-start = (bf16[2,160,128]{2,1,0:T(8,128)(2,1)S(1)}, bf16[2,160,128]{2,1,0:T(8,128)(2,1)}, u32[]{:S(2)}) copy-start(bf16[2,160,128]{2,1,0:T(8,128)(2,1)} %constant.9.clone.table) | copy-start | bytes 245764
  37.5 7.1 %collective-permute-start.2 = (f32[46,8,128]{2,1,0:T(8,128)S(1)}, f32[46,8,128]{2,1,0:T(8,128)S(1)}, u32[]{:S(2)}, u32[]{:S(2)}) collective-permute-start(f32[46,8,128]{2,1,0:T(8,128)S(1)} %get-tuple-element.27), channel_id=1, source_target_pairs={{4,0},{8,4},{12,8},{16,12},{20,16},{24,20},{28,24},{5,1},{9,5},{13... | collective-permute-start | bytes 565256 | tf_op jit(solution)/shard_map/ppermute | solution.py:503
  65.3 20.0 %copy-start.1 = (f32[128,128]{1,0:T(8,128)S(1)}, f32[128,128]{1,0:T(8,128)}, u32[]{:S(2)}) copy-start(f32[128,128]{1,0:T(8,128)} %constant.10.clone.table) | copy-start | bytes 196612

commit v11 on v9

--- a/solution.py
+++ b/solution.py
@@ -135,28 +135,40 @@
     return jnp.where(tm & 1 == 0, tm >> 1, TM - 1 - (tm >> 1))
 
 
-def transform_kernel(received, rate_rows, table, window, rate, swap):
+def spectra(received, table, starts):
     rows = []
-    for pair in range(ROWS // 2):
-        both = [received[pl.ds(2 * pair + j, 64, stride=ROWS), :] for j in range(2)]
+    for first, second in zip(starts[::2], starts[1::2]):
+        both = [received[pl.ds(start, 64, stride=ROWS), :] for start in (first, second)]
         turned = jnp.concatenate(both, axis=0).T
         rows += list(halves(turned[:64], turned[64:]))
-    spectrum = dot(jnp.concatenate(rows[: 8 + WY], axis=0), table, ((1,), (0,)))
-    strip = own_strip()
-    even = strip & 1 == 0
+    return dot(jnp.concatenate(rows, axis=0), table, ((1,), (0,)))
+
+
+def window_rates(rate_rows):
+    near = rate_rows[pl.ds(pl.multiple_of(own_strip() * 8, 8), 24), :]
+    return jnp.concatenate([near[8 - WY : 16 + WY], jnp.zeros((2, L), jnp.float32)], axis=0)
+
+
+def swap_kernel(received, rate_rows, table, swap):
+    even = own_strip() & 1 == 0
+    start = jnp.where(even, 0, 8)
+    spectrum = spectra(received, table, [start, start + 1, start + 2, start + 2])
+    for i in range(8 * WY):
+        swap[i] = spectrum[8 * i : 8 * i + 8]
+    mine = window_rates(rate_rows)
+    swap[PART - 1] = jnp.where(even, pltpu.roll(mine[0:8], 8 - WY, 0), mine[8:16])
+
+
+def transform_kernel(received, rate_rows, table, window, rate):
+    spectrum = spectra(received, table, range(ROWS))
     zero = jnp.zeros((8, L), jnp.float32)
     for i in range(8 * WY):
         window[i] = zero
         window[8 * (WY + 8) + i] = zero
-    offset = jnp.where(even, 8 * WY, 0)
+    offset = jnp.where(own_strip() & 1 == 0, 8 * WY, 0)
     for i in range(8 * (8 + WY)):
         window[offset + i] = spectrum[8 * i : 8 * i + 8]
-    near = rate_rows[pl.ds(pl.multiple_of(strip * 8, 8), 24), :]
-    mine = jnp.concatenate([near[8 - WY : 16 + WY], jnp.zeros((2, L), jnp.float32)], axis=0)
-    rate[...] = mine
-    for i in range(8 * WY):
-        swap[i] = jnp.where(even, window[8 * WY + i], window[64 + i])
-    swap[PART - 1] = jnp.where(even, pltpu.roll(mine[0:8], 8 - WY, 0), mine[8:16])
+    rate[...] = window_rates(rate_rows)
 
 
 def x_range(distance):
@@ -483,13 +495,12 @@
         rates=reaction_rates,
     )
     received = lax.all_to_all(packed, "tm", split_axis=0, concat_axis=0, tiled=True)
-    window, rate, swap = call(
-        transform_kernel,
-        "transform",
-        (shape(8 * SPAN_Y, 8, L), shape(16, L), shape(PART, 8, L)),
-        [received.reshape(TM * 4 * ROWS, L), rate_rows, forward],
-    )
+    arrays = [received.reshape(TM * 4 * ROWS, L), rate_rows, forward]
+    swap = call(swap_kernel, "swap_rows", shape(PART, 8, L), arrays)
     swapped = lax.ppermute(swap, ("tm", "sy"), swaps())
+    window, rate = call(
+        transform_kernel, "transform", (shape(8 * SPAN_Y, 8, L), shape(16, L)), arrays, flops=10**7
+    )
     tiles = len(EDGE) + 2
     to_left, to_right = call(
         edge_kernel, "edges", (shape(tiles, 8, L),) * 2, [window, rate, swapped]

time: 87.5 us -> 87.2 us (level)
    pallas_call x7 -> x8, Pallas kernels: 5.4 us -> 5.75 us  [call(): pl.pallas_call(kernel, name=name, out_shape=out_shape, in_specs=smem(len(...]
  transfers between devices with their start and end apart: 3 -> 3, of which waited for: 3 -> 3; matrix products, arithmetic and copies ran while one was open for 0% -> 0% of each run, Pallas kernels for 0% -> 1%
where the time goes in v11:
time: 87.2 us; the launch traced here: 86.9 us
  blocking collectives  63.5 us (73%)
  starting transfers between devices  9.48 us (11%)
  waiting for transfers between devices  8.01 us (9%)
  Pallas kernels  5.75 us (7%)
    all_to_all x1, blocking collectives, local(): lax.all_to_all(packed, 'tm', split_axis=0, concat_axis=0, tiled=True)  25 us
    all_to_all x1, blocking collectives, local(): lax.all_to_all(shared, ('sx', 'sy'), split_axis=0, concat_axis=0, tiled=T...  21.7 us
    all_to_all x1, blocking collectives, local(): lax.all_to_all(message.reshape(TM, TILES, 8, L), 'tm', split_axis=0, conc...  16.8 us
    pallas_call x8, Pallas kernels, call(): pl.pallas_call(kernel, name=name, out_shape=out_shape, in_specs=smem(len(...  5.75 us
    ppermute x1, waiting for transfers between devices, local(): right = lax.ppermute(to_left, 'sx', [(q, p) for p, q in across])  4.6 us
    ppermute x1, starting transfers between devices, local(): swapped = lax.ppermute(swap, ('tm', 'sy'), swaps())  4.05 us
    ppermute x1, starting transfers between devices, local(): left = lax.ppermute(to_right, 'sx', across)  4 us
    ppermute x1, waiting for transfers between devices, local(): swapped = lax.ppermute(swap, ('tm', 'sy'), swaps())  2.8 us
  transfers between devices with their start and end apart: 3, of which 3 were waited for; matrix products, arithmetic and copies ran while one was open for 0% of the time, Pallas kernels for 1%

profile of v11, /device:TPU:1, one launch (start us, length us, event | category | flops | bytes accessed | tf_op | source)
XLA Modules:
  0.0 86.9 jit_solution(8810472128085428875)
XLA Ops:
  0.0 1.2 %pack.1 = (f32[16,48,128]{2,1,0:T(8,128)S(1)}, f32[144,128]{1,0:T(8,128)S(1)}, f32[8,128]{1,0:T(8,128)S(1)}) custom-call(f32[8]{0:T(128)} %rates.1, f32[512,128]{1,0:T(8,128)} %bitcast.10, s32[64,128]{1,0:T(8,128)} %bitcast.11), custom_call_target="tpu_custom_call" | custom-call | tf_op jit(solution)/shard_map/pack/pallas_call | solution.py:468
  1.2 0.0 copy-start
  1.2 25.0 %all_to_all.15 = f32[16,48,128]{2,1,0:T(8,128)S(1)} all-to-all(f32[16,48,128]{2,1,0:T(8,128)S(1)} %get-tuple-element.16), channel_id=1, replica_groups=mesh['tm'=16,'sx'=8,'sy'=4] {'tm'}, dimensions={0} | all-to-all | bytes 786432 | tf_op jit(solution)/shard_map/all_to_all | solution.py:497
  26.3 0.0 copy-done
  26.3 0.4 swap_rows.1
  26.6 4.0 %collective-permute-start = (f32[25,8,128]{2,1,0:T(8,128)S(1)}, f32[25,8,128]{2,1,0:T(8,128)S(1)}, u32[]{:S(2)}, u32[]{:S(2)}) collective-permute-start(f32[25,8,128]{2,1,0:T(8,128)S(1)} %swap_rows.1), channel_id=1, source_target_pairs={{64,128},{192,256},{320,384},{448,480},{416,352},{288,224},{160,96... | collective-permute-start | bytes 307208 | tf_op jit(solution)/shard_map/ppermute | solution.py:500
  30.7 0.6 transform.1
  31.3 2.8 %collective-permute-done.swapped = f32[25,8,128]{2,1,0:T(8,128)S(1)} collective-permute-done((f32[25,8,128]{2,1,0:T(8,128)S(1)}, f32[25,8,128]{2,1,0:T(8,128)S(1)}, u32[]{:S(2)}, u32[]{:S(2)}) %collective-permute-start) | collective-permute-done | bytes 102432 | tf_op jit(solution)/shard_map/ppermute | solution.py:500
  34.1 0.0 copy-start.3
  34.1 4.0 %collective-permute-start.1 = (f32[46,8,128]{2,1,0:T(8,128)S(1)}, f32[46,8,128]{2,1,0:T(8,128)S(1)}, u32[]{:S(2)}, u32[]{:S(2)}) collective-permute-start(f32[46,8,128]{2,1,0:T(8,128)S(1)} %get-tuple-element.24), channel_id=1, source_target_pairs={{0,4},{4,8},{8,12},{12,16},{16,20},{20,24},{24,28},{1,5},{5,9},{9,... | collective-permute-start | bytes 565256 | tf_op jit(solution)/shard_map/ppermute | solution.py:509
  38.2 0.0 copy-start.1
  38.2 1.4 %collective-permute-start.2 = (f32[46,8,128]{2,1,0:T(8,128)S(1)}, f32[46,8,128]{2,1,0:T(8,128)S(1)}, u32[]{:S(2)}, u32[]{:S(2)}) collective-permute-start(f32[46,8,128]{2,1,0:T(8,128)S(1)} %get-tuple-element.25), channel_id=1, source_target_pairs={{4,0},{8,4},{12,8},{16,12},{20,16},{24,20},{28,24},{5,1},{9,5},{13... | collective-permute-start | bytes 565256 | tf_op jit(solution)/shard_map/ppermute | solution.py:510
  39.6 0.0 copy-done.3
  39.6 0.4 prepare.1
  40.1 0.6 collective-permute-done.1.left
  40.7 4.6 %collective-permute-done.2.right = f32[46,8,128]{2,1,0:T(8,128)S(1)} collective-permute-done((f32[46,8,128]{2,1,0:T(8,128)S(1)}, f32[46,8,128]{2,1,0:T(8,128)S(1)}, u32[]{:S(2)}, u32[]{:S(2)}) %collective-permute-start.2) | collective-permute-done | bytes 188448 | tf_op jit(solution)/shard_map/ppermute | solution.py:510
  45.3 0.0 copy-done.1
  45.3 1.3 %sweeps.1 = f32[640,128]{1,0:T(8,128)S(1)} custom-call(f32[14,8,8,128]{3,2,1,0:T(8,128)S(1)} %get-tuple-element.20.own_s, f32[14,8,8,128]{3,2,1,0:T(8,128)S(1)} %get-tuple-element.21.own_a, f32[14,8,8,128]{3,2,1,0:T(8,128)S(1)} %get-tuple-element.22.own_b, f32[14,8,8,128]{3,2,1,0:T(8,128)S(1)} %get-tuple-element.23.own_x, ...), custom_call_target="tpu_custom_call" | custom-call | tf_op jit(solution)/shard_map/sweeps/pallas_call | solution.py:468
  46.6 16.8 %all_to_all.16.received = f32[16,5,8,128]{3,2,1,0:T(8,128)S(1)} all-to-all(f32[16,5,8,128]{3,2,1,0:T(8,128)S(1)} %bitcast.8), channel_id=1, replica_groups=mesh['tm'=16,'sx'=8,'sy'=4] {'tm'}, dimensions={0} | all-to-all | bytes 655360 | tf_op jit(solution)/shard_map/all_to_all | solution.py:526
  63.3 0.0 copy-start.2
  63.4 21.7 %all_to_all.17 = f32[32,8,128]{2,1,0:T(8,128)S(1)} all-to-all(f32[32,8,128]{2,1,0:T(8,128)S(1)} %gather.1), channel_id=1, replica_groups=mesh['tm'=16,'sx'=8,'sy'=4] {'sx','sy'}, dimensions={0} | all-to-all | bytes 262144 | tf_op jit(solution)/shard_map/all_to_all | solution.py:530
  85.1 0.0 copy-done.2
  85.1 1.8 %coarse.1 = f32[512,128]{1,0:T(8,128)} custom-call(f32[8,4,8,128]{3,2,1,0:T(8,128)S(1)} %bitcast.9, f32[16,5,8,128]{3,2,1,0:T(8,128)S(1)} %all_to_all.16.received, f32[8,128]{1,0:T(8,128)S(1)} %copy-done.3, f32[128,128]{1,0:T(8,128)S(1)} %copy-done.2), custom_call_target="tpu_custom_call" | custom-call | tf_op jit(solution)/shard_map/coarse/pallas_call | solution.py:468
  (2 shorter events, 0.1 us)
Async XLA Ops:
  1.2 25.1 %copy-start = (bf16[2,128,128]{2,1,0:T(8,128)(2,1)S(1)}, bf16[2,128,128]{2,1,0:T(8,128)(2,1)}, u32[]{:S(2)}) copy-start(bf16[2,128,128]{2,1,0:T(8,128)(2,1)} %constant.8.clone.table) | copy-start | bytes 196612
  26.6 7.5 %collective-permute-start = (f32[25,8,128]{2,1,0:T(8,128)S(1)}, f32[25,8,128]{2,1,0:T(8,128)S(1)}, u32[]{:S(2)}, u32[]{:S(2)}) collective-permute-start(f32[25,8,128]{2,1,0:T(8,128)S(1)} %swap_rows.1), channel_id=1, source_target_pairs={{64,128},{192,256},{320,384},{448,480},{416,352},{288,224},{160,96... | collective-permute-start | bytes 307208 | tf_op jit(solution)/shard_map/ppermute | solution.py:500
  34.1 5.5 %copy-start.3 = (f32[8,128]{1,0:T(8,128)S(1)}, f32[8,128]{1,0:T(8,128)}, u32[]{:S(2)}) copy-start(f32[8,128]{1,0:T(8,128)} %constant.11.clone.lanes) | copy-start | bytes 12292
  34.1 6.5 %collective-permute-start.1 = (f32[46,8,128]{2,1,0:T(8,128)S(1)}, f32[46,8,128]{2,1,0:T(8,128)S(1)}, u32[]{:S(2)}, u32[]{:S(2)}) collective-permute-start(f32[46,8,128]{2,1,0:T(8,128)S(1)} %get-tuple-element.24), channel_id=1, source_target_pairs={{0,4},{4,8},{8,12},{12,16},{16,20},{20,24},{24,28},{1,5},{5,9},{9,... | collective-permute-start | bytes 565256 | tf_op jit(solution)/shard_map/ppermute | solution.py:509
  38.2 7.1 %copy-start.1 = (bf16[2,160,128]{2,1,0:T(8,128)(2,1)S(1)}, bf16[2,160,128]{2,1,0:T(8,128)(2,1)}, u32[]{:S(2)}) copy-start(bf16[2,160,128]{2,1,0:T(8,128)(2,1)} %constant.9.clone.table) | copy-start | bytes 245764
  38.2 7.1 %collective-permute-start.2 = (f32[46,8,128]{2,1,0:T(8,128)S(1)}, f32[46,8,128]{2,1,0:T(8,128)S(1)}, u32[]{:S(2)}, u32[]{:S(2)}) collective-permute-start(f32[46,8,128]{2,1,0:T(8,128)S(1)} %get-tuple-element.25), channel_id=1, source_target_pairs={{4,0},{8,4},{12,8},{16,12},{20,16},{24,20},{28,24},{5,1},{9,5},{13... | collective-permute-start | bytes 565256 | tf_op jit(solution)/shard_map/ppermute | solution.py:510
  63.3 21.7 %copy-start.2 = (f32[128,128]{1,0:T(8,128)S(1)}, f32[128,128]{1,0:T(8,128)}, u32[]{:S(2)}) copy-start(f32[128,128]{1,0:T(8,128)} %constant.10.clone.table) | copy-start | bytes 196612

commit v12 on v11

--- a/solution.py
+++ b/solution.py
@@ -24,7 +24,9 @@
 
 
 def strip_of(d):
-    return d // 2 if d % 2 == 0 else TM - 1 - d // 2
+    if d % 2 == 1:
+        return 7 + d // 2
+    return {0: 0, 2: TM - 1}.get(d, d // 2 - 1)
 
 
 MEMBER = {strip_of(d): d for d in range(TM)}
@@ -132,7 +134,9 @@
 
 def own_strip():
     tm = lax.axis_index("tm")
-    return jnp.where(tm & 1 == 0, tm >> 1, TM - 1 - (tm >> 1))
+    ends = jnp.where(tm == 0, 0, TM - 1)
+    even = jnp.where(tm <= 2, ends, (tm >> 1) - 1)
+    return jnp.where(tm & 1 == 1, 7 + (tm >> 1), even)
 
 
 def spectra(received, table, starts):

time: 87.2 us -> 87.2 us (level)
  waiting for transfers between devices: 8.01 us -> 7.08 us
  blocking collectives: 63.5 us -> 64.4 us
    all_to_all x1, blocking collectives: 16.8 us -> 19.3 us  [local(): lax.all_to_all(message.reshape(TM, TILES, 8, L), 'tm', split_axis=0, conc...]
    all_to_all x1, blocking collectives: 21.7 us -> 20 us  [local(): lax.all_to_all(shared, ('sx', 'sy'), split_axis=0, concat_axis=0, tiled=T...]
    ppermute x1, waiting for transfers between devices: 2.8 us -> 1.88 us  [local(): swapped = lax.ppermute(swap, ('tm', 'sy'), swaps())]
where the time goes in v12:
time: 87.2 us; the launch traced here: 86.8 us
  blocking collectives  64.4 us (74%)
  starting transfers between devices  9.48 us (11%)
  waiting for transfers between devices  7.08 us (8%)
  Pallas kernels  5.76 us (7%)
    all_to_all x1, blocking collectives, local(): lax.all_to_all(packed, 'tm', split_axis=0, concat_axis=0, tiled=True)  25 us
    all_to_all x1, blocking collectives, local(): lax.all_to_all(shared, ('sx', 'sy'), split_axis=0, concat_axis=0, tiled=T...  20 us
    all_to_all x1, blocking collectives, local(): lax.all_to_all(message.reshape(TM, TILES, 8, L), 'tm', split_axis=0, conc...  19.3 us
    pallas_call x8, Pallas kernels, call(): pl.pallas_call(kernel, name=name, out_shape=out_shape, in_specs=smem(len(...  5.76 us
    ppermute x1, waiting for transfers between devices, local(): right = lax.ppermute(to_left, 'sx', [(q, p) for p, q in across])  4.6 us
    ppermute x1, starting transfers between devices, local(): swapped = lax.ppermute(swap, ('tm', 'sy'), swaps())  4.05 us
    ppermute x1, starting transfers between devices, local(): left = lax.ppermute(to_right, 'sx', across)  4.01 us
    ppermute x1, waiting for transfers between devices, local(): swapped = lax.ppermute(swap, ('tm', 'sy'), swaps())  1.88 us
  transfers between devices with their start and end apart: 3, of which 3 were waited for; matrix products, arithmetic and copies ran while one was open for 0% of the time, Pallas kernels for 1%

profile of v12, /device:TPU:1, one launch (start us, length us, event | category | flops | bytes accessed | tf_op | source)
XLA Modules:
  0.0 86.8 jit_solution(5218834215942928675)
XLA Ops:
  0.0 1.2 %pack.1 = (f32[16,48,128]{2,1,0:T(8,128)S(1)}, f32[144,128]{1,0:T(8,128)S(1)}, f32[8,128]{1,0:T(8,128)S(1)}) custom-call(f32[8]{0:T(128)} %rates.1, f32[512,128]{1,0:T(8,128)} %bitcast.10, s32[64,128]{1,0:T(8,128)} %bitcast.11), custom_call_target="tpu_custom_call" | custom-call | tf_op jit(solution)/shard_map/pack/pallas_call | solution.py:472
  1.2 0.0 copy-start
  1.2 25.0 %all_to_all.15 = f32[16,48,128]{2,1,0:T(8,128)S(1)} all-to-all(f32[16,48,128]{2,1,0:T(8,128)S(1)} %get-tuple-element.16), channel_id=1, replica_groups=mesh['tm'=16,'sx'=8,'sy'=4] {'tm'}, dimensions={0} | all-to-all | bytes 786432 | tf_op jit(solution)/shard_map/all_to_all | solution.py:501
  26.3 0.0 copy-done
  26.3 0.4 swap_rows.1
  26.6 4.0 %collective-permute-start = (f32[25,8,128]{2,1,0:T(8,128)S(1)}, f32[25,8,128]{2,1,0:T(8,128)S(1)}, u32[]{:S(2)}, u32[]{:S(2)}) collective-permute-start(f32[25,8,128]{2,1,0:T(8,128)S(1)} %swap_rows.1), channel_id=1, source_target_pairs={{128,192},{256,320},{384,448},{32,96},{160,224},{288,352},{416,480... | collective-permute-start | bytes 307208 | tf_op jit(solution)/shard_map/ppermute | solution.py:504
  30.7 0.6 transform.1
  31.3 1.9 %collective-permute-done.swapped = f32[25,8,128]{2,1,0:T(8,128)S(1)} collective-permute-done((f32[25,8,128]{2,1,0:T(8,128)S(1)}, f32[25,8,128]{2,1,0:T(8,128)S(1)}, u32[]{:S(2)}, u32[]{:S(2)}) %collective-permute-start) | collective-permute-done | bytes 102432 | tf_op jit(solution)/shard_map/ppermute | solution.py:504
  33.2 0.0 copy-start.3
  33.2 4.0 %collective-permute-start.1 = (f32[46,8,128]{2,1,0:T(8,128)S(1)}, f32[46,8,128]{2,1,0:T(8,128)S(1)}, u32[]{:S(2)}, u32[]{:S(2)}) collective-permute-start(f32[46,8,128]{2,1,0:T(8,128)S(1)} %get-tuple-element.24), channel_id=1, source_target_pairs={{0,4},{4,8},{8,12},{12,16},{16,20},{20,24},{24,28},{1,5},{5,9},{9,... | collective-permute-start | bytes 565256 | tf_op jit(solution)/shard_map/ppermute | solution.py:513
  37.2 0.0 copy-start.1
  37.2 1.4 %collective-permute-start.2 = (f32[46,8,128]{2,1,0:T(8,128)S(1)}, f32[46,8,128]{2,1,0:T(8,128)S(1)}, u32[]{:S(2)}, u32[]{:S(2)}) collective-permute-start(f32[46,8,128]{2,1,0:T(8,128)S(1)} %get-tuple-element.25), channel_id=1, source_target_pairs={{4,0},{8,4},{12,8},{16,12},{20,16},{24,20},{28,24},{5,1},{9,5},{13... | collective-permute-start | bytes 565256 | tf_op jit(solution)/shard_map/ppermute | solution.py:514
  38.7 0.0 copy-done.3
  38.7 0.4 prepare.1
  39.1 0.6 collective-permute-done.1.left
  39.7 4.6 %collective-permute-done.2.right = f32[46,8,128]{2,1,0:T(8,128)S(1)} collective-permute-done((f32[46,8,128]{2,1,0:T(8,128)S(1)}, f32[46,8,128]{2,1,0:T(8,128)S(1)}, u32[]{:S(2)}, u32[]{:S(2)}) %collective-permute-start.2) | collective-permute-done | bytes 188448 | tf_op jit(solution)/shard_map/ppermute | solution.py:514
  44.3 0.0 copy-done.1
  44.3 1.3 %sweeps.1 = f32[640,128]{1,0:T(8,128)S(1)} custom-call(f32[14,8,8,128]{3,2,1,0:T(8,128)S(1)} %get-tuple-element.20.own_s, f32[14,8,8,128]{3,2,1,0:T(8,128)S(1)} %get-tuple-element.21.own_a, f32[14,8,8,128]{3,2,1,0:T(8,128)S(1)} %get-tuple-element.22.own_b, f32[14,8,8,128]{3,2,1,0:T(8,128)S(1)} %get-tuple-element.23.own_x, ...), custom_call_target="tpu_custom_call" | custom-call | tf_op jit(solution)/shard_map/sweeps/pallas_call | solution.py:472
  45.6 19.3 %all_to_all.16.received = f32[16,5,8,128]{3,2,1,0:T(8,128)S(1)} all-to-all(f32[16,5,8,128]{3,2,1,0:T(8,128)S(1)} %bitcast.8), channel_id=1, replica_groups=mesh['tm'=16,'sx'=8,'sy'=4] {'tm'}, dimensions={0} | all-to-all | bytes 655360 | tf_op jit(solution)/shard_map/all_to_all | solution.py:530
  65.0 0.0 copy-start.2
  65.0 20.0 %all_to_all.17 = f32[32,8,128]{2,1,0:T(8,128)S(1)} all-to-all(f32[32,8,128]{2,1,0:T(8,128)S(1)} %gather.1), channel_id=1, replica_groups=mesh['tm'=16,'sx'=8,'sy'=4] {'sx','sy'}, dimensions={0} | all-to-all | bytes 262144 | tf_op jit(solution)/shard_map/all_to_all | solution.py:534
  85.0 0.0 copy-done.2
  85.0 1.8 %coarse.1 = f32[512,128]{1,0:T(8,128)} custom-call(f32[8,4,8,128]{3,2,1,0:T(8,128)S(1)} %bitcast.9, f32[16,5,8,128]{3,2,1,0:T(8,128)S(1)} %all_to_all.16.received, f32[8,128]{1,0:T(8,128)S(1)} %copy-done.3, f32[128,128]{1,0:T(8,128)S(1)} %copy-done.2), custom_call_target="tpu_custom_call" | custom-call | tf_op jit(solution)/shard_map/coarse/pallas_call | solution.py:472
  (2 shorter events, 0.1 us)
Async XLA Ops:
  1.2 25.1 %copy-start = (bf16[2,128,128]{2,1,0:T(8,128)(2,1)S(1)}, bf16[2,128,128]{2,1,0:T(8,128)(2,1)}, u32[]{:S(2)}) copy-start(bf16[2,128,128]{2,1,0:T(8,128)(2,1)} %constant.8.clone.table) | copy-start | bytes 196612
  26.6 6.6 %collective-permute-start = (f32[25,8,128]{2,1,0:T(8,128)S(1)}, f32[25,8,128]{2,1,0:T(8,128)S(1)}, u32[]{:S(2)}, u32[]{:S(2)}) collective-permute-start(f32[25,8,128]{2,1,0:T(8,128)S(1)} %swap_rows.1), channel_id=1, source_target_pairs={{128,192},{256,320},{384,448},{32,96},{160,224},{288,352},{416,480... | collective-permute-start | bytes 307208 | tf_op jit(solution)/shard_map/ppermute | solution.py:504
  33.2 5.5 %copy-start.3 = (f32[8,128]{1,0:T(8,128)S(1)}, f32[8,128]{1,0:T(8,128)}, u32[]{:S(2)}) copy-start(f32[8,128]{1,0:T(8,128)} %constant.11.clone.lanes) | copy-start | bytes 12292
  33.2 6.5 %collective-permute-start.1 = (f32[46,8,128]{2,1,0:T(8,128)S(1)}, f32[46,8,128]{2,1,0:T(8,128)S(1)}, u32[]{:S(2)}, u32[]{:S(2)}) collective-permute-start(f32[46,8,128]{2,1,0:T(8,128)S(1)} %get-tuple-element.24), channel_id=1, source_target_pairs={{0,4},{4,8},{8,12},{12,16},{16,20},{20,24},{24,28},{1,5},{5,9},{9,... | collective-permute-start | bytes 565256 | tf_op jit(solution)/shard_map/ppermute | solution.py:513
  37.2 7.1 %copy-start.1 = (bf16[2,160,128]{2,1,0:T(8,128)(2,1)S(1)}, bf16[2,160,128]{2,1,0:T(8,128)(2,1)}, u32[]{:S(2)}) copy-start(bf16[2,160,128]{2,1,0:T(8,128)(2,1)} %constant.9.clone.table) | copy-start | bytes 245764
  37.2 7.1 %collective-permute-start.2 = (f32[46,8,128]{2,1,0:T(8,128)S(1)}, f32[46,8,128]{2,1,0:T(8,128)S(1)}, u32[]{:S(2)}, u32[]{:S(2)}) collective-permute-start(f32[46,8,128]{2,1,0:T(8,128)S(1)} %get-tuple-element.25), channel_id=1, source_target_pairs={{4,0},{8,4},{12,8},{16,12},{20,16},{24,20},{28,24},{5,1},{9,5},{13... | collective-permute-start | bytes 565256 | tf_op jit(solution)/shard_map/ppermute | solution.py:514
  65.0 20.0 %copy-start.2 = (f32[128,128]{1,0:T(8,128)S(1)}, f32[128,128]{1,0:T(8,128)}, u32[]{:S(2)}) copy-start(f32[128,128]{1,0:T(8,128)} %constant.10.clone.table) | copy-start | bytes 196612
